TPU v7x, 32 devices: a whole 2x2x4 slice. The times are simulated.
32 devices in a mesh: lat: 8 (over y, x, core), lon: 4 (over z).
Axes of the slice: x: 2, y: 2, z: 4, core: 2. Of those that a mesh axis runs over, the one named last changes fastest.
Arguments:
- tokens: bfloat16 [2, 48, 96, 512], P(None, 'lat', 'lon'), may hold values from -6 to 6
- land_sea: int32 [48, 96], P('lat', 'lon'), may hold values 0 or 1
- land_vector: float32 [512], replicated, may hold values from -3 to 3
- fine_inward: bfloat16 [512, 768], replicated, may hold values from -0.25 to 0.25
- fine_outward: bfloat16 [256, 512], replicated, may hold values from -0.375 to 0.375
- fine_gain: float32 [512], replicated, may hold values from 0.25 to 1.75
- fine_scale: float32 [4], replicated, may hold values from 3 to 12
- merge_gain: float32 [2048], replicated, may hold values from 0.25 to 1.75
- merge_weight: bfloat16 [2048, 1024], replicated, may hold values from -0.125 to 0.125
- coarse_inward: bfloat16 [1024, 1536], replicated, may hold values from -0.1875 to 0.1875
- coarse_outward: bfloat16 [512, 1024], replicated, may hold values from -0.25 to 0.25
- coarse_gain: float32 [1024], replicated, may hold values from 0.25 to 1.75
- coarse_scale: float32 [8], replicated, may hold values from 3 to 12
- coarse_cotangent: bfloat16 [2, 24, 48, 1024], P(None, 'lat', 'lon'), may hold values from -6 to 6
Outputs:
- coarse_output: bfloat16 [2, 24, 48, 1024], P(None, 'lat', 'lon')
- token_grad: bfloat16 [2, 48, 96, 512], P(None, 'lat', 'lon')
All inputs are finite; a program needn't handle non-finite values. No bound on the sum of `land_sea` on one device may be relied on, other than what follows from the above.
Results may differ from a plain program's by a relative error of at most 0.02.
Values may be sent and summed in bfloat16 or wider, within the bound.
No kernel may reach another device: no remote copies, remote signals or barrier semaphores. Data moves between devices by JAX's collectives and lax.ppermute only.
A program may use at most 64 MiB of HBM per device.

v0:
```python
import jax
import jax.numpy as jnp
from jax import lax
from jax.sharding import PartitionSpec as P

HEADS = 4
HEADS2 = 8
WIN_LAT = 6
WIN_LON = 12


EPS_NORM = 1e-05
EPS_HEAD = 1e-06


def passed_along(x, axis, by):
    count = lax.axis_size(axis)
    return lax.ppermute(x, axis, [(i, (i + by) % count) for i in range(count)])


def swapped(x, axis, stride):
    return lax.ppermute(x, axis, [(i, i ^ 1 << stride) for i in range(lax.axis_size(axis))])


def layer_norm(values, norm_gain):
    average = jnp.mean(values, axis=-1, keepdims=True)
    centred = values - average
    spread = jnp.mean(centred * centred, axis=-1, keepdims=True)
    return centred * lax.rsqrt(spread + EPS_NORM) * norm_gain


def into_windows(field):
    levels, height, breadth, channels = field.shape
    blocks = field.reshape(
        levels, height // WIN_LAT, WIN_LAT, breadth // WIN_LON, WIN_LON, channels
    )
    blocks = blocks.transpose(1, 3, 0, 2, 4, 5)
    return blocks.reshape(-1, levels * WIN_LAT * WIN_LON, channels)


def from_windows(blocks, levels, height, breadth):
    channels = blocks.shape[-1]
    field = blocks.reshape(
        height // WIN_LAT, breadth // WIN_LON, levels, WIN_LAT, WIN_LON, channels
    )
    return field.transpose(2, 0, 3, 1, 4, 5).reshape(levels, height, breadth, channels)


def attend(packed, scales, head_count, allowed):
    windows, length, width = packed.shape
    inner = width // 3
    head_size = inner // head_count
    span = head_count * length
    lane_head = lax.iota(jnp.int32, inner) // head_size
    column_head = lax.iota(jnp.int32, span) // length
    head_range = lax.iota(jnp.int32, head_count)
    lane_member = (lane_head[:, None] == head_range[None, :]).astype(jnp.float32)
    column_member = (column_head[:, None] == head_range[None, :]).astype(jnp.float32)

    def unit_rows(rows):
        squares = jnp.dot(rows * rows, lane_member, precision=lax.Precision.HIGHEST) / head_size
        factor = jnp.dot(
            lax.rsqrt(squares + EPS_HEAD), lane_member.T, precision=lax.Precision.HIGHEST
        )
        return (rows * factor).astype(jnp.bfloat16)

    query_unit = unit_rows(packed[:, :, :inner].astype(jnp.float32))
    key_unit = unit_rows(packed[:, :, inner : 2 * inner].astype(jnp.float32))
    values = packed[:, :, 2 * inner :]
    block_mask = lane_head[:, None] == column_head[None, :]
    zero_value = jnp.zeros((), jnp.bfloat16)
    key_block = jnp.where(
        block_mask, jnp.tile(jnp.swapaxes(key_unit, 1, 2), (1, 1, head_count)), zero_value
    )
    logits = jnp.einsum("wqc,wcm->wqm", query_unit, key_block, preferred_element_type=jnp.float32)
    column_scale = jnp.dot(column_member, scales / head_size, precision=lax.Precision.HIGHEST)
    weights = jnp.exp(logits * column_scale)
    if allowed is not None:
        weights = weights * jnp.tile(allowed, (1, 1, head_count))
    totals = jnp.dot(weights, column_member, precision=lax.Precision.HIGHEST)
    spread_totals = jnp.dot(totals, column_member.T, precision=lax.Precision.HIGHEST)
    probs = (weights / spread_totals).astype(jnp.bfloat16)
    value_block = jnp.where(block_mask.T, jnp.tile(values, (1, head_count, 1)), zero_value)
    mixture = jnp.einsum("wqm,wmc->wqc", probs, value_block, preferred_element_type=jnp.float32)
    return mixture.astype(jnp.bfloat16)


def window_branch(packed, allowed, scales, outward, norm_gain, head_count):
    levels, height, breadth = (packed.shape[0], packed.shape[1], packed.shape[2])
    blocks = into_windows(packed)
    mixture = attend(blocks, scales, head_count, allowed)
    mixture = from_windows(mixture, levels, height, breadth)
    projected = jnp.dot(mixture, outward, preferred_element_type=jnp.float32)
    return layer_norm(projected, norm_gain)


def merge_patches(fine_field, norm_gain, weight):
    levels, height, breadth, channels = fine_field.shape
    grouped = fine_field.reshape(levels, height // 2, 2, breadth // 2, 2, channels)
    grouped = grouped.transpose(0, 1, 3, 4, 2, 5).reshape(
        levels, height // 2, breadth // 2, 4 * channels
    )
    normed = layer_norm(grouped.astype(jnp.float32), norm_gain).astype(jnp.bfloat16)
    return jnp.dot(normed, weight, preferred_element_type=jnp.float32).astype(jnp.bfloat16)


def gather_region(field):
    half_lat = WIN_LAT // 2
    half_lon = WIN_LON // 2
    height, breadth = (field.shape[1], field.shape[2])
    upper = passed_along(field[:, height - half_lat :], "lat", 1)
    window_rows = jnp.concatenate([upper, field[:, :half_lat]], axis=1)
    left = passed_along(window_rows[:, :, breadth - half_lon :], "lon", 1)
    return jnp.concatenate([left, window_rows[:, :, : breadth - half_lon]], axis=2)


def return_region(region):
    half_lat = WIN_LAT // 2
    half_lon = WIN_LON // 2
    back_cols = passed_along(region[:, :, :half_lon], "lon", -1)
    columns = jnp.concatenate([region[:, :, half_lon:], back_cols], axis=2)
    back_rows = passed_along(columns[:, :half_lat], "lat", -1)
    return jnp.concatenate([columns[:, half_lat:], back_rows], axis=1)


def local(
    tokens,
    land_sea,
    land_vector,
    fine_inward,
    fine_outward,
    fine_gain,
    fine_scale,
    merge_gain,
    merge_weight,
    coarse_inward,
    coarse_outward,
    coarse_gain,
    coarse_scale,
    coarse_cotangent,
):
    levels, height, breadth = (tokens.shape[0], tokens.shape[1], tokens.shape[2])
    half_lat = WIN_LAT // 2
    biased = (
        tokens.astype(jnp.float32) + land_sea.astype(jnp.float32)[None, :, :, None] * land_vector
    ).astype(jnp.bfloat16)
    region = gather_region(biased)
    local_rows = lax.iota(jnp.int32, height)
    upper_side = ((local_rows < half_lat) & (lax.axis_index("lat") == 0)).astype(jnp.float32)
    marks = into_windows(
        jnp.broadcast_to(upper_side[None, :, None, None], (levels, height, breadth, 1))
    )[..., 0]
    allowed = (marks[:, :, None] == marks[:, None, :]).astype(jnp.float32)

    def fine_block(region_tokens):
        packed = jnp.dot(region_tokens, fine_inward, preferred_element_type=jnp.float32).astype(
            jnp.bfloat16
        )
        branch = window_branch(packed, allowed, fine_scale, fine_outward, fine_gain, HEADS)
        return (region_tokens.astype(jnp.float32) + branch).astype(jnp.bfloat16)

    result_region, fine_pull = jax.vjp(fine_block, region)
    fine_result = return_region(result_region)

    def merge_own(fine_field):
        return merge_patches(fine_field, merge_gain, merge_weight)

    coarse_own, merge_pull = jax.vjp(merge_own, fine_result)
    stacked = jnp.stack([coarse_own, coarse_cotangent])
    partner = swapped(stacked, "lat", 0)
    parity = lax.axis_index("lat") % 2
    north_part = jnp.where(parity == 0, stacked, partner)
    south_part = jnp.where(parity == 0, partner, stacked)
    coarse_band = jnp.concatenate([north_part, south_part], axis=2)

    def coarse_block(band_field):
        band_packed = jnp.dot(band_field, coarse_inward, preferred_element_type=jnp.float32).astype(
            jnp.bfloat16
        )
        band_branch = window_branch(
            band_packed, None, coarse_scale, coarse_outward, coarse_gain, HEADS2
        )
        return (band_field.astype(jnp.float32) + band_branch).astype(jnp.bfloat16)

    output_band, coarse_pull = jax.vjp(coarse_block, coarse_band[0])
    (band_grad,) = coarse_pull(coarse_band[1])
    offset = parity * (height // 2)
    coarse_output = lax.dynamic_slice_in_dim(output_band, offset, height // 2, 1)
    coarse_grad = lax.dynamic_slice_in_dim(band_grad, offset, height // 2, 1)
    (fine_grad,) = merge_pull(coarse_grad)
    grad_region = gather_region(fine_grad)
    (region_grad,) = fine_pull(grad_region)
    token_grad = return_region(region_grad)
    return (coarse_output, token_grad)


def solution(mesh):
    return jax.shard_map(
        local,
        mesh=mesh,
        in_specs=(
            P(None, "lat", "lon", None),
            P("lat", "lon"),
            P(),
            P(),
            P(),
            P(),
            P(),
            P(),
            P(),
            P(),
            P(),
            P(),
            P(),
            P(None, "lat", "lon", None),
        ),
        out_specs=(P(None, "lat", "lon", None), P(None, "lat", "lon", None)),
        check_vma=False,
    )
```

profile of v0, /device:TPU:1, one launch (start us, length us, event | category | flops | bytes accessed | tf_op | source)
XLA Modules:
  0.0 157.0 jit_solution(4717484522160616908)
XLA Ops:
  4.1 2.6 %collective-permute-start = (bf16[2,3,24,512]{3,2,1,0:T(8,128)(2,1)}, bf16[2,3,24,512]{3,2,1,0:T(8,128)(2,1)S(1)}, u32[]{:S(2)}, u32[]{:S(2)}) collective-permute-start(bf16[2,3,24,512]{3,2,1,0:T(8,128)(2,1)} %get-tuple-element.27), channel_id=1, source_target_pairs={{0,4},{4,8},{8,12},{12,16},{16,20},{20,24},{24,28},{28,0},{1,5},{5... | collective-permute-start | bytes 442376 | tf_op jit(solution)/shard_map/ppermute | solution.py:18
  10.5 2.9 %tile.52 = f32[2,144,576]{2,1,0:T(8,128)} reshape(f32[2,144,4,144]{3,2,1,0:T(4,128)} %tile.51) | data formatting | bytes 1327104 | tf_op jit(solution)/shard_map/jvp()/tile | solution.py:79
  14.9 4.2 %collective-permute-done.1 = bf16[2,6,6,512]{3,2,1,0:T(8,128)(2,1)S(1)} collective-permute-done((bf16[2,6,6,512]{3,2,1,0:T(8,128)(2,1)S(1)}, bf16[2,6,6,512]{3,2,1,0:T(8,128)(2,1)S(1)}, u32[]{:S(2)}, u32[]{:S(2)}) %collective-permute-start.1) | collective-permute-done | bytes 73760 | tf_op jit(solution)/shard_map/ppermute | solution.py:18
  29.4 1.8 %collective-permute-start.2 = (bf16[2,6,6,512]{3,2,1,0:T(8,128)(2,1)S(1)}, bf16[2,6,6,512]{3,2,1,0:T(8,128)(2,1)S(1)}, u32[]{:S(2)}, u32[]{:S(2)}) collective-permute-start(bf16[2,6,6,512]{3,2,1,0:T(8,128)(2,1)S(1)} %slice.102), channel_id=1, source_target_pairs={{0,3},{1,0},{2,1},{3,2},{4,7},{5,4},{6,5},{7,6},{8,11},{9,8},{10,9... | collective-permute-start | bytes 221192 | tf_op jit(solution)/shard_map/ppermute | solution.py:18
  31.3 2.7 %collective-permute-done.2 = bf16[2,6,6,512]{3,2,1,0:T(8,128)(2,1)S(1)} collective-permute-done((bf16[2,6,6,512]{3,2,1,0:T(8,128)(2,1)S(1)}, bf16[2,6,6,512]{3,2,1,0:T(8,128)(2,1)S(1)}, u32[]{:S(2)}, u32[]{:S(2)}) %collective-permute-start.2) | collective-permute-done | bytes 73760 | tf_op jit(solution)/shard_map/ppermute | solution.py:18
  37.7 2.1 %collective-permute-done.3 = bf16[2,3,24,512]{3,2,1,0:T(8,128)(2,1)} collective-permute-done((bf16[2,3,24,512]{3,2,1,0:T(8,128)(2,1)}, bf16[2,3,24,512]{3,2,1,0:T(8,128)(2,1)}, u32[]{:S(2)}, u32[]{:S(2)}) %collective-permute-start.3) | collective-permute-done | bytes 147488 | tf_op jit(solution)/shard_map/ppermute | solution.py:18
  39.8 1.8 %maximum_convert_fusion = f32[2,6,24,512]{3,2,1,0:T(8,128)} fusion(bf16[2,3,24,512]{3,2,1,0:T(8,128)(2,1)} %collective-permute-done.3, bf16[2,3,24,512]{3,2,1,0:T(8,128)(2,1)S(1)} %get-tuple-element.23), kind=kLoop, calls=%fused_computation.193 | loop fusion | flops 294912 | bytes 884736 | tf_op jit(solution)/shard_map/jvp()/convert_element_type | solution.py:103
  41.6 2.3 %reshape.674 = f32[2,3,2,12,2,512]{5,4,3,2,1,0:T(2,128)} reshape(f32[2,6,24,512]{3,2,1,0:T(8,128)} %maximum_convert_fusion) | data formatting | bytes 1179648 | tf_op jit(solution)/shard_map/jvp()/convert_element_type | solution.py:103
  43.8 2.4 %copy.208 = f32[2,3,2,12,2,512]{5,2,4,0,3,1:T(2,128)} copy(f32[2,3,2,12,2,512]{5,4,3,2,1,0:T(2,128)} %reshape.674) | data formatting | bytes 1179648 | tf_op jit(solution)/shard_map/jvp()/convert_element_type | solution.py:103
  47.6 2.6 %reshape.670 = f32[2,3,12,2048]{3,0,2,1:T(2,128)} reshape(f32[2,3,12,2,2,512]{5,4,3,0,2,1:T(2,128)} %bitcast.252) | data formatting | bytes 1179648 | tf_op jit(solution)/shard_map/jvp()/convert_element_type | solution.py:103
  51.0 3.4 %fusion.51 = bf16[1,2,3,12,1024]{4,3,2,1,0:T(8,128)(2,1)S(1)} fusion(bf16[2048,1024]{1,0:T(8,128)(2,1)} %param.22, f32[2,3,12,2048]{3,0,2,1:T(2,128)} %reshape.670, f32[2048]{0:T(1024)S(1)} %copy-done.56, f32[2,3,12]{2,1,0:T(4,128)S(1)} %copy.116, f32[2,3,12]{2,1,0:T(4,128)S(1)} %copy.112), kind=kOutput, calls=%fused_computation.68 | convolution fusion | flops 302653440 | bytes 4940352 | tf_op jit(solution)/shard_map/jvp()/dot_general | solution.py:104
  58.8 1.6 %fusion.14 = bf16[2,6,12,1536]{3,2,1,0:T(8,128)(2,1)} fusion(bf16[2,6,12,1024]{3,2,1,0:T(8,128)(2,1)S(1)} %fusion.98, bf16[1024,1536]{1,0:T(8,128)(2,1)S(1)} %copy-done), kind=kOutput, calls=%fused_computation.18 | convolution fusion | flops 453206016 | bytes 3883008 | tf_op jit(solution)/shard_map/jvp()/dot_general | solution.py:177
  60.4 1.9 %reshape.651 = bf16[1,144,1536]{2,1,0:T(8,128)(2,1)} reshape(bf16[2,6,12,1536]{3,2,1,0:T(8,128)(2,1)} %fusion.14) | data formatting | bytes 884736 | tf_op jit(solution)/shard_map/jvp()/reshape;jvp()/transpose;jvp()/reshape | solution.py:38
  74.7 1.6 %reshape.655 = bf16[2,6,12,512]{3,2,1,0:T(8,128)(2,1)} reshape(bf16[144,512]{1,0:T(8,128)(2,1)} %fusion.49) | data formatting | bytes 294912 | tf_op jit(solution)/shard_map/jvp()/reshape;jvp()/transpose;jvp()/reshape | solution.py:46
  76.3 1.8 %fusion.235 = (f32[2,6,12]{2,1,0:T(8,128)S(1)}, f32[2,6,12,1024]{3,2,1,0:T(8,128)S(1)}) fusion(bf16[2,6,12,512]{3,2,1,0:T(8,128)(2,1)} %reshape.655, bf16[512,1024]{1,0:T(8,128)(2,1)} %param.24), kind=kOutput, calls=%fused_computation.343 | convolution fusion | flops 151142256 | bytes 1786432 | tf_op jit(solution)/shard_map/jvp()/dot_general | solution.py:93
  80.9 2.7 %fusion.10 = bf16[1,1152,512]{1,2,0:T(8,128)(2,1)} fusion(bf16[144,512]{1,0:T(8,128)(2,1)S(1)} %reshape.656, bf16[144,1152]{1,0:T(8,128)(2,1)} %copy-done.101, s32[1152]{0:T(1024)S(1)} %copy-done.82, s32[512]{0:T(512)S(1)} %copy-done.60), kind=kOutput, calls=%fused_computation.12 | convolution fusion | flops 171638784 | bytes 1665536 | tf_op jit(solution)/shard_map/transpose(jvp(wqm,wmc->wqc))/dot_general | solution.py:84
  91.6 2.2 %reduce_sum.180 = bf16[512,144]{0,1:T(8,128)(2,1)} reduce(bf16[512,8,144]{0,2,1:T(8,128)(2,1)} %bitcast.258, bf16[]{:T(256)} %constant.119.clone.1), dimensions={1}, to_apply=%region_9.10 | reduce | flops 516096 | bytes 1327106 | tf_op jit(solution)/shard_map/transpose(jvp())/reduce_sum | solution.py:73
  95.2 2.1 %fusion.95 = bf16[1,144,512]{2,1,0:T(8,128)(2,1)} fusion(f32[144,8]{0,1:T(8,128)S(1)} %fusion.59, f32[1,144,512]{2,1,0:T(8,128)S(1)} %copy-done.28, bf16[512,144]{0,1:T(8,128)(2,1)} %reduce_sum.180, s32[512]{0:T(512)S(1)} %copy-done.60, bf16[1,144,1536]{2,1,0:T(8,128)(2,1)} %reshape.651), kind=kOutput, calls=%fused_computation.158 | convolution fusion | flops 7598080 | bytes 743936 | tf_op jit(solution)/shard_map/transpose(jvp())/dot_general | solution.py:61
  97.3 2.4 %copy.118 = bf16[1,1152,512]{2,1,0:T(8,128)(2,1)} copy(bf16[1,1152,512]{1,2,0:T(8,128)(2,1)} %fusion.10) | data formatting | bytes 2359296 | tf_op jit(solution)/shard_map/transpose(jvp(jit(_where)))/select_n | solution.py:83
  101.3 1.7 %pad_add_fusion.1 = bf16[1,144,1536]{2,1,0:T(8,128)(2,1)} fusion(bf16[1,144,512]{2,1,0:T(8,128)(2,1)S(1)} %copy-done.47, bf16[1,144,512]{2,1,0:T(8,128)(2,1)} %fusion.95, bf16[1,144,512]{2,1,0:T(8,128)(2,1)S(1)} %bitcast.262), kind=kLoop, calls=%fused_computation.150 | loop fusion | flops 1327104 | bytes 884736 | tf_op jit(solution)/shard_map/transpose(jvp())/add_any | solution.py:67
  103.0 1.9 %reshape.661 = bf16[2,6,12,1536]{3,2,1,0:T(8,128)(2,1)} reshape(bf16[1,144,1536]{2,1,0:T(8,128)(2,1)} %pad_add_fusion.1) | data formatting | bytes 884736 | tf_op jit(solution)/shard_map/transpose(jvp())/reshape;transpose(jvp())/transpose;transpose(jvp())/reshape | solution.py:34
  104.9 2.3 %fusion.4 = bf16[2,6,12,1024]{3,2,1,0:T(8,128)(2,1)S(1)} fusion(bf16[2,6,12,1536]{3,2,1,0:T(8,128)(2,1)} %reshape.661, bf16[1024,1536]{1,0:T(8,128)(2,1)S(1)} %copy-done), kind=kOutput, calls=%fused_computation.4 | convolution fusion | flops 452984832 | bytes 3883008 | tf_op jit(solution)/shard_map/transpose(jvp())/dot_general | solution.py:177
  107.3 3.9 %fusion.72 = (f32[2,3,12]{2,1,0:T(4,128)S(1)}, f32[2,3,12,2048]{3,2,1,0:T(8,128)S(1)}) fusion(f32[2,3,12,2048]{3,0,2,1:T(2,128)S(1)} %copy-done.1, f32[2,3,12]{2,1,0:T(4,128)S(1)} %copy-done.58, f32[2048]{0:T(1024)S(1)} %copy-done.56, bf16[2048,1024]{1,0:T(8,128)(2,1)} %param.22, bf16[2,6,12,1024]{3,2,1,0:T(8,128)(2,1)S(1)} %fusion.4, s32[]{:T(128)S(6)} %select_n.236, ...), kind=kOutput, calls=%fused_computation.101 | convolution fusion | flops 302948288 | bytes 5779748 | tf_op jit(solution)/shard_map/transpose(jvp())/dot_general | solution.py:104
  113.1 1.9 %copy.124 = bf16[2,3,2,12,2,512]{5,4,3,2,1,0:T(2,128)(2,1)} copy(bf16[2,3,2,12,2,512]{5,2,4,3,1,0:T(2,128)(2,1)} %bitcast.261) | data formatting | bytes 589824 | tf_op jit(solution)/shard_map/transpose(jvp())/transpose | solution.py:100
  116.2 2.0 %collective-permute-start.5 = (bf16[2,3,24,512]{3,2,1,0:T(8,128)(2,1)S(1)}, bf16[2,3,24,512]{3,2,1,0:T(8,128)(2,1)S(1)}, u32[]{:S(2)}, u32[]{:S(2)}) collective-permute-start(bf16[2,3,24,512]{3,2,1,0:T(8,128)(2,1)S(1)} %get-tuple-element.25), channel_id=1, source_target_pairs={{0,4},{4,8},{8,12},{12,16},{16,20},{20,24},{24,28},{28,0},{1,5},{5... | collective-permute-start | bytes 442376 | tf_op jit(solution)/shard_map/ppermute | solution.py:18
  118.1 2.1 %collective-permute-done.5 = bf16[2,3,24,512]{3,2,1,0:T(8,128)(2,1)S(1)} collective-permute-done((bf16[2,3,24,512]{3,2,1,0:T(8,128)(2,1)S(1)}, bf16[2,3,24,512]{3,2,1,0:T(8,128)(2,1)S(1)}, u32[]{:S(2)}, u32[]{:S(2)}) %collective-permute-start.5) | collective-permute-done | bytes 147488 | tf_op jit(solution)/shard_map/ppermute | solution.py:18
  120.6 5.3 %collective-permute-done.6 = bf16[2,6,6,512]{3,2,1,0:T(8,128)(2,1)S(1)} collective-permute-done((bf16[2,6,6,512]{3,2,1,0:T(8,128)(2,1)S(1)}, bf16[2,6,6,512]{3,2,1,0:T(8,128)(2,1)S(1)}, u32[]{:S(2)}, u32[]{:S(2)}) %collective-permute-start.6) | collective-permute-done | bytes 73760 | tf_op jit(solution)/shard_map/ppermute | solution.py:18
  136.4 1.8 %reduce_sum.186 = bf16[2,256,144]{1,2,0:T(8,128)(2,1)} reduce(bf16[2,256,4,144]{1,3,2,0:T(8,128)(2,1)} %bitcast.266, bf16[]{:T(256)} %constant.119.clone.1), dimensions={2}, to_apply=%region_15.16 | reduce | flops 221184 | bytes 737282 | tf_op jit(solution)/shard_map/transpose(jvp())/reduce_sum | solution.py:73
  139.5 2.0 %fusion.93 = bf16[2,144,256]{2,1,0:T(8,128)(2,1)} fusion(f32[2,144,4]{1,2,0:T(4,128)S(1)} %fusion.55, f32[2,144,256]{2,1,0:T(8,128)S(1)} %copy-done.26, bf16[2,256,144]{1,2,0:T(8,128)(2,1)} %reduce_sum.186, bf16[2,144,256]{2,0,1:T(2,128)(2,1)} %copy-done.38, s32[256]{0:T(256)S(1)} %copy-done.73), kind=kOutput, calls=%fused_computation.154 | convolution fusion | flops 4056064 | bytes 742912 | tf_op jit(solution)/shard_map/transpose(jvp())/dot_general | solution.py:61
  146.7 1.9 %collective-permute-done.7 = bf16[2,6,6,512]{3,2,1,0:T(8,128)(2,1)S(1)} collective-permute-done((bf16[2,6,6,512]{3,2,1,0:T(8,128)(2,1)S(1)}, bf16[2,6,6,512]{3,2,1,0:T(8,128)(2,1)S(1)}, u32[]{:S(2)}, u32[]{:S(2)}) %collective-permute-start.7) | collective-permute-done | bytes 73760 | tf_op jit(solution)/shard_map/ppermute | solution.py:18
  148.7 3.9 %collective-permute-start.8 = (bf16[2,3,24,512]{3,2,1,0:T(8,128)(2,1)S(1)}, bf16[2,3,24,512]{3,2,1,0:T(8,128)(2,1)S(1)}, u32[]{:S(2)}, u32[]{:S(2)}) collective-permute-start(bf16[2,3,24,512]{3,2,1,0:T(8,128)(2,1)S(1)} %get-tuple-element.22), channel_id=1, source_target_pairs={{0,28},{4,0},{8,4},{12,8},{16,12},{20,16},{24,20},{28,24},{1,29},{... | collective-permute-start | bytes 442376 | tf_op jit(solution)/shard_map/ppermute | solution.py:18
  153.5 2.8 %collective-permute-done.8 = bf16[2,3,24,512]{3,2,1,0:T(8,128)(2,1)S(1)} collective-permute-done((bf16[2,3,24,512]{3,2,1,0:T(8,128)(2,1)S(1)}, bf16[2,3,24,512]{3,2,1,0:T(8,128)(2,1)S(1)}, u32[]{:S(2)}, u32[]{:S(2)}) %collective-permute-start.8) | collective-permute-done | bytes 147488 | tf_op jit(solution)/shard_map/ppermute | solution.py:18
  (339 shorter events, 76.4 us)
Async XLA Ops:
  0.6 58.2 %copy-start = (bf16[1024,1536]{1,0:T(8,128)(2,1)S(1)}, bf16[1024,1536]{1,0:T(8,128)(2,1)}, u32[]{:S(2)}) copy-start(bf16[1024,1536]{1,0:T(8,128)(2,1)} %param.23) | copy-start | bytes 9437188
  4.1 9.4 %collective-permute-start = (bf16[2,3,24,512]{3,2,1,0:T(8,128)(2,1)}, bf16[2,3,24,512]{3,2,1,0:T(8,128)(2,1)S(1)}, u32[]{:S(2)}, u32[]{:S(2)}) collective-permute-start(bf16[2,3,24,512]{3,2,1,0:T(8,128)(2,1)} %get-tuple-element.27), channel_id=1, source_target_pairs={{0,4},{4,8},{8,12},{12,16},{16,20},{20,24},{24,28},{28,0},{1,5},{5... | collective-permute-start | bytes 442376 | tf_op jit(solution)/shard_map/ppermute | solution.py:18
  6.7 19.2 %copy-start.61 = (s32[576]{0:T(1024)}, s32[576]{0:T(1024)S(1)}, u32[]{:S(2)}) copy-start(s32[576]{0:T(1024)S(1)} %add_select_fusion.3) | copy-start | bytes 6916
  6.7 15.9 %copy-start.72 = (s32[256]{0:T(256)}, s32[256]{0:T(256)S(1)}, u32[]{:S(2)}) copy-start(s32[256]{0:T(256)S(1)} %and_select_fusion) | copy-start | bytes 3076
  13.5 10.6 %copy-start.87 = (f32[576]{0:T(1024)}, f32[576]{0:T(1024)S(1)}, u32[]{:S(2)}) copy-start(f32[576]{0:T(1024)S(1)} %convolution_reduce_fusion.1) | copy-start | bytes 6916
  13.5 5.5 %collective-permute-start.1 = (bf16[2,6,6,512]{3,2,1,0:T(8,128)(2,1)S(1)}, bf16[2,6,6,512]{3,2,1,0:T(8,128)(2,1)S(1)}, u32[]{:S(2)}, u32[]{:S(2)}) collective-permute-start(bf16[2,6,6,512]{3,2,1,0:T(8,128)(2,1)S(1)} %pad_maximum_fusion.8), channel_id=1, source_target_pairs={{0,1},{1,2},{2,3},{3,0},{4,5},{5,6},{6,7},{7,4},{8,9},{9,10},{10,1... | collective-permute-start | bytes 221192 | tf_op jit(solution)/shard_map/ppermute | solution.py:18
  14.9 21.6 %copy-start.80 = (s32[1152]{0:T(1024)}, s32[1152]{0:T(1024)S(1)}, u32[]{:S(2)}) copy-start(s32[1152]{0:T(1024)S(1)} %add_select_fusion.1) | copy-start | bytes 13828
  29.4 7.2 %copy-start.99 = (f32[8]{0:T(128)S(1)}, f32[8]{0:T(128)}, u32[]{:S(2)}) copy-start(f32[8]{0:T(128)} %param.26) | copy-start | bytes 100
  29.4 4.6 %collective-permute-start.2 = (bf16[2,6,6,512]{3,2,1,0:T(8,128)(2,1)S(1)}, bf16[2,6,6,512]{3,2,1,0:T(8,128)(2,1)S(1)}, u32[]{:S(2)}, u32[]{:S(2)}) collective-permute-start(bf16[2,6,6,512]{3,2,1,0:T(8,128)(2,1)S(1)} %slice.102), channel_id=1, source_target_pairs={{0,3},{1,0},{2,1},{3,2},{4,7},{5,4},{6,5},{7,6},{8,11},{9,8},{10,9... | collective-permute-start | bytes 221192 | tf_op jit(solution)/shard_map/ppermute | solution.py:18
  34.7 5.1 %collective-permute-start.3 = (bf16[2,3,24,512]{3,2,1,0:T(8,128)(2,1)}, bf16[2,3,24,512]{3,2,1,0:T(8,128)(2,1)}, u32[]{:S(2)}, u32[]{:S(2)}) collective-permute-start(bf16[2,3,24,512]{3,2,1,0:T(8,128)(2,1)} %get-tuple-element.24), channel_id=1, source_target_pairs={{0,28},{4,0},{8,4},{12,8},{16,12},{20,16},{24,20},{28,24},{1,29},{... | collective-permute-start | bytes 442376 | tf_op jit(solution)/shard_map/ppermute | solution.py:18
  36.3 18.1 %copy-start.37 = (bf16[2,3,12,1024]{3,2,1,0:T(8,128)(2,1)}, bf16[2,3,12,1024]{3,2,1,0:T(8,128)(2,1)S(1)}, u32[]{:S(2)}) copy-start(bf16[2,3,12,1024]{3,2,1,0:T(8,128)(2,1)S(1)} %copy.209) | copy-start | bytes 442372
  46.2 4.7 %copy-start.56 = (f32[2048]{0:T(1024)S(1)}, f32[2048]{0:T(1024)}, u32[]{:S(2)}) copy-start(f32[2048]{0:T(1024)} %param.21) | copy-start | bytes 24580
  47.6 6.8 %copy-start.57 = (f32[2,3,12]{2,1,0:T(4,128)}, f32[2,3,12]{2,1,0:T(4,128)S(1)}, u32[]{:S(2)}) copy-start(f32[2,3,12]{2,1,0:T(4,128)S(1)} %copy.112) | copy-start | bytes 868
  54.5 1.8 %collective-permute-start.4 = (bf16[2,2,3,12,1024]{4,3,2,1,0:T(8,128)(2,1)S(1)}, bf16[2,2,3,12,1024]{4,3,2,1,0:T(8,128)(2,1)S(1)}, u32[]{:S(2)}, u32[]{:S(2)}) collective-permute-start(bf16[2,2,3,12,1024]{4,3,2,1,0:T(8,128)(2,1)S(1)} %pad_maximum_fusion.1), channel_id=1, source_target_pairs={{0,4},{4,0},{8,12},{12,8},{16,20},{20,16},{24,28},{28,24},{1,5},{5... | collective-permute-start | bytes 884744 | tf_op jit(solution)/shard_map/ppermute | solution.py:22
  62.3 5.0 %copy-start.14 = (bf16[1,144,1536]{2,1,0:T(8,128)(2,1)S(1)}, bf16[1,144,1536]{2,1,0:T(8,128)(2,1)}, u32[]{:S(2)}) copy-start(bf16[1,144,1536]{2,1,0:T(8,128)(2,1)} %reshape.651) | copy-start | bytes 1327108
  62.3 5.7 %copy-start.59 = (s32[512]{0:T(512)S(1)}, s32[512]{0:T(512)}, u32[]{:S(2)}) copy-start(s32[512]{0:T(512)} %add_select_fusion.4) | copy-start | bytes 6148
  62.3 6.1 %copy-start.67 = (s32[8,144]{1,0:T(8,128)S(1)}, s32[8,144]{1,0:T(8,128)}, u32[]{:S(2)}) copy-start(s32[8,144]{1,0:T(8,128)} %add_select_fusion.2) | copy-start | bytes 13828
  90.5 4.7 %copy-start.28 = (f32[1,144,512]{2,1,0:T(8,128)S(1)}, f32[1,144,512]{2,1,0:T(8,128)}, u32[]{:S(2)}) copy-start(f32[1,144,512]{2,1,0:T(8,128)} %copy-done.27) | copy-start | bytes 884740
  115.0 11.8 %copy-start.66 = (f32[2,6,24]{2,1,0:T(8,128)S(1)}, f32[2,6,24]{2,1,0:T(8,128)}, u32[]{:S(2)}) copy-start(f32[2,6,24]{2,1,0:T(8,128)} %copy-done.65) | copy-start | bytes 3460
  116.1 9.8 %copy-start.3 = (f32[2,6,24,512]{3,2,1,0:T(8,128)S(1)}, f32[2,6,24,512]{3,2,1,0:T(8,128)}, u32[]{:S(2)}) copy-start(f32[2,6,24,512]{3,2,1,0:T(8,128)} %copy-done.2) | copy-start | bytes 1769476
  116.1 10.7 %copy-start.69 = (f32[2,6,24]{2,1,0:T(8,128)S(1)}, f32[2,6,24]{2,1,0:T(8,128)}, u32[]{:S(2)}) copy-start(f32[2,6,24]{2,1,0:T(8,128)} %copy-done.68) | copy-start | bytes 3460
  116.1 10.7 %copy-start.86 = (f32[512]{0:T(512)S(1)}, f32[512]{0:T(512)}, u32[]{:S(2)}) copy-start(f32[512]{0:T(512)} %param.19) | copy-start | bytes 6148
  116.2 11.1 %copy-start.35 = (bf16[2,3,24,512]{3,2,1,0:T(8,128)(2,1)}, bf16[2,3,24,512]{3,2,1,0:T(8,128)(2,1)S(1)}, u32[]{:S(2)}) copy-start(bf16[2,3,24,512]{3,2,1,0:T(8,128)(2,1)S(1)} %get-tuple-element.26) | copy-start | bytes 442372
  116.2 4.1 %collective-permute-start.5 = (bf16[2,3,24,512]{3,2,1,0:T(8,128)(2,1)S(1)}, bf16[2,3,24,512]{3,2,1,0:T(8,128)(2,1)S(1)}, u32[]{:S(2)}, u32[]{:S(2)}) collective-permute-start(bf16[2,3,24,512]{3,2,1,0:T(8,128)(2,1)S(1)} %get-tuple-element.25), channel_id=1, source_target_pairs={{0,4},{4,8},{8,12},{12,16},{16,20},{20,24},{24,28},{28,0},{1,5},{5... | collective-permute-start | bytes 442376 | tf_op jit(solution)/shard_map/ppermute | solution.py:18
  120.2 7.0 %copy-start.39 = (bf16[2,3,24,512]{3,2,1,0:T(8,128)(2,1)}, bf16[2,3,24,512]{3,2,1,0:T(8,128)(2,1)S(1)}, u32[]{:S(2)}) copy-start(bf16[2,3,24,512]{3,2,1,0:T(8,128)(2,1)S(1)} %collective-permute-done.5) | copy-start | bytes 442372
  120.2 7.0 %copy-start.55 = (bf16[256,512]{1,0:T(8,128)(2,1)S(1)}, bf16[256,512]{1,0:T(8,128)(2,1)}, u32[]{:S(2)}) copy-start(bf16[256,512]{1,0:T(8,128)(2,1)} %param.18) | copy-start | bytes 786436
  120.3 5.6 %collective-permute-start.6 = (bf16[2,6,6,512]{3,2,1,0:T(8,128)(2,1)S(1)}, bf16[2,6,6,512]{3,2,1,0:T(8,128)(2,1)S(1)}, u32[]{:S(2)}, u32[]{:S(2)}) collective-permute-start(bf16[2,6,6,512]{3,2,1,0:T(8,128)(2,1)S(1)} %pad_maximum_fusion.7), channel_id=1, source_target_pairs={{0,1},{1,2},{2,3},{3,0},{4,5},{5,6},{6,7},{7,4},{8,9},{9,10},{10,1... | collective-permute-start | bytes 221192 | tf_op jit(solution)/shard_map/ppermute | solution.py:18
  145.0 7.6 %copy-start.12 = (f32[2,6,12,1024]{3,2,1,0:T(8,128)S(1)}, f32[2,6,12,1024]{3,2,1,0:T(8,128)}, u32[]{:S(2)}) copy-start(f32[2,6,12,1024]{3,2,1,0:T(8,128)} %copy-done.11) | copy-start | bytes 1769476
  145.0 7.5 %copy-start.45 = (bf16[2,6,12,1024]{3,2,1,0:T(8,128)(2,1)S(1)}, bf16[2,6,12,1024]{3,2,1,0:T(8,128)(2,1)}, u32[]{:S(2)}) copy-start(bf16[2,6,12,1024]{3,2,1,0:T(8,128)(2,1)} %copy-done.44) | copy-start | bytes 884740
  145.1 7.5 %copy-start.75 = (f32[1024]{0:T(1024)S(1)}, f32[1024]{0:T(1024)}, u32[]{:S(2)}) copy-start(f32[1024]{0:T(1024)} %param.25) | copy-start | bytes 12292
  145.1 3.5 %collective-permute-start.7 = (bf16[2,6,6,512]{3,2,1,0:T(8,128)(2,1)S(1)}, bf16[2,6,6,512]{3,2,1,0:T(8,128)(2,1)S(1)}, u32[]{:S(2)}, u32[]{:S(2)}) collective-permute-start(bf16[2,6,6,512]{3,2,1,0:T(8,128)(2,1)S(1)} %slice.113), channel_id=1, source_target_pairs={{0,3},{1,0},{2,1},{3,2},{4,7},{5,4},{6,5},{7,6},{8,11},{9,8},{10,9... | collective-permute-start | bytes 221192 | tf_op jit(solution)/shard_map/ppermute | solution.py:18
  148.7 7.6 %collective-permute-start.8 = (bf16[2,3,24,512]{3,2,1,0:T(8,128)(2,1)S(1)}, bf16[2,3,24,512]{3,2,1,0:T(8,128)(2,1)S(1)}, u32[]{:S(2)}, u32[]{:S(2)}) collective-permute-start(bf16[2,3,24,512]{3,2,1,0:T(8,128)(2,1)S(1)} %get-tuple-element.22), channel_id=1, source_target_pairs={{0,28},{4,0},{8,4},{12,8},{16,12},{20,16},{24,20},{28,24},{1,29},{... | collective-permute-start | bytes 442376 | tf_op jit(solution)/shard_map/ppermute | solution.py:18
  (79 other events, 134.8 us)
where the time goes:
time: 159 us; the launch traced here: 157 us
  matrix products  52.1 us (33%)
  local copies, waits for them, and re-layouts  40.3 us (25%)
  other arithmetic  26.8 us (17%)
  waiting for transfers between devices  21.6 us (14%)
  starting transfers between devices  14.2 us (9%)
  between operations  1.99 us (1%)
    ppermute x8, waiting for transfers between devices, passed_along(): return lax.ppermute(x, axis, [(i, (i + by) % count) for i in range(count)])  21 us
    ppermute x8, starting transfers between devices, passed_along(): return lax.ppermute(x, axis, [(i, (i + by) % count) for i in range(count)])  14.1 us
    unnamed x206, local copies, waits for them, and re-layouts  12.3 us
    dot_general x8, matrix products, unit_rows(): jnp.dot(rows * rows, lane_member, precision=lax.Precision.HIGHEST)  9.7 us
    convert_element_type x3, local copies, waits for them, and re-layouts, merge_patches(): grouped.astype(jnp.float32)  7.29 us
    dot_general x2, matrix products, merge_patches(): jnp.dot(normed, weight, preferred_element_type=jnp.float32)  7.28 us
    dot_general x6, matrix products, attend(): jnp.einsum('wqm,wmc->wqc', probs, value_block, preferred_element_type=jnp...  6.37 us
    dot_general x8, matrix products, unit_rows(): jnp.dot(lax.rsqrt(squares + EPS_HEAD), lane_member.T, precision=lax.Preci...  5.7 us
  transfers between devices with their start and end apart: 9, of which 8 were waited for; matrix products, arithmetic and copies ran while one was open for 7% of the time, Pallas kernels for 0%

commit v1 on v0

v1 whole, which is shorter than its diff:
```python
import functools

import jax
import jax.numpy as jnp
import numpy as np
from jax import lax
from jax.experimental import pallas as pl
from jax.experimental.pallas import tpu as pltpu
from jax.sharding import PartitionSpec as P

HEADS = 4
HEADS2 = 8
WIN_LAT = 6
WIN_LON = 12

EPS_NORM = 1e-05
EPS_HEAD = 1e-06

F32 = jnp.float32
BF16 = jnp.bfloat16


def shifted_to(x, by_lat, by_lon):
    lats, lons = lax.axis_size("lat"), lax.axis_size("lon")
    pairs = [
        (i * lons + j, ((i + by_lat) % lats) * lons + (j + by_lon) % lons)
        for i in range(lats)
        for j in range(lons)
    ]
    return lax.ppermute(x, ("lat", "lon"), pairs)


def swapped(x):
    return lax.ppermute(x, "lat", [(i, i ^ 1) for i in range(lax.axis_size("lat"))])


def up8(n):
    return -(-n // 8) * 8


class Plan:
    def __init__(self, levels, height, breadth):
        half_lat, half_lon = WIN_LAT // 2, WIN_LON // 2
        assert height == WIN_LAT and breadth % WIN_LON == 0
        self.levels, self.height, self.breadth = levels, height, breadth
        self.cells = levels * height * breadth
        windows = breadth // WIN_LON
        cols = [(0, half_lon)]
        for w in range(1, windows):
            cols.append((half_lon + (w - 1) * WIN_LON, half_lon + w * WIN_LON))
        edge = [(breadth - half_lon, breadth)]

        def piece(first_row, ranges):
            rows, spans = [], []
            for low, high in ranges:
                cells = [
                    (l * height + r) * breadth + c
                    for l in range(levels)
                    for r in range(first_row, first_row + half_lat)
                    for c in range(low, high)
                ]
                spans.append((len(rows), up8(len(cells)), len(cells)))
                rows += cells + [-1] * (up8(len(cells)) - len(cells))
            return rows, spans

        a_rows, self.a_spans = piece(0, cols)
        b_rows, _ = piece(half_lat, cols)
        c_rows, self.c_spans = piece(0, edge)
        d_rows, _ = piece(half_lat, edge)
        self.sizes = [len(a_rows), len(b_rows), len(c_rows), len(d_rows)]
        order = np.array(a_rows + b_rows + c_rows + d_rows)
        self.rows = len(order)
        self.pack = (order[:, None] == np.arange(self.cells)[None, :]).astype(np.float32)
        half_h, half_b = height // 2, breadth // 2
        group = [
            (l * height + 2 * r + i) * breadth + 2 * c + j
            for j in range(2)
            for i in range(2)
            for l in range(levels)
            for r in range(half_h)
            for c in range(half_b)
        ]
        natural = (np.array(group)[:, None] == np.arange(self.cells)[None, :]).astype(np.float32)
        self.group = natural @ self.pack.T
        self.merged = levels * half_h * half_b
        self.masks = []
        for w in range(windows):
            size, real = self.a_spans[w][1], self.a_spans[w][2]
            block = np.where(np.arange(size) < real, 0, 2)
            upper = np.where(np.arange(size) < real, 1, 2)
            marks = [block, upper] + ([block, upper] if w == 0 else [])
            marks = np.concatenate(marks)
            flat = np.minimum(marks, 1) * (marks == 2)
            apart = (marks[:, None] == marks[None, :]).astype(np.float32)
            whole = (flat[:, None] == flat[None, :]).astype(np.float32)
            self.masks.append(np.stack([apart, whole]))

    def into_windows(self, a, b, c, d):
        result = []
        for w, (start, size, _) in enumerate(self.a_spans):
            parts = [a[start : start + size], b[start : start + size]]
            if w == 0:
                parts += [c, d]
            result.append(jnp.concatenate(parts, axis=0))
        return result

    def from_windows(self, windows):
        a, b = [], []
        for w, (_, size, _) in enumerate(self.a_spans):
            a.append(windows[w][:size])
            b.append(windows[w][size : 2 * size])
        base = 2 * self.a_spans[0][1]
        edge = self.c_spans[0][1]
        c = windows[0][base : base + edge]
        d = windows[0][base + edge :]
        return jnp.concatenate(a, axis=0), jnp.concatenate(b, axis=0), c, d


def mm(a, b):
    return lax.dot_general(a, b, (((1,), (0,)), ((), ())), preferred_element_type=F32)


def mm_t(a, b):
    return lax.dot_general(a, b, (((1,), (1,)), ((), ())), preferred_element_type=F32)


def t_mm(a, b):
    return lax.dot_general(a, b, (((0,), (0,)), ((), ())), preferred_element_type=F32)


def norm_parts(values):
    average = jnp.mean(values, axis=-1, keepdims=True)
    centred = values - average
    spread = jnp.mean(centred * centred, axis=-1, keepdims=True)
    factor = lax.rsqrt(spread + EPS_NORM)
    return centred * factor, factor


def norm_back(unit, factor, grad):
    first = jnp.mean(grad, axis=-1, keepdims=True)
    second = jnp.mean(grad * unit, axis=-1, keepdims=True)
    return factor * (grad - first - unit * second)


def head_lanes(lanes, size, index):
    lane = lax.broadcasted_iota(jnp.int32, (1, lanes), 1)
    return (lane >= index * size) & (lane < (index + 1) * size)


def head_mean_matrix(lanes, size):
    row = lax.broadcasted_iota(jnp.int32, (lanes, lanes), 0)
    col = lax.broadcasted_iota(jnp.int32, (lanes, lanes), 1)
    same = jnp.zeros((lanes, lanes), F32)
    for h in range(lanes // size):
        inside = (row >= h * size) & (row < (h + 1) * size) & (col >= h * size) & (col < (h + 1) * size)
        same = jnp.where(inside, 1.0 / size, same)
    return same.astype(BF16)


def unit_rows(rows, mean_matrix):
    squares = mm((rows * rows).astype(BF16), mean_matrix)
    factor = lax.rsqrt(squares + EPS_HEAD)
    return rows * factor, factor


def unit_back(unit, factor, grad, mean_matrix):
    overlap = mm((unit * grad).astype(BF16), mean_matrix)
    return factor * (grad - unit * overlap)


def spread_heads(rows, masks):
    return jnp.concatenate([jnp.where(m, rows, 0.0) for m in masks], axis=0).astype(BF16)


def join_heads(stacked, masks):
    n = stacked.shape[0] // len(masks)
    total = jnp.where(masks[0], stacked[:n], 0.0)
    for h in range(1, len(masks)):
        total = jnp.where(masks[h], stacked[h * n : (h + 1) * n], total)
    return total


def attend(query_stack, key_unit, values, masks, allowed):
    weights = jnp.exp(mm_t(query_stack, key_unit))
    if allowed is not None:
        weights = weights * jnp.concatenate([allowed] * len(masks), axis=0)
    totals = jnp.sum(weights, axis=-1, keepdims=True)
    probs = weights * (1.0 / totals)
    return probs


def attend_back(probs, query_stack, key_unit, values, mixture_grad, masks):
    grad_stack = spread_heads(mixture_grad, masks)
    probs_grad = mm_t(grad_stack, values)
    delta = jnp.sum(probs * probs_grad, axis=-1, keepdims=True)
    logits_grad = (probs * (probs_grad - delta)).astype(BF16)
    query_grad = join_heads(mm(logits_grad, key_unit), masks)
    key_grad = t_mm(logits_grad, query_stack)
    value_grad = t_mm(probs.astype(BF16), grad_stack)
    return query_grad, key_grad, value_grad


def bias_kernel(plan, tokens, land_sea, land_vector, pack, *outs):
    land = land_sea[...].astype(F32)
    breadth = plan.breadth
    eye = lax.broadcasted_iota(jnp.int32, (breadth, breadth), 0) == lax.broadcasted_iota(
        jnp.int32, (breadth, breadth), 1
    )
    vector = land_vector[...]
    rows = []
    for r in range(plan.height):
        column = jnp.sum(jnp.where(eye, land[r : r + 1, :], 0.0), axis=1, keepdims=True)
        rows.append(column * vector)
    biased = jnp.concatenate(
        [tokens[l, r].astype(F32) + rows[r] for l in range(plan.levels) for r in range(plan.height)],
        axis=0,
    ).astype(BF16)
    packed = mm(pack[...], biased)
    start = 0
    for out in outs:
        out[...] = packed[start : start + out.shape[0]].astype(BF16)
        start += out.shape[0]


def allowed_of(mask, first_band):
    return jnp.where(first_band, mask[0], mask[1])


def fine_window(rows, allowed, inward, outward, scale_lanes, masks, mean_matrix):
    inner = scale_lanes.shape[-1]
    packed = mm(rows.astype(BF16), inward).astype(BF16).astype(F32)
    query_unit, query_factor = unit_rows(packed[:, :inner], mean_matrix)
    key_unit, key_factor = unit_rows(packed[:, inner : 2 * inner], mean_matrix)
    values = packed[:, 2 * inner :].astype(BF16)
    query_stack = spread_heads(query_unit * scale_lanes, masks)
    probs = attend(query_stack, key_unit.astype(BF16), values, masks, allowed)
    mixture = join_heads(mm(probs.astype(BF16), values), masks).astype(BF16)
    unit, factor = norm_parts(mm(mixture, outward))
    return query_unit, query_factor, key_unit, key_factor, values, query_stack, probs, unit, factor


def scale_lanes_of(scales, masks, head_size):
    lanes = jnp.zeros(masks[0].shape, F32)
    for h, mask in enumerate(masks):
        lanes = jnp.where(mask, scales[h] / head_size, lanes)
    return lanes


def fine_setup(scales, inner):
    head_size = inner // HEADS
    masks = [head_lanes(inner, head_size, h) for h in range(HEADS)]
    return masks, scale_lanes_of(scales, masks, head_size), head_mean_matrix(inner, head_size)


def fine_kernel(plan, band, scales, a, b, c, d, inward, outward, gain, *rest):
    mask_refs, outs = rest[: len(plan.masks)], rest[len(plan.masks) :]
    masks, scale_lanes, mean_matrix = fine_setup(scales, outward.shape[0])
    first_band = band[0] == 0
    windows = plan.into_windows(*(x[...].astype(F32) for x in (a, b, c, d)))
    results = []
    for rows, mask in zip(windows, mask_refs):
        allowed = allowed_of(mask, first_band)
        unit = fine_window(
            rows, allowed, inward[...], outward[...], scale_lanes, masks, mean_matrix
        )[-2]
        results.append(rows + unit * gain[...])
    for out, value in zip(outs, plan.from_windows(results)):
        out[...] = value.astype(BF16)


def fine_back_kernel(plan, band, scales, a, b, c, d, ga, gb, gc, gd, inward, outward, gain, *rest):
    mask_refs, outs = rest[: len(plan.masks)], rest[len(plan.masks) :]
    masks, scale_lanes, mean_matrix = fine_setup(scales, outward.shape[0])
    first_band = band[0] == 0
    windows = plan.into_windows(*(x[...].astype(F32) for x in (a, b, c, d)))
    grads = plan.into_windows(*(x[...].astype(F32) for x in (ga, gb, gc, gd)))
    results = []
    for rows, grad, mask in zip(windows, grads, mask_refs):
        allowed = allowed_of(mask, first_band)
        query_unit, query_factor, key_unit, key_factor, values, query_stack, probs, unit, factor = (
            fine_window(rows, allowed, inward[...], outward[...], scale_lanes, masks, mean_matrix)
        )
        projected_grad = norm_back(unit, factor, grad * gain[...]).astype(BF16)
        mixture_grad = mm_t(projected_grad, outward[...])
        query_grad, key_grad, value_grad = attend_back(
            probs, query_stack, key_unit.astype(BF16), values, mixture_grad, masks
        )
        query_grad = unit_back(query_unit, query_factor, query_grad * scale_lanes, mean_matrix)
        key_grad = unit_back(key_unit, key_factor, key_grad, mean_matrix)
        packed_grad = jnp.concatenate(
            [query_grad.astype(BF16), key_grad.astype(BF16), value_grad.astype(BF16)], axis=1
        )
        results.append(grad + mm_t(packed_grad, inward[...]))
    for out, value in zip(outs, plan.from_windows(results)):
        out[...] = value.astype(BF16)


def merge_kernel(plan, a, b, c, d, group, gain, weight, coarse, grouped_out):
    pieces = jnp.concatenate([x[...].astype(F32) for x in (a, b, c, d)], axis=0).astype(BF16)
    rows = mm(group[...], pieces)
    n = plan.merged
    grouped = jnp.concatenate([rows[g * n : (g + 1) * n] for g in range(4)], axis=1)
    unit, _ = norm_parts(grouped)
    normed = (unit * gain[...]).astype(BF16)
    coarse[...] = mm(normed, weight[...]).astype(BF16)
    grouped_out[...] = grouped.astype(BF16)


def coarse_kernel(
    plan,
    scales,
    own,
    partner,
    own_cot,
    partner_cot,
    grouped,
    inward,
    outward,
    gain,
    merge_gain,
    merge_weight,
    ungroup,
    coarse_out,
    ga,
    gb,
    gc,
    gd,
    cot_rows,
    out_rows,
):
    inner = outward.shape[0]
    head_size = inner // HEADS2
    n = plan.merged
    half_b = plan.breadth // 2
    lines = [(l, r) for l in range(plan.levels) for r in range(plan.height // 2)]
    for k, (l, r) in enumerate(lines):
        cot_rows[k * half_b : (k + 1) * half_b, :] = own_cot[l, r].astype(F32)
        cot_rows[n + k * half_b : n + (k + 1) * half_b, :] = partner_cot[l, r].astype(F32)
    rows = jnp.concatenate([own[...].astype(F32), partner[...].astype(F32)], axis=0)
    packed = mm(rows.astype(BF16), inward[...]).astype(BF16).astype(F32)
    part = 256 if inner % 256 == 0 else inner
    per = part // head_size
    masks = [head_lanes(part, head_size, h) for h in range(per)]
    mean_matrix = head_mean_matrix(part, head_size)
    saved, mixtures = [], []
    for g in range(inner // part):
        low = g * part
        scale_lanes = scale_lanes_of([scales[g * per + h] for h in range(per)], masks, head_size)
        query_unit, query_factor = unit_rows(packed[:, low : low + part], mean_matrix)
        key_unit, key_factor = unit_rows(packed[:, inner + low : inner + low + part], mean_matrix)
        values = packed[:, 2 * inner + low : 2 * inner + low + part].astype(BF16)
        query_stack = spread_heads(query_unit * scale_lanes, masks)
        key_low = key_unit.astype(BF16)
        probs = attend(query_stack, key_low, values, masks, None)
        mixtures.append(join_heads(mm(probs.astype(BF16), values), masks).astype(BF16))
        saved.append(
            (query_unit, query_factor, key_unit, key_factor, values, query_stack, key_low, probs, scale_lanes)
        )
    unit, factor = norm_parts(mm(jnp.concatenate(mixtures, axis=1), outward[...]))
    out_rows[...] = rows[:n] + unit[:n] * gain[...]
    for k, (l, r) in enumerate(lines):
        coarse_out[l, r] = out_rows[k * half_b : (k + 1) * half_b, :].astype(BF16)

    cot = cot_rows[...]
    projected_grad = norm_back(unit, factor, cot * gain[...]).astype(BF16)
    mixture_grad = mm_t(projected_grad, outward[...])
    query_grads, key_grads, value_grads = [], [], []
    for g, (query_unit, query_factor, key_unit, key_factor, values, query_stack, key_low, probs, scale_lanes) in enumerate(saved):
        low = g * part
        query_grad, key_grad, value_grad = attend_back(
            probs, query_stack, key_low, values, mixture_grad[:, low : low + part], masks
        )
        query_grads.append(
            unit_back(query_unit[:n], query_factor[:n], query_grad[:n] * scale_lanes, mean_matrix).astype(BF16)
        )
        key_grads.append(unit_back(key_unit[:n], key_factor[:n], key_grad[:n], mean_matrix).astype(BF16))
        value_grads.append(value_grad[:n].astype(BF16))
    packed_grad = jnp.concatenate(query_grads + key_grads + value_grads, axis=1)
    coarse_grad = (cot[:n] + mm_t(packed_grad, inward[...])).astype(BF16)

    normed_grad = mm_t(coarse_grad, merge_weight[...])
    merge_unit, merge_factor = norm_parts(grouped[...].astype(F32))
    grouped_grad = norm_back(merge_unit, merge_factor, normed_grad * merge_gain[...])
    width = grouped_grad.shape[1] // 4
    stacked = jnp.concatenate(
        [grouped_grad[:, g * width : (g + 1) * width] for g in range(4)], axis=0
    ).astype(BF16)
    pieces = mm(ungroup[...], stacked)
    start = 0
    for out in (ga, gb, gc, gd):
        out[...] = pieces[start : start + out.shape[0]].astype(BF16)
        start += out.shape[0]


def unpack_kernel(plan, a, b, c, d, unpack, out):
    pieces = jnp.concatenate([x[...].astype(F32) for x in (a, b, c, d)], axis=0).astype(BF16)
    rows = mm(unpack[...], pieces)
    k = 0
    for l in range(plan.levels):
        for r in range(plan.height):
            out[l, r] = rows[k : k + plan.breadth].astype(BF16)
            k += plan.breadth


SMEM = functools.partial(pl.BlockSpec, memory_space=pltpu.SMEM)
VMEM = functools.partial(pl.BlockSpec, memory_space=pltpu.VMEM)


def call(kernel, name, outs, args, smem=0, scratch=()):
    specs = [SMEM()] * smem + [VMEM()] * (len(args) - smem)
    return pl.pallas_call(
        kernel,
        name=name,
        out_shape=outs,
        in_specs=specs,
        out_specs=[VMEM() for _ in outs],
        scratch_shapes=scratch,
        compiler_params=pltpu.CompilerParams(vmem_limit_bytes=56 * 1024 * 1024),
    )(*args)


def local(
    tokens,
    land_sea,
    land_vector,
    fine_inward,
    fine_outward,
    fine_gain,
    fine_scale,
    merge_gain,
    merge_weight,
    coarse_inward,
    coarse_outward,
    coarse_gain,
    coarse_scale,
    coarse_cotangent,
):
    levels, height, breadth, width = tokens.shape
    width2 = coarse_cotangent.shape[-1]
    plan = Plan(levels, height, breadth)
    pieces = [jax.ShapeDtypeStruct((n, width), BF16) for n in plan.sizes]
    constant = lambda x: jnp.asarray(x, BF16)
    row = lambda x: x.reshape(1, -1)
    band = lax.axis_index("lat").astype(jnp.int32).reshape(1)
    masks = [jnp.asarray(m, F32) for m in plan.masks]

    partner_cot = swapped(coarse_cotangent)

    def gather(a, b, c, d):
        return a, shifted_to(b, 1, 0), shifted_to(c, 0, 1), shifted_to(d, 1, 1)

    def give_back(a, b, c, d):
        return a, shifted_to(b, -1, 0), shifted_to(c, 0, -1), shifted_to(d, -1, -1)

    region = gather(
        *call(
            functools.partial(bias_kernel, plan),
            "bias",
            pieces,
            (tokens, land_sea, row(land_vector), constant(plan.pack)),
        )
    )
    fine_result = give_back(
        *call(
            functools.partial(fine_kernel, plan),
            "fine",
            pieces,
            (band, fine_scale, *region, fine_inward, fine_outward, row(fine_gain), *masks),
            smem=2,
        )
    )
    own, grouped = call(
        functools.partial(merge_kernel, plan),
        "merge",
        [
            jax.ShapeDtypeStruct((plan.merged, width2), BF16),
            jax.ShapeDtypeStruct((plan.merged, 4 * width), BF16),
        ],
        (*fine_result, constant(plan.group), row(merge_gain), merge_weight),
    )
    partner = swapped(own)
    coarse_output, *grads = call(
        functools.partial(coarse_kernel, plan),
        "coarse",
        [jax.ShapeDtypeStruct(coarse_cotangent.shape, BF16)] + pieces,
        (
            coarse_scale,
            own,
            partner,
            coarse_cotangent,
            partner_cot,
            grouped,
            coarse_inward,
            coarse_outward,
            row(coarse_gain),
            row(merge_gain),
            merge_weight,
            constant(plan.group.T),
        ),
        smem=1,
        scratch=[
            pltpu.VMEM((2 * plan.merged, width2), F32),
            pltpu.VMEM((plan.merged, width2), F32),
        ],
    )
    grads = gather(*grads)
    token_pieces = give_back(
        *call(
            functools.partial(fine_back_kernel, plan),
            "fine_back",
            pieces,
            (
                band,
                fine_scale,
                *region,
                *grads,
                fine_inward,
                fine_outward,
                row(fine_gain),
                *masks,
            ),
            smem=2,
        )
    )
    (token_grad,) = call(
        functools.partial(unpack_kernel, plan),
        "unpack",
        [jax.ShapeDtypeStruct(tokens.shape, BF16)],
        (*token_pieces, constant(plan.pack.T)),
    )
    return (coarse_output, token_grad)


def solution(mesh):
    whole, cells = P(), P(None, "lat", "lon", None)
    return jax.shard_map(
        local,
        mesh=mesh,
        in_specs=(cells, P("lat", "lon")) + (whole,) * 11 + (cells,),
        out_specs=(cells, cells),
        check_vma=False,
    )
```

time: 159 us -> 67.5 us (0.42); the launches traced: 157 us -> 67.3 us
  matrix products: 52.1 us -> 0 us
  local copies, waits for them, and re-layouts: 40.3 us -> 5.97 us
  Pallas kernels: 0 us -> 31.5 us
  other arithmetic: 26.8 us -> 0 us
  waiting for transfers between devices: 21.6 us -> 14.8 us
    dot_general x48 -> x0, matrix products: 52.1 us -> none  [the longest x8 9.7 us: unit_rows(): jnp.dot(rows * rows, lane_member, precision=lax.Precision.HIGHEST)]
    pallas_call x0 -> x6, Pallas kernels: none -> 31.5 us  [call(): pl.pallas_call(kernel, name=name, out_shape=outs, in_specs=specs, out_spe...]
    reduce_sum x12 -> x0, other arithmetic: 10.5 us -> none  [the longest x2 4.01 us: attend(): jnp.tile(jnp.swapaxes(key_unit, 1, 2), (1, 1, head_count))]
    convert_element_type x6 -> x0, local copies, waits for them, and re-layouts: 7.87 us -> none  [the longest x3 7.29 us: merge_patches(): grouped.astype(jnp.float32)]
    reshape x5 -> x0, local copies, waits for them, and re-layouts: 7.47 us -> none  [the longest x1 1.94 us: into_windows(): return blocks.reshape(-1, levels * WIN_LAT * WIN_LON, channels)]
    ppermute x9 -> x14, waiting for transfers between devices: 21.6 us -> 14.8 us  [the longest x12 13.2 us: shifted_to(): return lax.ppermute(x, ('lat', 'lon'), pairs)]
    unnamed x206 -> x32, local copies, waits for them, and re-layouts: 12.3 us -> 5.97 us
    another operation x6 -> x0, local copies, waits for them, and re-layouts: 5.3 us -> none  [the longest x2 4.13 us: attend(): weights = weights * jnp.tile(allowed, (1, 1, head_count))]
  transfers between devices with their start and end apart: 9 -> 14, of which waited for: 8 -> 7; matrix products, arithmetic and copies ran while one was open for 7% -> 4% of each run, Pallas kernels for 0% -> 7%
where the time goes in v1:
time: 67.5 us; the launch traced here: 67.3 us
  Pallas kernels  31.5 us (47%)
  waiting for transfers between devices  14.8 us (22%)
  starting transfers between devices  14.3 us (21%)
  local copies, waits for them, and re-layouts  5.97 us (9%)
  between operations  0.69 us (1%)
    pallas_call x6, Pallas kernels, call(): pl.pallas_call(kernel, name=name, out_shape=outs, in_specs=specs, out_spe...  31.5 us
    ppermute x12, starting transfers between devices, shifted_to(): return lax.ppermute(x, ('lat', 'lon'), pairs)  13.9 us
    ppermute x12, waiting for transfers between devices, shifted_to(): return lax.ppermute(x, ('lat', 'lon'), pairs)  13.2 us
    unnamed x32, local copies, waits for them, and re-layouts  5.97 us
    ppermute x2, waiting for transfers between devices, swapped(): lax.ppermute(x, 'lat', [(i, i ^ 1) for i in range(lax.axis_size('lat'))])  1.55 us
  transfers between devices with their start and end apart: 14, of which 7 were waited for; matrix products, arithmetic and copies ran while one was open for 4% of the time, Pallas kernels for 7%

profile of v1, /device:TPU:1, one launch (start us, length us, event | category | flops | bytes accessed | tf_op | source)
XLA Modules:
  0.0 67.3 jit_solution(5153864379679404493)
XLA Ops:
  0.6 2.1 %bias.1 = (bf16[112,512]{1,0:T(8,128)(2,1)}, bf16[112,512]{1,0:T(8,128)(2,1)}, bf16[40,512]{1,0:T(8,128)(2,1)}, bf16[40,512]{1,0:T(8,128)(2,1)}) custom-call(bf16[2,6,24,512]{3,2,1,0:T(8,128)(2,1)} %tokens.1, s32[6,24]{1,0:T(8,128)} %land_sea.1, f32[1,512]{1,0:T(1,128)} %bitcast.10, bf16[304,288]{1,0:T(8,128)(2,1)} %constant.20.clone.pack), custom_call_target="tpu_custom_call" | custom-call | tf_op jit(solution)/shard_map/bias/pallas_call | solution.py:411
  2.8 2.6 %collective-permute-start = (bf16[112,512]{1,0:T(8,128)(2,1)}, bf16[112,512]{1,0:T(8,128)(2,1)S(1)}, u32[]{:S(2)}, u32[]{:S(2)}) collective-permute-start(bf16[112,512]{1,0:T(8,128)(2,1)} %get-tuple-element.22), channel_id=1, source_target_pairs={{0,4},{1,5},{2,6},{3,7},{4,8},{5,9},{6,10},{7,11},{8,12},{9,13},{1... | collective-permute-start | bytes 344072 | tf_op jit(solution)/shard_map/ppermute | solution.py:30
  5.4 1.3 %collective-permute-start.1 = (bf16[40,512]{1,0:T(8,128)(2,1)}, bf16[40,512]{1,0:T(8,128)(2,1)S(1)}, u32[]{:S(2)}, u32[]{:S(2)}) collective-permute-start(bf16[40,512]{1,0:T(8,128)(2,1)} %get-tuple-element.23), channel_id=1, source_target_pairs={{0,1},{1,2},{2,3},{3,0},{4,5},{5,6},{6,7},{7,4},{8,9},{9,10},{10,1... | collective-permute-start | bytes 122888 | tf_op jit(solution)/shard_map/ppermute | solution.py:30
  6.6 1.3 %collective-permute-start.2 = (bf16[40,512]{1,0:T(8,128)(2,1)}, bf16[40,512]{1,0:T(8,128)(2,1)S(1)}, u32[]{:S(2)}, u32[]{:S(2)}) collective-permute-start(bf16[40,512]{1,0:T(8,128)(2,1)} %get-tuple-element.24), channel_id=1, source_target_pairs={{0,5},{1,6},{2,7},{3,4},{4,9},{5,10},{6,11},{7,8},{8,13},{9,14},{1... | collective-permute-start | bytes 122888 | tf_op jit(solution)/shard_map/ppermute | solution.py:30
  8.0 2.3 %collective-permute-done.1.c = bf16[40,512]{1,0:T(8,128)(2,1)S(1)} collective-permute-done((bf16[40,512]{1,0:T(8,128)(2,1)}, bf16[40,512]{1,0:T(8,128)(2,1)S(1)}, u32[]{:S(2)}, u32[]{:S(2)}) %collective-permute-start.1) | collective-permute-done | bytes 40992 | tf_op jit(solution)/shard_map/ppermute | solution.py:30
  10.3 2.1 %collective-permute-done.2.d = bf16[40,512]{1,0:T(8,128)(2,1)S(1)} collective-permute-done((bf16[40,512]{1,0:T(8,128)(2,1)}, bf16[40,512]{1,0:T(8,128)(2,1)S(1)}, u32[]{:S(2)}, u32[]{:S(2)}) %collective-permute-start.2) | collective-permute-done | bytes 40992 | tf_op jit(solution)/shard_map/ppermute | solution.py:30
  12.4 0.6 copy-done.4
  13.0 4.4 %fine.1 = (bf16[112,512]{1,0:T(8,128)(2,1)}, bf16[112,512]{1,0:T(8,128)(2,1)}, bf16[40,512]{1,0:T(8,128)(2,1)}, bf16[40,512]{1,0:T(8,128)(2,1)}) custom-call(s32[1]{0:T(128)} %bitcast.band, f32[4]{0:T(128)} %scales.5, bf16[112,512]{1,0:T(8,128)(2,1)} %get-tuple-element.21.a, bf16[112,512]{1,0:T(8,128)(2,1)} %copy-done.1, bf16[40,512]{1,0:T(8,128)(2,1)} %copy-done.3, ...), custom_call_target="tpu_custom_call" | custom-call | tf_op jit(solution)/shard_map/fine/pallas_call | solution.py:411
  17.4 0.7 %collective-permute-start.3 = (bf16[112,512]{1,0:T(8,128)(2,1)}, bf16[112,512]{1,0:T(8,128)(2,1)S(1)}, u32[]{:S(2)}, u32[]{:S(2)}) collective-permute-start(bf16[112,512]{1,0:T(8,128)(2,1)} %get-tuple-element.26), channel_id=1, source_target_pairs={{0,28},{1,29},{2,30},{3,31},{4,0},{5,1},{6,2},{7,3},{8,4},{9,5},{1... | collective-permute-start | bytes 344072 | tf_op jit(solution)/shard_map/ppermute | solution.py:30
  18.1 1.1 %collective-permute-start.4 = (bf16[40,512]{1,0:T(8,128)(2,1)}, bf16[40,512]{1,0:T(8,128)(2,1)S(1)}, u32[]{:S(2)}, u32[]{:S(2)}) collective-permute-start(bf16[40,512]{1,0:T(8,128)(2,1)} %get-tuple-element.27), channel_id=1, source_target_pairs={{0,3},{1,0},{2,1},{3,2},{4,7},{5,4},{6,5},{7,6},{8,11},{9,8},{10,9... | collective-permute-start | bytes 122888 | tf_op jit(solution)/shard_map/ppermute | solution.py:30
  19.3 1.5 %collective-permute-start.5 = (bf16[40,512]{1,0:T(8,128)(2,1)}, bf16[40,512]{1,0:T(8,128)(2,1)S(1)}, u32[]{:S(2)}, u32[]{:S(2)}) collective-permute-start(bf16[40,512]{1,0:T(8,128)(2,1)} %get-tuple-element.28), channel_id=1, source_target_pairs={{0,31},{1,28},{2,29},{3,30},{4,3},{5,0},{6,1},{7,2},{8,7},{9,4},{1... | collective-permute-start | bytes 122888 | tf_op jit(solution)/shard_map/ppermute | solution.py:30
  20.8 0.9 %copy.23.own_cot = bf16[2,3,12,1024]{3,2,1,0:T(8,128)(2,1)S(1)} copy(bf16[2,3,12,1024]{3,0,2,1:T(2,128)(2,1)} %param.33) | data formatting | bytes 294912 | tf_op args[13]
  21.8 0.4 collective-permute-start.7
  22.2 1.6 %collective-permute-done.5.d = bf16[40,512]{1,0:T(8,128)(2,1)S(1)} collective-permute-done((bf16[40,512]{1,0:T(8,128)(2,1)}, bf16[40,512]{1,0:T(8,128)(2,1)S(1)}, u32[]{:S(2)}, u32[]{:S(2)}) %collective-permute-start.5) | collective-permute-done | bytes 40992 | tf_op jit(solution)/shard_map/ppermute | solution.py:30
  23.8 0.6 copy-done.10
  24.5 4.5 %merge.1 = (bf16[72,1024]{1,0:T(8,128)(2,1)}, bf16[72,2048]{1,0:T(8,128)(2,1)}) custom-call(bf16[112,512]{1,0:T(8,128)(2,1)} %get-tuple-element.25.a, bf16[112,512]{1,0:T(8,128)(2,1)} %copy-done.8, bf16[40,512]{1,0:T(8,128)(2,1)} %copy-done.9, bf16[40,512]{1,0:T(8,128)(2,1)} %copy-done.10, bf16[288,304]{1,0:T(8,128)(2,1)} %constant.21.clone.group, ...), custom_call_target="tpu_custom_call" | custom-call | tf_op jit(solution)/shard_map/merge/pallas_call | solution.py:411
  29.0 1.5 %collective-permute-done.6.partner = bf16[72,1024]{1,0:T(8,128)(2,1)S(1)} collective-permute-done((bf16[72,1024]{1,0:T(8,128)(2,1)}, bf16[72,1024]{1,0:T(8,128)(2,1)S(1)}, u32[]{:S(2)}, u32[]{:S(2)}) %collective-permute-start.6) | collective-permute-done | bytes 147488 | tf_op jit(solution)/shard_map/ppermute | solution.py:34
  30.6 0.6 copy-done.5
  31.2 11.2 %coarse.1 = (bf16[2,3,12,1024]{3,2,1,0:T(8,128)(2,1)}, bf16[112,512]{1,0:T(8,128)(2,1)}, bf16[112,512]{1,0:T(8,128)(2,1)}, bf16[40,512]{1,0:T(8,128)(2,1)}, bf16[40,512]{1,0:T(8,128)(2,1)}) custom-call(f32[8]{0:T(128)} %scales.4, bf16[72,1024]{1,0:T(8,128)(2,1)} %get-tuple-element.29.own, bf16[72,1024]{1,0:T(8,128)(2,1)} %copy-done.5, ...), custom_call_target="tpu_custom_call" | custom-call | tf_op jit(solution)/shard_map/coarse/pallas_call | solution.py:411
  42.4 1.4 %collective-permute-start.8 = (bf16[112,512]{1,0:T(8,128)(2,1)}, bf16[112,512]{1,0:T(8,128)(2,1)S(1)}, u32[]{:S(2)}, u32[]{:S(2)}) collective-permute-start(bf16[112,512]{1,0:T(8,128)(2,1)} %get-tuple-element.33), channel_id=1, source_target_pairs={{0,4},{1,5},{2,6},{3,7},{4,8},{5,9},{6,10},{7,11},{8,12},{9,13},{1... | collective-permute-start | bytes 344072 | tf_op jit(solution)/shard_map/ppermute | solution.py:30
  44.2 0.6 collective-permute-start.10
  44.8 3.8 %collective-permute-done.9.gc = bf16[40,512]{1,0:T(8,128)(2,1)S(1)} collective-permute-done((bf16[40,512]{1,0:T(8,128)(2,1)}, bf16[40,512]{1,0:T(8,128)(2,1)S(1)}, u32[]{:S(2)}, u32[]{:S(2)}) %collective-permute-start.9) | collective-permute-done | bytes 40992 | tf_op jit(solution)/shard_map/ppermute | solution.py:30
  48.6 1.5 %collective-permute-done.10.gd = bf16[40,512]{1,0:T(8,128)(2,1)S(1)} collective-permute-done((bf16[40,512]{1,0:T(8,128)(2,1)}, bf16[40,512]{1,0:T(8,128)(2,1)S(1)}, u32[]{:S(2)}, u32[]{:S(2)}) %collective-permute-start.10) | collective-permute-done | bytes 40992 | tf_op jit(solution)/shard_map/ppermute | solution.py:30
  50.2 0.6 copy-done.14
  50.8 7.2 %fine_back.1 = (bf16[112,512]{1,0:T(8,128)(2,1)}, bf16[112,512]{1,0:T(8,128)(2,1)}, bf16[40,512]{1,0:T(8,128)(2,1)}, bf16[40,512]{1,0:T(8,128)(2,1)}) custom-call(s32[1]{0:T(128)} %bitcast.band, f32[4]{0:T(128)} %scales.5, bf16[112,512]{1,0:T(8,128)(2,1)} %get-tuple-element.21.a, bf16[112,512]{1,0:T(8,128)(2,1)} %copy-done.1, bf16[40,512]{1,0:T(8,128)(2,1)} %copy-done.3, ...), custom_call_target="tpu_custom_call" | custom-call | tf_op jit(solution)/shard_map/fine_back/pallas_call | solution.py:411
  58.0 1.0 %collective-permute-start.11 = (bf16[112,512]{1,0:T(8,128)(2,1)}, bf16[112,512]{1,0:T(8,128)(2,1)S(1)}, u32[]{:S(2)}, u32[]{:S(2)}) collective-permute-start(bf16[112,512]{1,0:T(8,128)(2,1)} %get-tuple-element.37), channel_id=1, source_target_pairs={{0,28},{1,29},{2,30},{3,31},{4,0},{5,1},{6,2},{7,3},{8,4},{9,5},{1... | collective-permute-start | bytes 344072 | tf_op jit(solution)/shard_map/ppermute | solution.py:30
  59.0 0.9 %collective-permute-start.12 = (bf16[40,512]{1,0:T(8,128)(2,1)}, bf16[40,512]{1,0:T(8,128)(2,1)S(1)}, u32[]{:S(2)}, u32[]{:S(2)}) collective-permute-start(bf16[40,512]{1,0:T(8,128)(2,1)} %get-tuple-element.38), channel_id=1, source_target_pairs={{0,3},{1,0},{2,1},{3,2},{4,7},{5,4},{6,5},{7,6},{8,11},{9,8},{10,9... | collective-permute-start | bytes 122888 | tf_op jit(solution)/shard_map/ppermute | solution.py:30
  59.9 0.9 %collective-permute-start.13 = (bf16[40,512]{1,0:T(8,128)(2,1)}, bf16[40,512]{1,0:T(8,128)(2,1)S(1)}, u32[]{:S(2)}, u32[]{:S(2)}) collective-permute-start(bf16[40,512]{1,0:T(8,128)(2,1)} %get-tuple-element.39), channel_id=1, source_target_pairs={{0,31},{1,28},{2,29},{3,30},{4,3},{5,0},{6,1},{7,2},{8,7},{9,4},{1... | collective-permute-start | bytes 122888 | tf_op jit(solution)/shard_map/ppermute | solution.py:30
  60.9 1.7 %copy.24 = bf16[2,3,12,1024]{3,0,2,1:T(2,128)(2,1)} copy(bf16[2,3,12,1024]{3,2,1,0:T(8,128)(2,1)} %get-tuple-element.40) | data formatting | bytes 294912
  62.6 1.9 %collective-permute-done.13.d = bf16[40,512]{1,0:T(8,128)(2,1)S(1)} collective-permute-done((bf16[40,512]{1,0:T(8,128)(2,1)}, bf16[40,512]{1,0:T(8,128)(2,1)S(1)}, u32[]{:S(2)}, u32[]{:S(2)}) %collective-permute-start.13) | collective-permute-done | bytes 40992 | tf_op jit(solution)/shard_map/ppermute | solution.py:30
  64.5 0.6 copy-done.12
  65.2 2.1 %unpack.2 = bf16[2,6,24,512]{3,2,1,0:T(8,128)(2,1)} custom-call(bf16[112,512]{1,0:T(8,128)(2,1)} %get-tuple-element.36.a, bf16[112,512]{1,0:T(8,128)(2,1)} %copy-done.6, bf16[40,512]{1,0:T(8,128)(2,1)} %copy-done.11, bf16[40,512]{1,0:T(8,128)(2,1)} %copy-done.12, bf16[288,304]{1,0:T(8,128)(2,1)} %constant.23.clone.unpack), custom_call_target="tpu_custom_call" | custom-call | tf_op jit(solution)/shard_map/unpack/pallas_call | solution.py:411
  (34 shorter events, 0.7 us)
Async XLA Ops:
  2.8 9.6 %collective-permute-start = (bf16[112,512]{1,0:T(8,128)(2,1)}, bf16[112,512]{1,0:T(8,128)(2,1)S(1)}, u32[]{:S(2)}, u32[]{:S(2)}) collective-permute-start(bf16[112,512]{1,0:T(8,128)(2,1)} %get-tuple-element.22), channel_id=1, source_target_pairs={{0,4},{1,5},{2,6},{3,7},{4,8},{5,9},{6,10},{7,11},{8,12},{9,13},{1... | collective-permute-start | bytes 344072 | tf_op jit(solution)/shard_map/ppermute | solution.py:30
  5.4 4.9 %collective-permute-start.1 = (bf16[40,512]{1,0:T(8,128)(2,1)}, bf16[40,512]{1,0:T(8,128)(2,1)S(1)}, u32[]{:S(2)}, u32[]{:S(2)}) collective-permute-start(bf16[40,512]{1,0:T(8,128)(2,1)} %get-tuple-element.23), channel_id=1, source_target_pairs={{0,1},{1,2},{2,3},{3,0},{4,5},{5,6},{6,7},{7,4},{8,9},{9,10},{10,1... | collective-permute-start | bytes 122888 | tf_op jit(solution)/shard_map/ppermute | solution.py:30
  6.6 5.7 %collective-permute-start.2 = (bf16[40,512]{1,0:T(8,128)(2,1)}, bf16[40,512]{1,0:T(8,128)(2,1)S(1)}, u32[]{:S(2)}, u32[]{:S(2)}) collective-permute-start(bf16[40,512]{1,0:T(8,128)(2,1)} %get-tuple-element.24), channel_id=1, source_target_pairs={{0,5},{1,6},{2,7},{3,4},{4,9},{5,10},{6,11},{7,8},{8,13},{9,14},{1... | collective-permute-start | bytes 122888 | tf_op jit(solution)/shard_map/ppermute | solution.py:30
  10.3 2.1 %copy-start.3 = (bf16[40,512]{1,0:T(8,128)(2,1)}, bf16[40,512]{1,0:T(8,128)(2,1)S(1)}, u32[]{:S(2)}) copy-start(bf16[40,512]{1,0:T(8,128)(2,1)S(1)} %collective-permute-done.1.c) | copy-start | bytes 122884
  12.4 0.6 copy-start.4
  12.4 0.7 copy-start.1
  17.4 6.4 %collective-permute-start.3 = (bf16[112,512]{1,0:T(8,128)(2,1)}, bf16[112,512]{1,0:T(8,128)(2,1)S(1)}, u32[]{:S(2)}, u32[]{:S(2)}) collective-permute-start(bf16[112,512]{1,0:T(8,128)(2,1)} %get-tuple-element.26), channel_id=1, source_target_pairs={{0,28},{1,29},{2,30},{3,31},{4,0},{5,1},{6,2},{7,3},{8,4},{9,5},{1... | collective-permute-start | bytes 344072 | tf_op jit(solution)/shard_map/ppermute | solution.py:30
  18.1 4.1 %collective-permute-start.4 = (bf16[40,512]{1,0:T(8,128)(2,1)}, bf16[40,512]{1,0:T(8,128)(2,1)S(1)}, u32[]{:S(2)}, u32[]{:S(2)}) collective-permute-start(bf16[40,512]{1,0:T(8,128)(2,1)} %get-tuple-element.27), channel_id=1, source_target_pairs={{0,3},{1,0},{2,1},{3,2},{4,7},{5,4},{6,5},{7,6},{8,11},{9,8},{10,9... | collective-permute-start | bytes 122888 | tf_op jit(solution)/shard_map/ppermute | solution.py:30
  19.3 4.5 %collective-permute-start.5 = (bf16[40,512]{1,0:T(8,128)(2,1)}, bf16[40,512]{1,0:T(8,128)(2,1)S(1)}, u32[]{:S(2)}, u32[]{:S(2)}) collective-permute-start(bf16[40,512]{1,0:T(8,128)(2,1)} %get-tuple-element.28), channel_id=1, source_target_pairs={{0,31},{1,28},{2,29},{3,30},{4,3},{5,0},{6,1},{7,2},{8,7},{9,4},{1... | collective-permute-start | bytes 122888 | tf_op jit(solution)/shard_map/ppermute | solution.py:30
  21.8 8.8 %copy-start = (bf16[2,3,12,1024]{3,2,1,0:T(8,128)(2,1)}, bf16[2,3,12,1024]{3,2,1,0:T(8,128)(2,1)S(1)}, u32[]{:S(2)}) copy-start(bf16[2,3,12,1024]{3,2,1,0:T(8,128)(2,1)S(1)} %copy.23.own_cot) | copy-start | bytes 442372
  21.8 7.2 %collective-permute-start.7 = (bf16[2,3,12,1024]{3,2,1,0:T(8,128)(2,1)S(1)}, bf16[2,3,12,1024]{3,2,1,0:T(8,128)(2,1)S(1)}, u32[]{:S(2)}, u32[]{:S(2)}) collective-permute-start(bf16[2,3,12,1024]{3,2,1,0:T(8,128)(2,1)S(1)} %copy.23.own_cot), channel_id=1, source_target_pairs={{0,4},{4,0},{8,12},{12,8},{16,20},{20,16},{24,28},{28,24},{1,5},{5... | collective-permute-start | bytes 442376 | tf_op jit(solution)/shard_map/ppermute | solution.py:34
  22.2 1.6 %copy-start.9 = (bf16[40,512]{1,0:T(8,128)(2,1)}, bf16[40,512]{1,0:T(8,128)(2,1)S(1)}, u32[]{:S(2)}) copy-start(bf16[40,512]{1,0:T(8,128)(2,1)S(1)} %collective-permute-done.4.c) | copy-start | bytes 122884
  23.8 0.6 copy-start.10
  23.8 0.7 copy-start.8
  29.0 1.6 %collective-permute-start.6 = (bf16[72,1024]{1,0:T(8,128)(2,1)}, bf16[72,1024]{1,0:T(8,128)(2,1)S(1)}, u32[]{:S(2)}, u32[]{:S(2)}) collective-permute-start(bf16[72,1024]{1,0:T(8,128)(2,1)} %get-tuple-element.29.own), channel_id=1, source_target_pairs={{0,4},{4,0},{8,12},{12,8},{16,20},{20,16},{24,28},{28,24},{1,5},{5... | collective-permute-start | bytes 442376 | tf_op jit(solution)/shard_map/ppermute | solution.py:34
  29.0 1.6 %copy-start.2 = (bf16[2,3,12,1024]{3,2,1,0:T(8,128)(2,1)}, bf16[2,3,12,1024]{3,2,1,0:T(8,128)(2,1)S(1)}, u32[]{:S(2)}) copy-start(bf16[2,3,12,1024]{3,2,1,0:T(8,128)(2,1)S(1)} %collective-permute-done.7.partner_cot) | copy-start | bytes 442372
  30.6 0.7 copy-start.5
  42.4 7.8 %collective-permute-start.8 = (bf16[112,512]{1,0:T(8,128)(2,1)}, bf16[112,512]{1,0:T(8,128)(2,1)S(1)}, u32[]{:S(2)}, u32[]{:S(2)}) collective-permute-start(bf16[112,512]{1,0:T(8,128)(2,1)} %get-tuple-element.33), channel_id=1, source_target_pairs={{0,4},{1,5},{2,6},{3,7},{4,8},{5,9},{6,10},{7,11},{8,12},{9,13},{1... | collective-permute-start | bytes 344072 | tf_op jit(solution)/shard_map/ppermute | solution.py:30
  43.8 4.9 %collective-permute-start.9 = (bf16[40,512]{1,0:T(8,128)(2,1)}, bf16[40,512]{1,0:T(8,128)(2,1)S(1)}, u32[]{:S(2)}, u32[]{:S(2)}) collective-permute-start(bf16[40,512]{1,0:T(8,128)(2,1)} %get-tuple-element.34), channel_id=1, source_target_pairs={{0,1},{1,2},{2,3},{3,0},{4,5},{5,6},{6,7},{7,4},{8,9},{9,10},{10,1... | collective-permute-start | bytes 122888 | tf_op jit(solution)/shard_map/ppermute | solution.py:30
  44.2 6.0 %collective-permute-start.10 = (bf16[40,512]{1,0:T(8,128)(2,1)}, bf16[40,512]{1,0:T(8,128)(2,1)S(1)}, u32[]{:S(2)}, u32[]{:S(2)}) collective-permute-start(bf16[40,512]{1,0:T(8,128)(2,1)} %get-tuple-element.35), channel_id=1, source_target_pairs={{0,5},{1,6},{2,7},{3,4},{4,9},{5,10},{6,11},{7,8},{8,13},{9,14},{1... | collective-permute-start | bytes 122888 | tf_op jit(solution)/shard_map/ppermute | solution.py:30
  48.6 1.5 %copy-start.13 = (bf16[40,512]{1,0:T(8,128)(2,1)}, bf16[40,512]{1,0:T(8,128)(2,1)S(1)}, u32[]{:S(2)}) copy-start(bf16[40,512]{1,0:T(8,128)(2,1)S(1)} %collective-permute-done.9.gc) | copy-start | bytes 122884
  50.2 0.6 copy-start.14
  50.2 0.7 copy-start.7
  58.0 6.5 %collective-permute-start.11 = (bf16[112,512]{1,0:T(8,128)(2,1)}, bf16[112,512]{1,0:T(8,128)(2,1)S(1)}, u32[]{:S(2)}, u32[]{:S(2)}) collective-permute-start(bf16[112,512]{1,0:T(8,128)(2,1)} %get-tuple-element.37), channel_id=1, source_target_pairs={{0,28},{1,29},{2,30},{3,31},{4,0},{5,1},{6,2},{7,3},{8,4},{9,5},{1... | collective-permute-start | bytes 344072 | tf_op jit(solution)/shard_map/ppermute | solution.py:30
  59.0 3.6 %collective-permute-start.12 = (bf16[40,512]{1,0:T(8,128)(2,1)}, bf16[40,512]{1,0:T(8,128)(2,1)S(1)}, u32[]{:S(2)}, u32[]{:S(2)}) collective-permute-start(bf16[40,512]{1,0:T(8,128)(2,1)} %get-tuple-element.38), channel_id=1, source_target_pairs={{0,3},{1,0},{2,1},{3,2},{4,7},{5,4},{6,5},{7,6},{8,11},{9,8},{10,9... | collective-permute-start | bytes 122888 | tf_op jit(solution)/shard_map/ppermute | solution.py:30
  59.9 4.5 %collective-permute-start.13 = (bf16[40,512]{1,0:T(8,128)(2,1)}, bf16[40,512]{1,0:T(8,128)(2,1)S(1)}, u32[]{:S(2)}, u32[]{:S(2)}) collective-permute-start(bf16[40,512]{1,0:T(8,128)(2,1)} %get-tuple-element.39), channel_id=1, source_target_pairs={{0,31},{1,28},{2,29},{3,30},{4,3},{5,0},{6,1},{7,2},{8,7},{9,4},{1... | collective-permute-start | bytes 122888 | tf_op jit(solution)/shard_map/ppermute | solution.py:30
  62.6 1.9 %copy-start.11 = (bf16[40,512]{1,0:T(8,128)(2,1)}, bf16[40,512]{1,0:T(8,128)(2,1)S(1)}, u32[]{:S(2)}) copy-start(bf16[40,512]{1,0:T(8,128)(2,1)S(1)} %collective-permute-done.12.c) | copy-start | bytes 122884
  64.5 0.6 copy-start.12
  64.5 0.7 copy-start.6

commit v2 on v1

--- a/solution.py
+++ b/solution.py
@@ -406,8 +406,13 @@
 VMEM = functools.partial(pl.BlockSpec, memory_space=pltpu.VMEM)
 
 
-def call(kernel, name, outs, args, smem=0, scratch=()):
+def call(kernel, name, outs, args, smem=0, scratch=(), keep_in=True, keep_out=True):
     specs = [SMEM()] * smem + [VMEM()] * (len(args) - smem)
+    space = pltpu.VMEM if keep_in else pltpu.HBM
+    near = tuple(pltpu.with_memory_space_constraint(x, space) for x in args[smem:])
+    args = tuple(args[:smem]) + near
+    if keep_out:
+        outs = [pltpu.VMEM(o.shape, o.dtype) for o in outs]
     return pl.pallas_call(
         kernel,
         name=name,
@@ -415,8 +420,32 @@
         in_specs=specs,
         out_specs=[VMEM() for _ in outs],
         scratch_shapes=scratch,
-        compiler_params=pltpu.CompilerParams(vmem_limit_bytes=56 * 1024 * 1024),
+        compiler_params=pltpu.CompilerParams(vmem_limit_bytes=24 * 1024 * 1024),
     )(*args)
+
+
+def load_kernel(after, *refs):
+    n = (len(refs) - 1) // 2
+    sems = refs[-1]
+    copies = [pltpu.make_async_copy(refs[k], refs[n + k], sems.at[k]) for k in range(n)]
+    for copy in copies:
+        copy.start()
+    for copy in copies:
+        copy.wait()
+
+
+def load(after, args):
+    anywhere = pl.BlockSpec(memory_space=pl.ANY)
+    args = tuple(pltpu.with_memory_space_constraint(x, pltpu.HBM) for x in args)
+    return pl.pallas_call(
+        load_kernel,
+        name="load",
+        out_shape=[pltpu.VMEM(x.shape, x.dtype) for x in args],
+        in_specs=[anywhere] * (len(args) + 1),
+        out_specs=[VMEM() for _ in args],
+        scratch_shapes=[pltpu.SemaphoreType.DMA((len(args),))],
+        compiler_params=pltpu.CompilerParams(vmem_limit_bytes=24 * 1024 * 1024),
+    )(after, *args)
 
 
 def local(
@@ -444,31 +473,61 @@
     band = lax.axis_index("lat").astype(jnp.int32).reshape(1)
     masks = [jnp.asarray(m, F32) for m in plan.masks]
 
-    partner_cot = swapped(coarse_cotangent)
-
     def gather(a, b, c, d):
         return a, shifted_to(b, 1, 0), shifted_to(c, 0, 1), shifted_to(d, 1, 1)
 
     def give_back(a, b, c, d):
         return a, shifted_to(b, -1, 0), shifted_to(c, 0, -1), shifted_to(d, -1, -1)
 
-    region = gather(
-        *call(
-            functools.partial(bias_kernel, plan),
-            "bias",
-            pieces,
-            (tokens, land_sea, row(land_vector), constant(plan.pack)),
-        )
-    )
+    biased = call(
+        functools.partial(bias_kernel, plan),
+        "bias",
+        pieces,
+        (tokens, land_sea, row(land_vector), constant(plan.pack)),
+        keep_in=False,
+    )
+    region = gather(*biased)
+    (
+        fine_inward,
+        fine_outward,
+        merge_weight,
+        coarse_inward,
+        coarse_outward,
+        fine_gain,
+        merge_gain,
+        coarse_gain,
+        group,
+        ungroup,
+        unpack,
+        *masks,
+    ) = load(
+        biased[0],
+        (
+            fine_inward,
+            fine_outward,
+            merge_weight,
+            coarse_inward,
+            coarse_outward,
+            row(fine_gain),
+            row(merge_gain),
+            row(coarse_gain),
+            constant(plan.group),
+            constant(plan.group.T),
+            constant(plan.pack.T),
+            *masks,
+        ),
+    )
+    fine_weights = (fine_inward, fine_outward, fine_gain, *masks)
     fine_result = give_back(
         *call(
             functools.partial(fine_kernel, plan),
             "fine",
             pieces,
-            (band, fine_scale, *region, fine_inward, fine_outward, row(fine_gain), *masks),
+            (band, fine_scale, *region, *fine_weights),
             smem=2,
         )
     )
+    partner_cot = swapped(coarse_cotangent)
     own, grouped = call(
         functools.partial(merge_kernel, plan),
         "merge",
@@ -476,7 +535,7 @@
             jax.ShapeDtypeStruct((plan.merged, width2), BF16),
             jax.ShapeDtypeStruct((plan.merged, 4 * width), BF16),
         ],
-        (*fine_result, constant(plan.group), row(merge_gain), merge_weight),
+        (*fine_result, group, merge_gain, merge_weight),
     )
     partner = swapped(own)
     coarse_output, *grads = call(
@@ -492,10 +551,10 @@
             grouped,
             coarse_inward,
             coarse_outward,
-            row(coarse_gain),
-            row(merge_gain),
+            coarse_gain,
+            merge_gain,
             merge_weight,
-            constant(plan.group.T),
+            ungroup,
         ),
         smem=1,
         scratch=[
@@ -509,16 +568,7 @@
             functools.partial(fine_back_kernel, plan),
             "fine_back",
             pieces,
-            (
-                band,
-                fine_scale,
-                *region,
-                *grads,
-                fine_inward,
-                fine_outward,
-                row(fine_gain),
-                *masks,
-            ),
+            (band, fine_scale, *region, *grads, *fine_weights),
             smem=2,
         )
     )
@@ -526,7 +576,8 @@
         functools.partial(unpack_kernel, plan),
         "unpack",
         [jax.ShapeDtypeStruct(tokens.shape, BF16)],
-        (*token_pieces, constant(plan.pack.T)),
+        (*token_pieces, unpack),
+        keep_out=False,
     )
     return (coarse_output, token_grad)
 

time: 67.5 us -> 52.4 us (0.78)
  Pallas kernels: 31.5 us -> 23.5 us
  local copies, waits for them, and re-layouts: 5.97 us -> 0.86 us
  waiting for transfers between devices: 14.8 us -> 11.3 us
  starting transfers between devices: 14.3 us -> 15.9 us
    pallas_call x6, Pallas kernels: 31.5 us -> 19.3 us  [call(): pl.pallas_call(kernel, name=name, out_shape=outs, in_specs=specs, out_spe...]
    unnamed x32 -> x8, local copies, waits for them, and re-layouts: 5.97 us -> 0.86 us
    pallas_call x0 -> x1, Pallas kernels: none -> 4.17 us  [load(): pl.pallas_call(load_kernel, name='load', out_shape=[pltpu.VMEM(x.shape, x...]
    ppermute x12, waiting for transfers between devices: 13.2 us -> 10.3 us  [shifted_to(): return lax.ppermute(x, ('lat', 'lon'), pairs)]
    ppermute x12, starting transfers between devices: 13.9 us -> 15.2 us  [shifted_to(): return lax.ppermute(x, ('lat', 'lon'), pairs)]
  transfers between devices with their start and end apart: 14 -> 14, of which waited for: 7 -> 6; matrix products, arithmetic and copies ran while one was open for 4% -> 2% of each run, Pallas kernels for 7% -> 11%
where the time goes in v2:
time: 52.4 us; the launch traced here: 52.3 us
  Pallas kernels  23.5 us (45%)
  starting transfers between devices  15.9 us (30%)
  waiting for transfers between devices  11.3 us (22%)
  local copies, waits for them, and re-layouts  0.86 us (2%)
  between operations  0.74 us (1%)
    pallas_call x6, Pallas kernels, call(): pl.pallas_call(kernel, name=name, out_shape=outs, in_specs=specs, out_spe...  19.3 us
    ppermute x12, starting transfers between devices, shifted_to(): return lax.ppermute(x, ('lat', 'lon'), pairs)  15.2 us
    ppermute x12, waiting for transfers between devices, shifted_to(): return lax.ppermute(x, ('lat', 'lon'), pairs)  10.3 us
    pallas_call x1, Pallas kernels, load(): pl.pallas_call(load_kernel, name='load', out_shape=[pltpu.VMEM(x.shape, x...  4.17 us
  transfers between devices with their start and end apart: 14, of which 6 were waited for; matrix products, arithmetic and copies ran while one was open for 2% of the time, Pallas kernels for 11%

profile of v2, /device:TPU:1, one launch (start us, length us, event | category | flops | bytes accessed | tf_op | source)
XLA Modules:
  0.0 52.3 jit_solution(18260158869248306207)
XLA Ops:
  0.6 1.5 %bias.1 = (bf16[112,512]{1,0:T(8,128)(2,1)S(1)}, bf16[112,512]{1,0:T(8,128)(2,1)S(1)}, bf16[40,512]{1,0:T(8,128)(2,1)S(1)}, bf16[40,512]{1,0:T(8,128)(2,1)S(1)}) custom-call(bf16[2,6,24,512]{3,2,1,0:T(8,128)(2,1)} %tokens.1, s32[6,24]{1,0:T(8,128)} %land_sea.1, f32[1,512]{1,0:T(1,128)} %bitcast.7, bf16[304,288]{1,0:T(8,128)(2,1)} %constant.20.clone.pack), custom_call_target="tpu_custom_call" | custom-call | tf_op jit(solution)/shard_map/bias/pallas_call | solution.py:416
  2.1 2.6 %collective-permute-start = (bf16[112,512]{1,0:T(8,128)(2,1)S(1)}, bf16[112,512]{1,0:T(8,128)(2,1)S(1)}, u32[]{:S(2)}, u32[]{:S(2)}) collective-permute-start(bf16[112,512]{1,0:T(8,128)(2,1)S(1)} %get-tuple-element.35), channel_id=1, source_target_pairs={{0,4},{1,5},{2,6},{3,7},{4,8},{5,9},{6,10},{7,11},{8,12},{9,13},{1... | collective-permute-start | bytes 344072 | tf_op jit(solution)/shard_map/ppermute | solution.py:30
  4.8 1.3 %collective-permute-start.1 = (bf16[40,512]{1,0:T(8,128)(2,1)S(1)}, bf16[40,512]{1,0:T(8,128)(2,1)S(1)}, u32[]{:S(2)}, u32[]{:S(2)}) collective-permute-start(bf16[40,512]{1,0:T(8,128)(2,1)S(1)} %get-tuple-element.36), channel_id=1, source_target_pairs={{0,1},{1,2},{2,3},{3,0},{4,5},{5,6},{6,7},{7,4},{8,9},{9,10},{10,1... | collective-permute-start | bytes 122888 | tf_op jit(solution)/shard_map/ppermute | solution.py:30
  6.1 1.4 %collective-permute-start.2 = (bf16[40,512]{1,0:T(8,128)(2,1)S(1)}, bf16[40,512]{1,0:T(8,128)(2,1)S(1)}, u32[]{:S(2)}, u32[]{:S(2)}) collective-permute-start(bf16[40,512]{1,0:T(8,128)(2,1)S(1)} %get-tuple-element.37), channel_id=1, source_target_pairs={{0,5},{1,6},{2,7},{3,4},{4,9},{5,10},{6,11},{7,8},{8,13},{9,14},{1... | collective-permute-start | bytes 122888 | tf_op jit(solution)/shard_map/ppermute | solution.py:30
  7.4 4.2 %load.1 = (bf16[512,768]{1,0:T(8,128)(2,1)S(1)}, bf16[256,512]{1,0:T(8,128)(2,1)S(1)}, bf16[2048,1024]{1,0:T(8,128)(2,1)S(1)}, bf16[1024,1536]{1,0:T(8,128)(2,1)...) custom-call(bf16[112,512]{1,0:T(8,128)(2,1)S(1)} %get-tuple-element., ...), custom_call_target="tpu_custom_call" | custom-call | tf_op jit(solution)/shard_map/load/pallas_call | solution.py:440
  11.6 0.0 copy-start.1
  11.6 0.0 collective-permute-done.2.d
  11.6 0.0 collective-permute-done.b
  11.7 2.7 %fine.1 = (bf16[112,512]{1,0:T(8,128)(2,1)S(1)}, bf16[112,512]{1,0:T(8,128)(2,1)S(1)}, bf16[40,512]{1,0:T(8,128)(2,1)S(1)}, bf16[40,512]{1,0:T(8,128)(2,1)S(1)}) custom-call(s32[1]{0:T(128)} %bitcast.band, f32[4]{0:T(128)S(1)} %copy-done, bf16[112,512]{1,0:T(8,128)(2,1)S(1)} %get-tuple-element.34.after.a, bf16[112,512]{1,0:T(8,128)(2,1)S(1)} %collective-permute-done.b, ...), custom_call_target="tpu_custom_call" | custom-call | tf_op jit(solution)/shard_map/fine/pallas_call | solution.py:416
  14.4 0.7 %collective-permute-start.3 = (bf16[112,512]{1,0:T(8,128)(2,1)S(1)}, bf16[112,512]{1,0:T(8,128)(2,1)S(1)}, u32[]{:S(2)}, u32[]{:S(2)}) collective-permute-start(bf16[112,512]{1,0:T(8,128)(2,1)S(1)} %get-tuple-element.44), channel_id=1, source_target_pairs={{0,28},{1,29},{2,30},{3,31},{4,0},{5,1},{6,2},{7,3},{8,4},{9,5},{1... | collective-permute-start | bytes 344072 | tf_op jit(solution)/shard_map/ppermute | solution.py:30
  15.1 1.6 %collective-permute-start.4 = (bf16[40,512]{1,0:T(8,128)(2,1)S(1)}, bf16[40,512]{1,0:T(8,128)(2,1)S(1)}, u32[]{:S(2)}, u32[]{:S(2)}) collective-permute-start(bf16[40,512]{1,0:T(8,128)(2,1)S(1)} %get-tuple-element.45), channel_id=1, source_target_pairs={{0,3},{1,0},{2,1},{3,2},{4,7},{5,4},{6,5},{7,6},{8,11},{9,8},{10,9... | collective-permute-start | bytes 122888 | tf_op jit(solution)/shard_map/ppermute | solution.py:30
  16.7 1.6 %collective-permute-start.5 = (bf16[40,512]{1,0:T(8,128)(2,1)S(1)}, bf16[40,512]{1,0:T(8,128)(2,1)S(1)}, u32[]{:S(2)}, u32[]{:S(2)}) collective-permute-start(bf16[40,512]{1,0:T(8,128)(2,1)S(1)} %get-tuple-element.46), channel_id=1, source_target_pairs={{0,31},{1,28},{2,29},{3,30},{4,3},{5,0},{6,1},{7,2},{8,7},{9,4},{1... | collective-permute-start | bytes 122888 | tf_op jit(solution)/shard_map/ppermute | solution.py:30
  18.3 0.1 collective-permute-start.7
  18.4 3.0 %collective-permute-done.5.d = bf16[40,512]{1,0:T(8,128)(2,1)S(1)} collective-permute-done((bf16[40,512]{1,0:T(8,128)(2,1)S(1)}, bf16[40,512]{1,0:T(8,128)(2,1)S(1)}, u32[]{:S(2)}, u32[]{:S(2)}) %collective-permute-start.5) | collective-permute-done | bytes 40992 | tf_op jit(solution)/shard_map/ppermute | solution.py:30
  21.4 0.0 collective-permute-done.3.b
  21.4 1.3 %merge.1 = (bf16[72,1024]{1,0:T(8,128)(2,1)S(1)}, bf16[72,2048]{1,0:T(8,128)(2,1)S(1)}) custom-call(bf16[112,512]{1,0:T(8,128)(2,1)S(1)} %get-tuple-element.43.a, bf16[112,512]{1,0:T(8,128)(2,1)S(1)} %collective-permute-done.3.b, bf16[40,512]{1,0:T(8,128)(2,1)S(1)} %collective-permute-done.4.c, bf16[40,512]{1,0:T(8,128)(2,1)S(1)} %collective-permute-done.5.d, ...), custom_call_target="tpu_custom_call" | custom-call | tf_op jit(solution)/shard_map/merge/pallas_call | solution.py:416
  22.8 0.7 %collective-permute-start.6 = (bf16[72,1024]{1,0:T(8,128)(2,1)S(1)}, bf16[72,1024]{1,0:T(8,128)(2,1)S(1)}, u32[]{:S(2)}, u32[]{:S(2)}) collective-permute-start(bf16[72,1024]{1,0:T(8,128)(2,1)S(1)} %get-tuple-element.50.own), channel_id=1, source_target_pairs={{0,4},{4,0},{8,12},{12,8},{16,20},{20,16},{24,28},{28,24},{1,5},{5... | collective-permute-start | bytes 442376 | tf_op jit(solution)/shard_map/ppermute | solution.py:34
  23.5 1.0 %collective-permute-done.6.partner = bf16[72,1024]{1,0:T(8,128)(2,1)S(1)} collective-permute-done((bf16[72,1024]{1,0:T(8,128)(2,1)S(1)}, bf16[72,1024]{1,0:T(8,128)(2,1)S(1)}, u32[]{:S(2)}, u32[]{:S(2)}) %collective-permute-start.6) | collective-permute-done | bytes 147488 | tf_op jit(solution)/shard_map/ppermute | solution.py:34
  24.5 7.3 %coarse.1 = (bf16[2,3,12,1024]{3,2,1,0:T(8,128)(2,1)S(1)}, bf16[112,512]{1,0:T(8,128)(2,1)S(1)}, bf16[112,512]{1,0:T(8,128)(2,1)S(1)}, bf16[40,512]{1,0:T(8,128)(2,1)S(1)}, bf16[40,512]{1,0:T(8,128)(2,1)S(1)}) custom-call(f32[8]{0:T(128)S(1)} %copy-done.1, bf16[72,1024]{1,0:T(8,128)(2,1)S(1)} %get-tuple-element.50.own, ...), custom_call_target="tpu_custom_call" | custom-call | tf_op jit(solution)/shard_map/coarse/pallas_call | solution.py:416
  31.8 1.9 %collective-permute-start.8 = (bf16[112,512]{1,0:T(8,128)(2,1)S(1)}, bf16[112,512]{1,0:T(8,128)(2,1)S(1)}, u32[]{:S(2)}, u32[]{:S(2)}) collective-permute-start(bf16[112,512]{1,0:T(8,128)(2,1)S(1)} %get-tuple-element.58), channel_id=1, source_target_pairs={{0,4},{1,5},{2,6},{3,7},{4,8},{5,9},{6,10},{7,11},{8,12},{9,13},{1... | collective-permute-start | bytes 344072 | tf_op jit(solution)/shard_map/ppermute | solution.py:30
  33.7 0.0 collective-permute-start.9
  33.7 1.1 %collective-permute-start.10 = (bf16[40,512]{1,0:T(8,128)(2,1)S(1)}, bf16[40,512]{1,0:T(8,128)(2,1)S(1)}, u32[]{:S(2)}, u32[]{:S(2)}) collective-permute-start(bf16[40,512]{1,0:T(8,128)(2,1)S(1)} %get-tuple-element.60), channel_id=1, source_target_pairs={{0,5},{1,6},{2,7},{3,4},{4,9},{5,10},{6,11},{7,8},{8,13},{9,14},{1... | collective-permute-start | bytes 122888 | tf_op jit(solution)/shard_map/ppermute | solution.py:30
  34.8 3.5 %collective-permute-done.9.gc = bf16[40,512]{1,0:T(8,128)(2,1)S(1)} collective-permute-done((bf16[40,512]{1,0:T(8,128)(2,1)S(1)}, bf16[40,512]{1,0:T(8,128)(2,1)S(1)}, u32[]{:S(2)}, u32[]{:S(2)}) %collective-permute-start.9) | collective-permute-done | bytes 40992 | tf_op jit(solution)/shard_map/ppermute | solution.py:30
  38.3 1.2 %collective-permute-done.10.gd = bf16[40,512]{1,0:T(8,128)(2,1)S(1)} collective-permute-done((bf16[40,512]{1,0:T(8,128)(2,1)S(1)}, bf16[40,512]{1,0:T(8,128)(2,1)S(1)}, u32[]{:S(2)}, u32[]{:S(2)}) %collective-permute-start.10) | collective-permute-done | bytes 40992 | tf_op jit(solution)/shard_map/ppermute | solution.py:30
  39.5 5.5 %fine_back.1 = (bf16[112,512]{1,0:T(8,128)(2,1)S(1)}, bf16[112,512]{1,0:T(8,128)(2,1)S(1)}, bf16[40,512]{1,0:T(8,128)(2,1)S(1)}, bf16[40,512]{1,0:T(8,128)(2,1)S(1)}) custom-call(s32[1]{0:T(128)} %bitcast.band, f32[4]{0:T(128)S(1)} %copy-done, bf16[112,512]{1,0:T(8,128)(2,1)S(1)} %get-tuple-element.34.after.a, bf16[112,512]{1,0:T(8,128)(2,1)S(1)} %collective-permute-done.b, ...), custom_call_target="tpu_custom_call" | custom-call | tf_op jit(solution)/shard_map/fine_back/pallas_call | solution.py:416
  45.0 1.2 %collective-permute-start.11 = (bf16[112,512]{1,0:T(8,128)(2,1)S(1)}, bf16[112,512]{1,0:T(8,128)(2,1)S(1)}, u32[]{:S(2)}, u32[]{:S(2)}) collective-permute-start(bf16[112,512]{1,0:T(8,128)(2,1)S(1)} %get-tuple-element.62), channel_id=1, source_target_pairs={{0,28},{1,29},{2,30},{3,31},{4,0},{5,1},{6,2},{7,3},{8,4},{9,5},{1... | collective-permute-start | bytes 344072 | tf_op jit(solution)/shard_map/ppermute | solution.py:30
  46.2 0.5 collective-permute-start.12
  46.6 1.2 %collective-permute-start.13 = (bf16[40,512]{1,0:T(8,128)(2,1)S(1)}, bf16[40,512]{1,0:T(8,128)(2,1)S(1)}, u32[]{:S(2)}, u32[]{:S(2)}) collective-permute-start(bf16[40,512]{1,0:T(8,128)(2,1)S(1)} %get-tuple-element.64), channel_id=1, source_target_pairs={{0,31},{1,28},{2,29},{3,30},{4,3},{5,0},{6,1},{7,2},{8,7},{9,4},{1... | collective-permute-start | bytes 122888 | tf_op jit(solution)/shard_map/ppermute | solution.py:30
  47.9 0.8 %copy.24 = bf16[2,3,12,1024]{3,0,2,1:T(2,128)(2,1)} copy(bf16[2,3,12,1024]{3,2,1,0:T(8,128)(2,1)S(1)} %get-tuple-element.66) | data formatting | bytes 294912
  48.7 0.3 collective-permute-done.12.c
  49.0 2.3 %collective-permute-done.13.d = bf16[40,512]{1,0:T(8,128)(2,1)S(1)} collective-permute-done((bf16[40,512]{1,0:T(8,128)(2,1)S(1)}, bf16[40,512]{1,0:T(8,128)(2,1)S(1)}, u32[]{:S(2)}, u32[]{:S(2)}) %collective-permute-start.13) | collective-permute-done | bytes 40992 | tf_op jit(solution)/shard_map/ppermute | solution.py:30
  51.3 1.0 %unpack.1 = bf16[2,6,24,512]{3,2,1,0:T(8,128)(2,1)} custom-call(bf16[112,512]{1,0:T(8,128)(2,1)S(1)} %get-tuple-element.61.a, bf16[112,512]{1,0:T(8,128)(2,1)S(1)} %collective-permute-done.11.b, bf16[40,512]{1,0:T(8,128)(2,1)S(1)} %collective-permute-done.12.c, bf16[40,512]{1,0:T(8,128)(2,1)S(1)} %collective-permute-done.13.d, ...), custom_call_target="tpu_custom_call" | custom-call | tf_op jit(solution)/shard_map/unpack/pallas_call | solution.py:416
  (11 shorter events, 0.1 us)
Async XLA Ops:
  2.1 9.5 %collective-permute-start = (bf16[112,512]{1,0:T(8,128)(2,1)S(1)}, bf16[112,512]{1,0:T(8,128)(2,1)S(1)}, u32[]{:S(2)}, u32[]{:S(2)}) collective-permute-start(bf16[112,512]{1,0:T(8,128)(2,1)S(1)} %get-tuple-element.35), channel_id=1, source_target_pairs={{0,4},{1,5},{2,6},{3,7},{4,8},{5,9},{6,10},{7,11},{8,12},{9,13},{1... | collective-permute-start | bytes 344072 | tf_op jit(solution)/shard_map/ppermute | solution.py:30
  4.8 6.9 %collective-permute-start.1 = (bf16[40,512]{1,0:T(8,128)(2,1)S(1)}, bf16[40,512]{1,0:T(8,128)(2,1)S(1)}, u32[]{:S(2)}, u32[]{:S(2)}) collective-permute-start(bf16[40,512]{1,0:T(8,128)(2,1)S(1)} %get-tuple-element.36), channel_id=1, source_target_pairs={{0,1},{1,2},{2,3},{3,0},{4,5},{5,6},{6,7},{7,4},{8,9},{9,10},{10,1... | collective-permute-start | bytes 122888 | tf_op jit(solution)/shard_map/ppermute | solution.py:30
  6.1 5.6 %collective-permute-start.2 = (bf16[40,512]{1,0:T(8,128)(2,1)S(1)}, bf16[40,512]{1,0:T(8,128)(2,1)S(1)}, u32[]{:S(2)}, u32[]{:S(2)}) collective-permute-start(bf16[40,512]{1,0:T(8,128)(2,1)S(1)} %get-tuple-element.37), channel_id=1, source_target_pairs={{0,5},{1,6},{2,7},{3,4},{4,9},{5,10},{6,11},{7,8},{8,13},{9,14},{1... | collective-permute-start | bytes 122888 | tf_op jit(solution)/shard_map/ppermute | solution.py:30
  7.4 4.2 %copy-start = (f32[4]{0:T(128)S(1)}, f32[4]{0:T(128)}, u32[]{:S(2)}) copy-start(f32[4]{0:T(128)} %scales.5) | copy-start | bytes 52
  7.4 10.9 %copy-start.2 = (bf16[2,3,12,1024]{3,0,2,1:T(2,128)(2,1)S(1)}, bf16[2,3,12,1024]{3,0,2,1:T(2,128)(2,1)}, u32[]{:S(2)}) copy-start(bf16[2,3,12,1024]{3,0,2,1:T(2,128)(2,1)} %param.33) | copy-start | bytes 442372
  11.6 12.9 %copy-start.1 = (f32[8]{0:T(128)S(1)}, f32[8]{0:T(128)}, u32[]{:S(2)}) copy-start(f32[8]{0:T(128)} %scales.4) | copy-start | bytes 100
  14.4 7.0 %collective-permute-start.3 = (bf16[112,512]{1,0:T(8,128)(2,1)S(1)}, bf16[112,512]{1,0:T(8,128)(2,1)S(1)}, u32[]{:S(2)}, u32[]{:S(2)}) collective-permute-start(bf16[112,512]{1,0:T(8,128)(2,1)S(1)} %get-tuple-element.44), channel_id=1, source_target_pairs={{0,28},{1,29},{2,30},{3,31},{4,0},{5,1},{6,2},{7,3},{8,4},{9,5},{1... | collective-permute-start | bytes 344072 | tf_op jit(solution)/shard_map/ppermute | solution.py:30
  15.1 3.3 %collective-permute-start.4 = (bf16[40,512]{1,0:T(8,128)(2,1)S(1)}, bf16[40,512]{1,0:T(8,128)(2,1)S(1)}, u32[]{:S(2)}, u32[]{:S(2)}) collective-permute-start(bf16[40,512]{1,0:T(8,128)(2,1)S(1)} %get-tuple-element.45), channel_id=1, source_target_pairs={{0,3},{1,0},{2,1},{3,2},{4,7},{5,4},{6,5},{7,6},{8,11},{9,8},{10,9... | collective-permute-start | bytes 122888 | tf_op jit(solution)/shard_map/ppermute | solution.py:30
  16.7 4.7 %collective-permute-start.5 = (bf16[40,512]{1,0:T(8,128)(2,1)S(1)}, bf16[40,512]{1,0:T(8,128)(2,1)S(1)}, u32[]{:S(2)}, u32[]{:S(2)}) collective-permute-start(bf16[40,512]{1,0:T(8,128)(2,1)S(1)} %get-tuple-element.46), channel_id=1, source_target_pairs={{0,31},{1,28},{2,29},{3,30},{4,3},{5,0},{6,1},{7,2},{8,7},{9,4},{1... | collective-permute-start | bytes 122888 | tf_op jit(solution)/shard_map/ppermute | solution.py:30
  18.3 5.1 %collective-permute-start.7 = (bf16[2,3,12,1024]{3,2,1,0:T(8,128)(2,1)S(1)}, bf16[2,3,12,1024]{3,2,1,0:T(8,128)(2,1)S(1)}, u32[]{:S(2)}, u32[]{:S(2)}) collective-permute-start(bf16[2,3,12,1024]{3,2,1,0:T(8,128)(2,1)S(1)} %copy.23.own_cot), channel_id=1, source_target_pairs={{0,4},{4,0},{8,12},{12,8},{16,20},{20,16},{24,28},{28,24},{1,5},{5... | collective-permute-start | bytes 442376 | tf_op jit(solution)/shard_map/ppermute | solution.py:34
  22.8 1.7 %collective-permute-start.6 = (bf16[72,1024]{1,0:T(8,128)(2,1)S(1)}, bf16[72,1024]{1,0:T(8,128)(2,1)S(1)}, u32[]{:S(2)}, u32[]{:S(2)}) collective-permute-start(bf16[72,1024]{1,0:T(8,128)(2,1)S(1)} %get-tuple-element.50.own), channel_id=1, source_target_pairs={{0,4},{4,0},{8,12},{12,8},{16,20},{20,16},{24,28},{28,24},{1,5},{5... | collective-permute-start | bytes 442376 | tf_op jit(solution)/shard_map/ppermute | solution.py:34
  31.8 7.8 %collective-permute-start.8 = (bf16[112,512]{1,0:T(8,128)(2,1)S(1)}, bf16[112,512]{1,0:T(8,128)(2,1)S(1)}, u32[]{:S(2)}, u32[]{:S(2)}) collective-permute-start(bf16[112,512]{1,0:T(8,128)(2,1)S(1)} %get-tuple-element.58), channel_id=1, source_target_pairs={{0,4},{1,5},{2,6},{3,7},{4,8},{5,9},{6,10},{7,11},{8,12},{9,13},{1... | collective-permute-start | bytes 344072 | tf_op jit(solution)/shard_map/ppermute | solution.py:30
  33.7 4.7 %collective-permute-start.9 = (bf16[40,512]{1,0:T(8,128)(2,1)S(1)}, bf16[40,512]{1,0:T(8,128)(2,1)S(1)}, u32[]{:S(2)}, u32[]{:S(2)}) collective-permute-start(bf16[40,512]{1,0:T(8,128)(2,1)S(1)} %get-tuple-element.59), channel_id=1, source_target_pairs={{0,1},{1,2},{2,3},{3,0},{4,5},{5,6},{6,7},{7,4},{8,9},{9,10},{10,1... | collective-permute-start | bytes 122888 | tf_op jit(solution)/shard_map/ppermute | solution.py:30
  33.7 5.8 %collective-permute-start.10 = (bf16[40,512]{1,0:T(8,128)(2,1)S(1)}, bf16[40,512]{1,0:T(8,128)(2,1)S(1)}, u32[]{:S(2)}, u32[]{:S(2)}) collective-permute-start(bf16[40,512]{1,0:T(8,128)(2,1)S(1)} %get-tuple-element.60), channel_id=1, source_target_pairs={{0,5},{1,6},{2,7},{3,4},{4,9},{5,10},{6,11},{7,8},{8,13},{9,14},{1... | collective-permute-start | bytes 122888 | tf_op jit(solution)/shard_map/ppermute | solution.py:30
  45.0 6.3 %collective-permute-start.11 = (bf16[112,512]{1,0:T(8,128)(2,1)S(1)}, bf16[112,512]{1,0:T(8,128)(2,1)S(1)}, u32[]{:S(2)}, u32[]{:S(2)}) collective-permute-start(bf16[112,512]{1,0:T(8,128)(2,1)S(1)} %get-tuple-element.62), channel_id=1, source_target_pairs={{0,28},{1,29},{2,30},{3,31},{4,0},{5,1},{6,2},{7,3},{8,4},{9,5},{1... | collective-permute-start | bytes 344072 | tf_op jit(solution)/shard_map/ppermute | solution.py:30
  46.2 2.9 %collective-permute-start.12 = (bf16[40,512]{1,0:T(8,128)(2,1)S(1)}, bf16[40,512]{1,0:T(8,128)(2,1)S(1)}, u32[]{:S(2)}, u32[]{:S(2)}) collective-permute-start(bf16[40,512]{1,0:T(8,128)(2,1)S(1)} %get-tuple-element.63), channel_id=1, source_target_pairs={{0,3},{1,0},{2,1},{3,2},{4,7},{5,4},{6,5},{7,6},{8,11},{9,8},{10,9... | collective-permute-start | bytes 122888 | tf_op jit(solution)/shard_map/ppermute | solution.py:30
  46.6 4.6 %collective-permute-start.13 = (bf16[40,512]{1,0:T(8,128)(2,1)S(1)}, bf16[40,512]{1,0:T(8,128)(2,1)S(1)}, u32[]{:S(2)}, u32[]{:S(2)}) collective-permute-start(bf16[40,512]{1,0:T(8,128)(2,1)S(1)} %get-tuple-element.64), channel_id=1, source_target_pairs={{0,31},{1,28},{2,29},{3,30},{4,3},{5,0},{6,1},{7,2},{8,7},{9,4},{1... | collective-permute-start | bytes 122888 | tf_op jit(solution)/shard_map/ppermute | solution.py:30

commit v3 on v2

--- a/solution.py
+++ b/solution.py
@@ -95,25 +95,32 @@
             whole = (flat[:, None] == flat[None, :]).astype(np.float32)
             self.masks.append(np.stack([apart, whole]))
 
-    def into_windows(self, a, b, c, d):
-        result = []
-        for w, (start, size, _) in enumerate(self.a_spans):
-            parts = [a[start : start + size], b[start : start + size]]
-            if w == 0:
-                parts += [c, d]
-            result.append(jnp.concatenate(parts, axis=0))
-        return result
-
-    def from_windows(self, windows):
+    def window_rows(self, w, a, b, c=None, d=None):
+        start, size, _ = self.a_spans[w]
+        parts = [x[...].astype(F32)[start : start + size] for x in (a, b)]
+        if w == 0:
+            parts += [x[...].astype(F32) for x in (c, d)]
+        return jnp.concatenate(parts, axis=0)
+
+    def length(self, w):
+        return self.masks[w].shape[-1]
+
+    def put_pieces(self, outs, first, others):
         a, b = [], []
         for w, (_, size, _) in enumerate(self.a_spans):
-            a.append(windows[w][:size])
-            b.append(windows[w][size : 2 * size])
+            rows = first if w == 0 else others[w - 1][...].astype(F32)
+            a.append(rows[:size])
+            b.append(rows[size : 2 * size])
         base = 2 * self.a_spans[0][1]
         edge = self.c_spans[0][1]
-        c = windows[0][base : base + edge]
-        d = windows[0][base + edge :]
-        return jnp.concatenate(a, axis=0), jnp.concatenate(b, axis=0), c, d
+        values = (
+            jnp.concatenate(a, axis=0),
+            jnp.concatenate(b, axis=0),
+            first[base : base + edge],
+            first[base + edge :],
+        )
+        for out, value in zip(outs, values):
+            out[...] = value.astype(BF16)
 
 
 def mm(a, b):
@@ -192,11 +199,13 @@
 def attend_back(probs, query_stack, key_unit, values, mixture_grad, masks):
     grad_stack = spread_heads(mixture_grad, masks)
     probs_grad = mm_t(grad_stack, values)
+    low = probs.astype(BF16)
+    probs = probs.astype(F32)
     delta = jnp.sum(probs * probs_grad, axis=-1, keepdims=True)
     logits_grad = (probs * (probs_grad - delta)).astype(BF16)
     query_grad = join_heads(mm(logits_grad, key_unit), masks)
     key_grad = t_mm(logits_grad, query_stack)
-    value_grad = t_mm(probs.astype(BF16), grad_stack)
+    value_grad = t_mm(low, grad_stack)
     return query_grad, key_grad, value_grad
 
 
@@ -252,47 +261,63 @@
     return masks, scale_lanes_of(scales, masks, head_size), head_mean_matrix(inner, head_size)
 
 
-def fine_kernel(plan, band, scales, a, b, c, d, inward, outward, gain, *rest):
-    mask_refs, outs = rest[: len(plan.masks)], rest[len(plan.masks) :]
+def saved_shapes(n, inner, width):
+    return [
+        jax.ShapeDtypeStruct((n, inner), F32),
+        jax.ShapeDtypeStruct((n, inner), F32),
+        jax.ShapeDtypeStruct((n, inner), F32),
+        jax.ShapeDtypeStruct((n, inner), F32),
+        jax.ShapeDtypeStruct((n, inner), BF16),
+        jax.ShapeDtypeStruct((HEADS * n, inner), BF16),
+        jax.ShapeDtypeStruct((HEADS * n, n), BF16),
+        jax.ShapeDtypeStruct((n, width), F32),
+        jax.ShapeDtypeStruct((n, 1), F32),
+    ]
+
+
+SAVED = 9
+
+
+def fine_kernel(plan, w, band, scales, inward, outward, gain, mask, *rest):
+    pieces = rest[: 4 if w == 0 else 2]
+    rest = rest[len(pieces) :]
     masks, scale_lanes, mean_matrix = fine_setup(scales, outward.shape[0])
-    first_band = band[0] == 0
-    windows = plan.into_windows(*(x[...].astype(F32) for x in (a, b, c, d)))
-    results = []
-    for rows, mask in zip(windows, mask_refs):
-        allowed = allowed_of(mask, first_band)
-        unit = fine_window(
-            rows, allowed, inward[...], outward[...], scale_lanes, masks, mean_matrix
-        )[-2]
-        results.append(rows + unit * gain[...])
-    for out, value in zip(outs, plan.from_windows(results)):
-        out[...] = value.astype(BF16)
-
-
-def fine_back_kernel(plan, band, scales, a, b, c, d, ga, gb, gc, gd, inward, outward, gain, *rest):
-    mask_refs, outs = rest[: len(plan.masks)], rest[len(plan.masks) :]
+    rows = plan.window_rows(w, *pieces)
+    allowed = allowed_of(mask, band[0] == 0)
+    saved = fine_window(rows, allowed, inward[...], outward[...], scale_lanes, masks, mean_matrix)
+    result = rows + saved[-2] * gain[...]
+    finish(plan, w, result, rest[:-SAVED])
+    for out, value in zip(rest[-SAVED:], saved):
+        out[...] = value.astype(out.dtype)
+
+
+def finish(plan, w, result, refs):
+    if w == 0:
+        plan.put_pieces(refs[-4:], result, refs[:-4])
+    else:
+        refs[0][...] = result.astype(BF16)
+
+
+def fine_back_kernel(plan, w, scales, inward, outward, gain, *rest):
+    pieces = rest[: 4 if w == 0 else 2]
+    saved = rest[len(pieces) : len(pieces) + SAVED]
+    rest = rest[len(pieces) + SAVED :]
     masks, scale_lanes, mean_matrix = fine_setup(scales, outward.shape[0])
-    first_band = band[0] == 0
-    windows = plan.into_windows(*(x[...].astype(F32) for x in (a, b, c, d)))
-    grads = plan.into_windows(*(x[...].astype(F32) for x in (ga, gb, gc, gd)))
-    results = []
-    for rows, grad, mask in zip(windows, grads, mask_refs):
-        allowed = allowed_of(mask, first_band)
-        query_unit, query_factor, key_unit, key_factor, values, query_stack, probs, unit, factor = (
-            fine_window(rows, allowed, inward[...], outward[...], scale_lanes, masks, mean_matrix)
-        )
-        projected_grad = norm_back(unit, factor, grad * gain[...]).astype(BF16)
-        mixture_grad = mm_t(projected_grad, outward[...])
-        query_grad, key_grad, value_grad = attend_back(
-            probs, query_stack, key_unit.astype(BF16), values, mixture_grad, masks
-        )
-        query_grad = unit_back(query_unit, query_factor, query_grad * scale_lanes, mean_matrix)
-        key_grad = unit_back(key_unit, key_factor, key_grad, mean_matrix)
-        packed_grad = jnp.concatenate(
-            [query_grad.astype(BF16), key_grad.astype(BF16), value_grad.astype(BF16)], axis=1
-        )
-        results.append(grad + mm_t(packed_grad, inward[...]))
-    for out, value in zip(outs, plan.from_windows(results)):
-        out[...] = value.astype(BF16)
+    query_unit, query_factor, key_unit, key_factor, values, query_stack, probs, unit, factor = (
+        x[...] for x in saved
+    )
+    grad = plan.window_rows(w, *pieces)
+    projected_grad = norm_back(unit, factor, grad * gain[...]).astype(BF16)
+    mixture_grad = mm_t(projected_grad, outward[...])
+    query_grad, key_grad, value_grad = attend_back(
+        probs, query_stack, key_unit.astype(BF16), values, mixture_grad, masks
+    )
+    query_grad = unit_back(query_unit, query_factor, query_grad * scale_lanes, mean_matrix)
+    key_grad = unit_back(key_unit, key_factor, key_grad, mean_matrix)
+    packed_grad = jnp.concatenate(
+        [query_grad.astype(BF16), key_grad.astype(BF16), value_grad.astype(BF16)], axis=1
+    )
+    finish(plan, w, grad + mm_t(packed_grad, inward[...]), rest)
 
 
 def merge_kernel(plan, a, b, c, d, group, gain, weight, coarse, grouped_out):
@@ -406,7 +431,7 @@
 VMEM = functools.partial(pl.BlockSpec, memory_space=pltpu.VMEM)
 
 
-def call(kernel, name, outs, args, smem=0, scratch=(), keep_in=True, keep_out=True):
+def call(kernel, name, outs, args, smem=0, scratch=(), keep_in=True, keep_out=True, cost=None):
     specs = [SMEM()] * smem + [VMEM()] * (len(args) - smem)
     space = pltpu.VMEM if keep_in else pltpu.HBM
     near = tuple(pltpu.with_memory_space_constraint(x, space) for x in args[smem:])
@@ -420,6 +445,7 @@
         in_specs=specs,
         out_specs=[VMEM() for _ in outs],
         scratch_shapes=scratch,
+        cost_estimate=cost,
         compiler_params=pltpu.CompilerParams(vmem_limit_bytes=24 * 1024 * 1024),
     )(*args)
 
@@ -487,46 +513,51 @@
         keep_in=False,
     )
     region = gather(*biased)
-    (
-        fine_inward,
-        fine_outward,
-        merge_weight,
-        coarse_inward,
-        coarse_outward,
-        fine_gain,
-        merge_gain,
-        coarse_gain,
-        group,
-        ungroup,
-        unpack,
-        *masks,
-    ) = load(
+    fine_inward, fine_outward, fine_gain, group, merge_gain, *masks = load(
         biased[0],
+        (fine_inward, fine_outward, row(fine_gain), constant(plan.group), row(merge_gain), *masks),
+    )
+    fine_weights = (fine_inward, fine_outward, fine_gain)
+    cost = pl.CostEstimate(flops=2 * 10**8, transcendentals=0, bytes_accessed=10**6)
+    windows = len(plan.masks)
+    inner = fine_outward.shape[0]
+    shapes = [
+        [jax.ShapeDtypeStruct((plan.length(w), width), BF16)]
+        + saved_shapes(plan.length(w), inner, width)
+        for w in range(windows)
+    ]
+    others, saved = [], [None] * windows
+    for w in range(1, windows):
+        result, *saved[w] = call(
+            functools.partial(fine_kernel, plan, w),
+            "fine_inside",
+            shapes[w],
+            (band, fine_scale, *fine_weights, masks[w], region[0], region[1]),
+            smem=2,
+            cost=cost,
+        )
+        others.append(result)
+    outs = call(
+        functools.partial(fine_kernel, plan, 0),
+        "fine_edge",
+        pieces + shapes[0][1:],
+        (band, fine_scale, *fine_weights, masks[0], *region, *others),
+        smem=2,
+        cost=cost,
+    )
+    saved[0] = outs[4:]
+    merge_weight, coarse_inward, coarse_outward, coarse_gain, ungroup, unpack = load(
+        outs[0],
         (
-            fine_inward,
-            fine_outward,
             merge_weight,
             coarse_inward,
             coarse_outward,
-            row(fine_gain),
-            row(merge_gain),
             row(coarse_gain),
-            constant(plan.group),
             constant(plan.group.T),
             constant(plan.pack.T),
-            *masks,
         ),
     )
-    fine_weights = (fine_inward, fine_outward, fine_gain, *masks)
-    fine_result = give_back(
-        *call(
-            functools.partial(fine_kernel, plan),
-            "fine",
-            pieces,
-            (band, fine_scale, *region, *fine_weights),
-            smem=2,
-        )
-    )
+    fine_result = give_back(*outs[:4])
     partner_cot = swapped(coarse_cotangent)
     own, grouped = call(
         functools.partial(merge_kernel, plan),
@@ -563,13 +594,25 @@
         ],
     )
     grads = gather(*grads)
+    others = []
+    for w in range(1, windows):
+        (result,) = call(
+            functools.partial(fine_back_kernel, plan, w),
+            "fine_back_inside",
+            shapes[w][:1],
+            (fine_scale, *fine_weights, grads[0], grads[1], *saved[w]),
+            smem=1,
+            cost=cost,
+        )
+        others.append(result)
     token_pieces = give_back(
         *call(
-            functools.partial(fine_back_kernel, plan),
-            "fine_back",
+            functools.partial(fine_back_kernel, plan, 0),
+            "fine_back_edge",
             pieces,
-            (band, fine_scale, *region, *grads, *fine_weights),
-            smem=2,
+            (fine_scale, *fine_weights, *grads, *saved[0], *others),
+            smem=1,
+            cost=cost,
         )
     )
     (token_grad,) = call(

time: 52.4 us -> 49.1 us (0.937)
  waiting for transfers between devices: 11.3 us -> 7.72 us
  starting transfers between devices: 15.9 us -> 15 us
  local copies, waits for them, and re-layouts: 0.86 us -> 1.51 us
    ppermute x12, waiting for transfers between devices: 10.3 us -> 6.38 us  [shifted_to(): return lax.ppermute(x, ('lat', 'lon'), pairs)]
    ppermute x12, starting transfers between devices: 15.2 us -> 14.1 us  [shifted_to(): return lax.ppermute(x, ('lat', 'lon'), pairs)]
    pallas_call x1 -> x2, Pallas kernels: 4.17 us -> 5.07 us  [load(): pl.pallas_call(load_kernel, name='load', out_shape=[pltpu.VMEM(x.shape, x...]
    pallas_call x6 -> x8, Pallas kernels: 19.3 us -> 18.6 us  [call(): pl.pallas_call(kernel, name=name, out_shape=outs, in_specs=specs, out_spe...]
    unnamed x8 -> x10, local copies, waits for them, and re-layouts: 0.86 us -> 1.51 us
  transfers between devices with their start and end apart: 14 -> 14, of which waited for: 6 -> 7; matrix products, arithmetic and copies ran while one was open for 2% -> 2% of each run, Pallas kernels for 11% -> 21%
where the time goes in v3:
time: 49.1 us; the launch traced here: 48.7 us
  Pallas kernels  23.7 us (48%)
  starting transfers between devices  15 us (31%)
  waiting for transfers between devices  7.72 us (16%)
  local copies, waits for them, and re-layouts  1.51 us (3%)
  between operations  0.77 us (2%)
    pallas_call x8, Pallas kernels, call(): pl.pallas_call(kernel, name=name, out_shape=outs, in_specs=specs, out_spe...  18.6 us
    ppermute x12, starting transfers between devices, shifted_to(): return lax.ppermute(x, ('lat', 'lon'), pairs)  14.1 us
    ppermute x12, waiting for transfers between devices, shifted_to(): return lax.ppermute(x, ('lat', 'lon'), pairs)  6.38 us
    pallas_call x2, Pallas kernels, load(): pl.pallas_call(load_kernel, name='load', out_shape=[pltpu.VMEM(x.shape, x...  5.07 us
    unnamed x10, local copies, waits for them, and re-layouts  1.51 us
    ppermute x2, waiting for transfers between devices, swapped(): lax.ppermute(x, 'lat', [(i, i ^ 1) for i in range(lax.axis_size('lat'))])  1.34 us
  transfers between devices with their start and end apart: 14, of which 7 were waited for; matrix products, arithmetic and copies ran while one was open for 2% of the time, Pallas kernels for 21%

profile of v3, /device:TPU:1, one launch (start us, length us, event | category | flops | bytes accessed | tf_op | source)
XLA Modules:
  0.0 48.7 jit_solution(2819531936941085745)
XLA Ops:
  0.6 1.5 %bias.1 = (bf16[112,512]{1,0:T(8,128)(2,1)S(1)}, bf16[112,512]{1,0:T(8,128)(2,1)S(1)}, bf16[40,512]{1,0:T(8,128)(2,1)S(1)}, bf16[40,512]{1,0:T(8,128)(2,1)S(1)}) custom-call(bf16[2,6,24,512]{3,2,1,0:T(8,128)(2,1)} %tokens.1, s32[6,24]{1,0:T(8,128)} %land_sea.1, f32[1,512]{1,0:T(1,128)} %bitcast.7, bf16[304,288]{1,0:T(8,128)(2,1)} %constant.20.clone.pack), custom_call_target="tpu_custom_call" | custom-call | tf_op jit(solution)/shard_map/bias/pallas_call | solution.py:441
  2.2 2.6 %collective-permute-start = (bf16[112,512]{1,0:T(8,128)(2,1)S(1)}, bf16[112,512]{1,0:T(8,128)(2,1)S(1)}, u32[]{:S(2)}, u32[]{:S(2)}) collective-permute-start(bf16[112,512]{1,0:T(8,128)(2,1)S(1)} %get-tuple-element.58), channel_id=1, source_target_pairs={{0,4},{1,5},{2,6},{3,7},{4,8},{5,9},{6,10},{7,11},{8,12},{9,13},{1... | collective-permute-start | bytes 344072 | tf_op jit(solution)/shard_map/ppermute | solution.py:30
  4.8 1.3 %collective-permute-start.1 = (bf16[40,512]{1,0:T(8,128)(2,1)S(1)}, bf16[40,512]{1,0:T(8,128)(2,1)S(1)}, u32[]{:S(2)}, u32[]{:S(2)}) collective-permute-start(bf16[40,512]{1,0:T(8,128)(2,1)S(1)} %get-tuple-element.59), channel_id=1, source_target_pairs={{0,1},{1,2},{2,3},{3,0},{4,5},{5,6},{6,7},{7,4},{8,9},{9,10},{10,1... | collective-permute-start | bytes 122888 | tf_op jit(solution)/shard_map/ppermute | solution.py:30
  6.1 1.4 %collective-permute-start.2 = (bf16[40,512]{1,0:T(8,128)(2,1)S(1)}, bf16[40,512]{1,0:T(8,128)(2,1)S(1)}, u32[]{:S(2)}, u32[]{:S(2)}) collective-permute-start(bf16[40,512]{1,0:T(8,128)(2,1)S(1)} %get-tuple-element.60), channel_id=1, source_target_pairs={{0,5},{1,6},{2,7},{3,4},{4,9},{5,10},{6,11},{7,8},{8,13},{9,14},{1... | collective-permute-start | bytes 122888 | tf_op jit(solution)/shard_map/ppermute | solution.py:30
  7.5 1.5 %load.2 = (bf16[512,768]{1,0:T(8,128)(2,1)S(1)}, bf16[256,512]{1,0:T(8,128)(2,1)S(1)}, f32[1,512]{1,0:T(1,128)S(1)}, bf16[288,304]{1,0:T(8,128)(2,1)S(1)}, f32[1...) custom-call(bf16[112,512]{1,0:T(8,128)(2,1)S(1)} %get-tuple-element.53.after.rest_0_, ...), custom_call_target="tpu_custom_call" | custom-call | tf_op jit(solution)/shard_map/load/pallas_call | solution.py:466
  9.0 0.6 %copy-done = f32[4]{0:T(128)S(1)} copy-done((f32[4]{0:T(128)S(1)}, f32[4]{0:T(128)}, u32[]{:S(2)}) %copy-start) | copy-done | bytes 40
  9.7 1.8 %fine_inside.1 = (bf16[144,512]{1,0:T(8,128)(2,1)S(1)}, f32[144,256]{1,0:T(8,128)S(1)}, f32[144,256]{1,0:T(8,128)S(1)}, f32[144,256]{1,0:T(8,128)S(1)}, f32[144,...) custom-call(s32[1]{0:T(128)} %bitcast.band, ...), custom_call_target="tpu_custom_call" | custom-call | flops 200000000 | bytes 1000000 | tf_op jit(solution)/shard_map/fine_inside/pallas_call | solution.py:441
  11.5 0.2 collective-permute-done.2.rest_3_
  11.6 1.8 %fine_edge.1 = (bf16[112,512]{1,0:T(8,128)(2,1)S(1)}, bf16[112,512]{1,0:T(8,128)(2,1)S(1)}, bf16[40,512]{1,0:T(8,128)(2,1)S(1)}, bf16[40,512]{1,0:T(8,128)(2,1)S...) custom-call(s32[1]{0:T(128)} %bitcast.band, ...), custom_call_target="tpu_custom_call" | custom-call | flops 200000000 | bytes 1000000 | tf_op jit(solution)/shard_map/fine_edge/pallas_call | solution.py:441
  13.4 0.8 %collective-permute-start.3 = (bf16[112,512]{1,0:T(8,128)(2,1)S(1)}, bf16[112,512]{1,0:T(8,128)(2,1)S(1)}, u32[]{:S(2)}, u32[]{:S(2)}) collective-permute-start(bf16[112,512]{1,0:T(8,128)(2,1)S(1)} %get-tuple-element.64), channel_id=1, source_target_pairs={{0,28},{1,29},{2,30},{3,31},{4,0},{5,1},{6,2},{7,3},{8,4},{9,5},{1... | collective-permute-start | bytes 344072 | tf_op jit(solution)/shard_map/ppermute | solution.py:30
  14.2 2.2 %collective-permute-start.4 = (bf16[40,512]{1,0:T(8,128)(2,1)S(1)}, bf16[40,512]{1,0:T(8,128)(2,1)S(1)}, u32[]{:S(2)}, u32[]{:S(2)}) collective-permute-start(bf16[40,512]{1,0:T(8,128)(2,1)S(1)} %get-tuple-element.65), channel_id=1, source_target_pairs={{0,3},{1,0},{2,1},{3,2},{4,7},{5,4},{6,5},{7,6},{8,11},{9,8},{10,9... | collective-permute-start | bytes 122888 | tf_op jit(solution)/shard_map/ppermute | solution.py:30
  16.5 0.7 %collective-permute-start.5 = (bf16[40,512]{1,0:T(8,128)(2,1)S(1)}, bf16[40,512]{1,0:T(8,128)(2,1)S(1)}, u32[]{:S(2)}, u32[]{:S(2)}) collective-permute-start(bf16[40,512]{1,0:T(8,128)(2,1)S(1)} %get-tuple-element.66), channel_id=1, source_target_pairs={{0,31},{1,28},{2,29},{3,30},{4,3},{5,0},{6,1},{7,2},{8,7},{9,4},{1... | collective-permute-start | bytes 122888 | tf_op jit(solution)/shard_map/ppermute | solution.py:30
  17.2 0.9 %collective-permute-start.7 = (bf16[2,3,12,1024]{3,2,1,0:T(8,128)(2,1)S(1)}, bf16[2,3,12,1024]{3,2,1,0:T(8,128)(2,1)S(1)}, u32[]{:S(2)}, u32[]{:S(2)}) collective-permute-start(bf16[2,3,12,1024]{3,2,1,0:T(8,128)(2,1)S(1)} %copy.23.own_cot), channel_id=1, source_target_pairs={{0,4},{4,0},{8,12},{12,8},{16,20},{20,16},{24,28},{28,24},{1,5},{5... | collective-permute-start | bytes 442376 | tf_op jit(solution)/shard_map/ppermute | solution.py:34
  18.1 3.5 %load.3 = (bf16[2048,1024]{1,0:T(8,128)(2,1)S(1)}, bf16[1024,1536]{1,0:T(8,128)(2,1)S(1)}, bf16[512,1024]{1,0:T(8,128)(2,1)S(1)}, f32[1,1024]{1,0:T(1,128)S(1)},...) custom-call(bf16[112,512]{1,0:T(8,128)(2,1)S(1)} %get-tuple-element.63.after.a, bf16[2048,1024]{1,0:T(8,128)(2,1)} %refs_0_.3, ...), custom_call_target="tpu_custom_call" | custom-call | tf_op jit(solution)/shard_map/load/pallas_call | solution.py:466
  21.7 1.3 %merge.1 = (bf16[72,1024]{1,0:T(8,128)(2,1)S(1)}, bf16[72,2048]{1,0:T(8,128)(2,1)S(1)}) custom-call(bf16[112,512]{1,0:T(8,128)(2,1)S(1)} %get-tuple-element.63.after.a, bf16[112,512]{1,0:T(8,128)(2,1)S(1)} %collective-permute-done.3.b, bf16[40,512]{1,0:T(8,128)(2,1)S(1)} %collective-permute-done.4.c, bf16[40,512]{1,0:T(8,128)(2,1)S(1)} %collective-permute-done.5.d, ...), custom_call_target="tpu_custom_call" | custom-call | tf_op jit(solution)/shard_map/merge/pallas_call | solution.py:441
  23.2 1.3 %collective-permute-done.6.partner = bf16[72,1024]{1,0:T(8,128)(2,1)S(1)} collective-permute-done((bf16[72,1024]{1,0:T(8,128)(2,1)S(1)}, bf16[72,1024]{1,0:T(8,128)(2,1)S(1)}, u32[]{:S(2)}, u32[]{:S(2)}) %collective-permute-start.6) | collective-permute-done | bytes 147488 | tf_op jit(solution)/shard_map/ppermute | solution.py:34
  24.5 7.3 %coarse.1 = (bf16[2,3,12,1024]{3,2,1,0:T(8,128)(2,1)S(1)}, bf16[112,512]{1,0:T(8,128)(2,1)S(1)}, bf16[112,512]{1,0:T(8,128)(2,1)S(1)}, bf16[40,512]{1,0:T(8,128)(2,1)S(1)}, bf16[40,512]{1,0:T(8,128)(2,1)S(1)}) custom-call(f32[8]{0:T(128)S(1)} %copy-done.2, bf16[72,1024]{1,0:T(8,128)(2,1)S(1)} %get-tuple-element.70.own, ...), custom_call_target="tpu_custom_call" | custom-call | tf_op jit(solution)/shard_map/coarse/pallas_call | solution.py:441
  31.8 0.8 %collective-permute-start.8 = (bf16[112,512]{1,0:T(8,128)(2,1)S(1)}, bf16[112,512]{1,0:T(8,128)(2,1)S(1)}, u32[]{:S(2)}, u32[]{:S(2)}) collective-permute-start(bf16[112,512]{1,0:T(8,128)(2,1)S(1)} %get-tuple-element.78), channel_id=1, source_target_pairs={{0,4},{1,5},{2,6},{3,7},{4,8},{5,9},{6,10},{7,11},{8,12},{9,13},{1... | collective-permute-start | bytes 344072 | tf_op jit(solution)/shard_map/ppermute | solution.py:30
  32.6 0.8 %collective-permute-start.9 = (bf16[40,512]{1,0:T(8,128)(2,1)S(1)}, bf16[40,512]{1,0:T(8,128)(2,1)S(1)}, u32[]{:S(2)}, u32[]{:S(2)}) collective-permute-start(bf16[40,512]{1,0:T(8,128)(2,1)S(1)} %get-tuple-element.79), channel_id=1, source_target_pairs={{0,1},{1,2},{2,3},{3,0},{4,5},{5,6},{6,7},{7,4},{8,9},{9,10},{10,1... | collective-permute-start | bytes 122888 | tf_op jit(solution)/shard_map/ppermute | solution.py:30
  33.4 0.4 collective-permute-start.10
  33.8 0.6 %collective-permute-done.8.rest_1_ = bf16[112,512]{1,0:T(8,128)(2,1)S(1)} collective-permute-done((bf16[112,512]{1,0:T(8,128)(2,1)S(1)}, bf16[112,512]{1,0:T(8,128)(2,1)S(1)}, u32[]{:S(2)}, u32[]{:S(2)}) %collective-permute-start.8) | collective-permute-done | bytes 114720 | tf_op jit(solution)/shard_map/ppermute | solution.py:30
  34.4 1.9 %fine_back_inside.1.rest_13_ = bf16[144,512]{1,0:T(8,128)(2,1)S(1)} custom-call(f32[4]{0:T(128)S(1)} %copy-done.1, bf16[512,768]{1,0:T(8,128)(2,1)S(1)} %get-tuple-element.54.inward, bf16[256,512]{1,0:T(8,128)(2,1)S(1)} %get-tuple-element.55.outward, f32[1,512]{1,0:T(1,128)S(1)} %get-tuple-element.56.gain, bf16[112,512]{1,0:T(8,128)(2,1)S(1)} %get-tuple-element.77.rest_0_, ...), custom_call_target="tpu_custom_call" | custom-call | flops 200000000 | bytes 1000000 | tf_op jit(solution)/shard_map/fine_back_inside/pallas_call | solution.py:441
  36.3 1.5 %collective-permute-done.9.rest_2_ = bf16[40,512]{1,0:T(8,128)(2,1)S(1)} collective-permute-done((bf16[40,512]{1,0:T(8,128)(2,1)S(1)}, bf16[40,512]{1,0:T(8,128)(2,1)S(1)}, u32[]{:S(2)}, u32[]{:S(2)}) %collective-permute-start.9) | collective-permute-done | bytes 40992 | tf_op jit(solution)/shard_map/ppermute | solution.py:30
  37.8 1.0 %collective-permute-done.10.rest_3_ = bf16[40,512]{1,0:T(8,128)(2,1)S(1)} collective-permute-done((bf16[40,512]{1,0:T(8,128)(2,1)S(1)}, bf16[40,512]{1,0:T(8,128)(2,1)S(1)}, u32[]{:S(2)}, u32[]{:S(2)}) %collective-permute-start.10) | collective-permute-done | bytes 40992 | tf_op jit(solution)/shard_map/ppermute | solution.py:30
  38.8 2.0 %fine_back_edge.1 = (bf16[112,512]{1,0:T(8,128)(2,1)S(1)}, bf16[112,512]{1,0:T(8,128)(2,1)S(1)}, bf16[40,512]{1,0:T(8,128)(2,1)S(1)}, bf16[40,512]{1,0:T(8,128)(2,1)S(1)}) custom-call(f32[4]{0:T(128)S(1)} %copy-done.1, bf16[512,768]{1,0:T(8,128)(2,1)S(1)} %get-tuple-element.54.inward, bf16[256,512]{1,0:T(8,128)(2,1)S(1)} %get-tuple-element.55.outward, ...), custom_call_target="tpu_custom_call" | custom-call | flops 200000000 | bytes 1000000 | tf_op jit(solution)/shard_map/fine_back_edge/pallas_call | solution.py:441
  40.8 2.4 %collective-permute-start.11 = (bf16[112,512]{1,0:T(8,128)(2,1)S(1)}, bf16[112,512]{1,0:T(8,128)(2,1)S(1)}, u32[]{:S(2)}, u32[]{:S(2)}) collective-permute-start(bf16[112,512]{1,0:T(8,128)(2,1)S(1)} %get-tuple-element.100), channel_id=1, source_target_pairs={{0,28},{1,29},{2,30},{3,31},{4,0},{5,1},{6,2},{7,3},{8,4},{9,5},{1... | collective-permute-start | bytes 344072 | tf_op jit(solution)/shard_map/ppermute | solution.py:30
  43.2 0.2 collective-permute-start.12
  43.4 0.5 collective-permute-start.13
  43.8 0.8 %copy.24 = bf16[2,3,12,1024]{3,0,2,1:T(2,128)(2,1)} copy(bf16[2,3,12,1024]{3,2,1,0:T(8,128)(2,1)S(1)} %get-tuple-element.104) | data formatting | bytes 294912
  44.7 1.4 %collective-permute-done.12.c = bf16[40,512]{1,0:T(8,128)(2,1)S(1)} collective-permute-done((bf16[40,512]{1,0:T(8,128)(2,1)S(1)}, bf16[40,512]{1,0:T(8,128)(2,1)S(1)}, u32[]{:S(2)}, u32[]{:S(2)}) %collective-permute-start.12) | collective-permute-done | bytes 40992 | tf_op jit(solution)/shard_map/ppermute | solution.py:30
  46.0 1.7 %collective-permute-done.13.d = bf16[40,512]{1,0:T(8,128)(2,1)S(1)} collective-permute-done((bf16[40,512]{1,0:T(8,128)(2,1)S(1)}, bf16[40,512]{1,0:T(8,128)(2,1)S(1)}, u32[]{:S(2)}, u32[]{:S(2)}) %collective-permute-start.13) | collective-permute-done | bytes 40992 | tf_op jit(solution)/shard_map/ppermute | solution.py:30
  47.7 1.0 %unpack.1 = bf16[2,6,24,512]{3,2,1,0:T(8,128)(2,1)} custom-call(bf16[112,512]{1,0:T(8,128)(2,1)S(1)} %get-tuple-element.99.a, bf16[112,512]{1,0:T(8,128)(2,1)S(1)} %collective-permute-done.11.b, bf16[40,512]{1,0:T(8,128)(2,1)S(1)} %collective-permute-done.12.c, bf16[40,512]{1,0:T(8,128)(2,1)S(1)} %collective-permute-done.13.d, ...), custom_call_target="tpu_custom_call" | custom-call | tf_op jit(solution)/shard_map/unpack/pallas_call | solution.py:441
  (16 shorter events, 0.2 us)
Async XLA Ops:
  0.6 16.6 %copy-start.3 = (bf16[2,3,12,1024]{3,0,2,1:T(2,128)(2,1)S(1)}, bf16[2,3,12,1024]{3,0,2,1:T(2,128)(2,1)}, u32[]{:S(2)}) copy-start(bf16[2,3,12,1024]{3,0,2,1:T(2,128)(2,1)} %param.33) | copy-start | bytes 442372
  2.2 6.8 %collective-permute-start = (bf16[112,512]{1,0:T(8,128)(2,1)S(1)}, bf16[112,512]{1,0:T(8,128)(2,1)S(1)}, u32[]{:S(2)}, u32[]{:S(2)}) collective-permute-start(bf16[112,512]{1,0:T(8,128)(2,1)S(1)} %get-tuple-element.58), channel_id=1, source_target_pairs={{0,4},{1,5},{2,6},{3,7},{4,8},{5,9},{6,10},{7,11},{8,12},{9,13},{1... | collective-permute-start | bytes 344072 | tf_op jit(solution)/shard_map/ppermute | solution.py:30
  4.8 6.7 %collective-permute-start.1 = (bf16[40,512]{1,0:T(8,128)(2,1)S(1)}, bf16[40,512]{1,0:T(8,128)(2,1)S(1)}, u32[]{:S(2)}, u32[]{:S(2)}) collective-permute-start(bf16[40,512]{1,0:T(8,128)(2,1)S(1)} %get-tuple-element.59), channel_id=1, source_target_pairs={{0,1},{1,2},{2,3},{3,0},{4,5},{5,6},{6,7},{7,4},{8,9},{9,10},{10,1... | collective-permute-start | bytes 122888 | tf_op jit(solution)/shard_map/ppermute | solution.py:30
  6.1 5.5 %collective-permute-start.2 = (bf16[40,512]{1,0:T(8,128)(2,1)S(1)}, bf16[40,512]{1,0:T(8,128)(2,1)S(1)}, u32[]{:S(2)}, u32[]{:S(2)}) collective-permute-start(bf16[40,512]{1,0:T(8,128)(2,1)S(1)} %get-tuple-element.60), channel_id=1, source_target_pairs={{0,5},{1,6},{2,7},{3,4},{4,9},{5,10},{6,11},{7,8},{8,13},{9,14},{1... | collective-permute-start | bytes 122888 | tf_op jit(solution)/shard_map/ppermute | solution.py:30
  9.0 0.7 %copy-start = (f32[4]{0:T(128)S(1)}, f32[4]{0:T(128)}, u32[]{:S(2)}) copy-start(f32[4]{0:T(128)} %scales.9) | copy-start | bytes 52
  13.4 8.3 %collective-permute-start.3 = (bf16[112,512]{1,0:T(8,128)(2,1)S(1)}, bf16[112,512]{1,0:T(8,128)(2,1)S(1)}, u32[]{:S(2)}, u32[]{:S(2)}) collective-permute-start(bf16[112,512]{1,0:T(8,128)(2,1)S(1)} %get-tuple-element.64), channel_id=1, source_target_pairs={{0,28},{1,29},{2,30},{3,31},{4,0},{5,1},{6,2},{7,3},{8,4},{9,5},{1... | collective-permute-start | bytes 344072 | tf_op jit(solution)/shard_map/ppermute | solution.py:30
  14.2 7.4 %collective-permute-start.4 = (bf16[40,512]{1,0:T(8,128)(2,1)S(1)}, bf16[40,512]{1,0:T(8,128)(2,1)S(1)}, u32[]{:S(2)}, u32[]{:S(2)}) collective-permute-start(bf16[40,512]{1,0:T(8,128)(2,1)S(1)} %get-tuple-element.65), channel_id=1, source_target_pairs={{0,3},{1,0},{2,1},{3,2},{4,7},{5,4},{6,5},{7,6},{8,11},{9,8},{10,9... | collective-permute-start | bytes 122888 | tf_op jit(solution)/shard_map/ppermute | solution.py:30
  16.5 5.2 %collective-permute-start.5 = (bf16[40,512]{1,0:T(8,128)(2,1)S(1)}, bf16[40,512]{1,0:T(8,128)(2,1)S(1)}, u32[]{:S(2)}, u32[]{:S(2)}) collective-permute-start(bf16[40,512]{1,0:T(8,128)(2,1)S(1)} %get-tuple-element.66), channel_id=1, source_target_pairs={{0,31},{1,28},{2,29},{3,30},{4,3},{5,0},{6,1},{7,2},{8,7},{9,4},{1... | collective-permute-start | bytes 122888 | tf_op jit(solution)/shard_map/ppermute | solution.py:30
  17.2 5.9 %collective-permute-start.7 = (bf16[2,3,12,1024]{3,2,1,0:T(8,128)(2,1)S(1)}, bf16[2,3,12,1024]{3,2,1,0:T(8,128)(2,1)S(1)}, u32[]{:S(2)}, u32[]{:S(2)}) collective-permute-start(bf16[2,3,12,1024]{3,2,1,0:T(8,128)(2,1)S(1)} %copy.23.own_cot), channel_id=1, source_target_pairs={{0,4},{4,0},{8,12},{12,8},{16,20},{20,16},{24,28},{28,24},{1,5},{5... | collective-permute-start | bytes 442376 | tf_op jit(solution)/shard_map/ppermute | solution.py:34
  21.7 2.8 %copy-start.2 = (f32[8]{0:T(128)S(1)}, f32[8]{0:T(128)}, u32[]{:S(2)}) copy-start(f32[8]{0:T(128)} %scales.7) | copy-start | bytes 100
  23.1 1.4 %collective-permute-start.6 = (bf16[72,1024]{1,0:T(8,128)(2,1)S(1)}, bf16[72,1024]{1,0:T(8,128)(2,1)S(1)}, u32[]{:S(2)}, u32[]{:S(2)}) collective-permute-start(bf16[72,1024]{1,0:T(8,128)(2,1)S(1)} %get-tuple-element.70.own), channel_id=1, source_target_pairs={{0,4},{4,0},{8,12},{12,8},{16,20},{20,16},{24,28},{28,24},{1,5},{5... | collective-permute-start | bytes 442376 | tf_op jit(solution)/shard_map/ppermute | solution.py:34
  24.5 9.9 %copy-start.1 = (f32[4]{0:T(128)S(1)}, f32[4]{0:T(128)}, u32[]{:S(2)}) copy-start(f32[4]{0:T(128)} %scales.9) | copy-start | bytes 52
  31.8 2.6 %collective-permute-start.8 = (bf16[112,512]{1,0:T(8,128)(2,1)S(1)}, bf16[112,512]{1,0:T(8,128)(2,1)S(1)}, u32[]{:S(2)}, u32[]{:S(2)}) collective-permute-start(bf16[112,512]{1,0:T(8,128)(2,1)S(1)} %get-tuple-element.78), channel_id=1, source_target_pairs={{0,4},{1,5},{2,6},{3,7},{4,8},{5,9},{6,10},{7,11},{8,12},{9,13},{1... | collective-permute-start | bytes 344072 | tf_op jit(solution)/shard_map/ppermute | solution.py:30
  32.6 5.2 %collective-permute-start.9 = (bf16[40,512]{1,0:T(8,128)(2,1)S(1)}, bf16[40,512]{1,0:T(8,128)(2,1)S(1)}, u32[]{:S(2)}, u32[]{:S(2)}) collective-permute-start(bf16[40,512]{1,0:T(8,128)(2,1)S(1)} %get-tuple-element.79), channel_id=1, source_target_pairs={{0,1},{1,2},{2,3},{3,0},{4,5},{5,6},{6,7},{7,4},{8,9},{9,10},{10,1... | collective-permute-start | bytes 122888 | tf_op jit(solution)/shard_map/ppermute | solution.py:30
  33.4 5.5 %collective-permute-start.10 = (bf16[40,512]{1,0:T(8,128)(2,1)S(1)}, bf16[40,512]{1,0:T(8,128)(2,1)S(1)}, u32[]{:S(2)}, u32[]{:S(2)}) collective-permute-start(bf16[40,512]{1,0:T(8,128)(2,1)S(1)} %get-tuple-element.80), channel_id=1, source_target_pairs={{0,5},{1,6},{2,7},{3,4},{4,9},{5,10},{6,11},{7,8},{8,13},{9,14},{1... | collective-permute-start | bytes 122888 | tf_op jit(solution)/shard_map/ppermute | solution.py:30
  40.8 6.9 %collective-permute-start.11 = (bf16[112,512]{1,0:T(8,128)(2,1)S(1)}, bf16[112,512]{1,0:T(8,128)(2,1)S(1)}, u32[]{:S(2)}, u32[]{:S(2)}) collective-permute-start(bf16[112,512]{1,0:T(8,128)(2,1)S(1)} %get-tuple-element.100), channel_id=1, source_target_pairs={{0,28},{1,29},{2,30},{3,31},{4,0},{5,1},{6,2},{7,3},{8,4},{9,5},{1... | collective-permute-start | bytes 344072 | tf_op jit(solution)/shard_map/ppermute | solution.py:30
  43.2 2.9 %collective-permute-start.12 = (bf16[40,512]{1,0:T(8,128)(2,1)S(1)}, bf16[40,512]{1,0:T(8,128)(2,1)S(1)}, u32[]{:S(2)}, u32[]{:S(2)}) collective-permute-start(bf16[40,512]{1,0:T(8,128)(2,1)S(1)} %get-tuple-element.101), channel_id=1, source_target_pairs={{0,3},{1,0},{2,1},{3,2},{4,7},{5,4},{6,5},{7,6},{8,11},{9,8},{10,9... | collective-permute-start | bytes 122888 | tf_op jit(solution)/shard_map/ppermute | solution.py:30
  43.4 4.3 %collective-permute-start.13 = (bf16[40,512]{1,0:T(8,128)(2,1)S(1)}, bf16[40,512]{1,0:T(8,128)(2,1)S(1)}, u32[]{:S(2)}, u32[]{:S(2)}) collective-permute-start(bf16[40,512]{1,0:T(8,128)(2,1)S(1)} %get-tuple-element.102), channel_id=1, source_target_pairs={{0,31},{1,28},{2,29},{3,30},{4,3},{5,0},{6,1},{7,2},{8,7},{9,4},{1... | collective-permute-start | bytes 122888 | tf_op jit(solution)/shard_map/ppermute | solution.py:30

commit v4 on v3

--- a/solution.py
+++ b/solution.py
@@ -175,16 +175,24 @@
     return factor * (grad - unit * overlap)
 
 
-def spread_heads(rows, masks):
-    return jnp.concatenate([jnp.where(m, rows, 0.0) for m in masks], axis=0).astype(BF16)
-
-
-def join_heads(stacked, masks):
-    n = stacked.shape[0] // len(masks)
-    total = jnp.where(masks[0], stacked[:n], 0.0)
-    for h in range(1, len(masks)):
-        total = jnp.where(masks[h], stacked[h * n : (h + 1) * n], total)
-    return total
+def spread_heads(rows, masks, blocks=1):
+    n = rows.shape[0] // blocks
+    return jnp.concatenate(
+        [jnp.where(m, rows[b * n : (b + 1) * n], 0.0) for b in range(blocks) for m in masks], axis=0
+    ).astype(BF16)
+
+
+def join_heads(stacked, masks, blocks=1):
+    heads = len(masks)
+    n = stacked.shape[0] // (heads * blocks)
+    parts = []
+    for b in range(blocks):
+        low = b * heads * n
+        total = jnp.where(masks[0], stacked[low : low + n], 0.0)
+        for h in range(1, heads):
+            total = jnp.where(masks[h], stacked[low + h * n : low + (h + 1) * n], total)
+        parts.append(total)
+    return parts[0] if blocks == 1 else jnp.concatenate(parts, axis=0)
 
 
 def attend(query_stack, key_unit, values, masks, allowed):
@@ -196,16 +204,17 @@
     return probs
 
 
-def attend_back(probs, query_stack, key_unit, values, mixture_grad, masks):
-    grad_stack = spread_heads(mixture_grad, masks)
+def attend_back(probs, query_stack, key_unit, values, mixture_grad, masks, blocks=1):
+    grad_stack = spread_heads(mixture_grad, masks, blocks)
+    own = key_unit.shape[0] // blocks
     probs_grad = mm_t(grad_stack, values)
     low = probs.astype(BF16)
     probs = probs.astype(F32)
     delta = jnp.sum(probs * probs_grad, axis=-1, keepdims=True)
     logits_grad = (probs * (probs_grad - delta)).astype(BF16)
-    query_grad = join_heads(mm(logits_grad, key_unit), masks)
-    key_grad = t_mm(logits_grad, query_stack)
-    value_grad = t_mm(low, grad_stack)
+    query_grad = join_heads(mm(logits_grad[: own * len(masks)], key_unit), masks)
+    key_grad = t_mm(logits_grad[:, :own], query_stack)
+    value_grad = t_mm(low[:, :own], grad_stack)
     return query_grad, key_grad, value_grad
 
 
@@ -232,7 +241,7 @@
 
 
 def allowed_of(mask, first_band):
-    return jnp.where(first_band, mask[0], mask[1])
+    return jnp.where(first_band, mask[0].astype(F32), mask[1].astype(F32))
 
 
 def fine_window(rows, allowed, inward, outward, scale_lanes, masks, mean_matrix):
@@ -251,14 +260,14 @@
 def scale_lanes_of(scales, masks, head_size):
     lanes = jnp.zeros(masks[0].shape, F32)
     for h, mask in enumerate(masks):
-        lanes = jnp.where(mask, scales[h] / head_size, lanes)
+        lanes = jnp.where(mask, scales[:, h : h + 1] / head_size, lanes)
     return lanes
 
 
 def fine_setup(scales, inner):
     head_size = inner // HEADS
     masks = [head_lanes(inner, head_size, h) for h in range(HEADS)]
-    return masks, scale_lanes_of(scales, masks, head_size), head_mean_matrix(inner, head_size)
+    return masks, scale_lanes_of(scales[...], masks, head_size), head_mean_matrix(inner, head_size)
 
 
 def saved_shapes(n, inner, width):
@@ -278,7 +287,7 @@
 SAVED = 9
 
 
-def fine_kernel(plan, w, band, scales, inward, outward, gain, mask, *rest):
+def fine_kernel(plan, w, band, inward, outward, gain, scales, mask, *rest):
     pieces = rest[: 4 if w == 0 else 2]
     rest = rest[len(pieces) :]
     masks, scale_lanes, mean_matrix = fine_setup(scales, outward.shape[0])
@@ -298,17 +307,17 @@
         refs[0][...] = result.astype(BF16)
 
 
-def fine_back_kernel(plan, w, scales, inward, outward, gain, *rest):
+def fine_back_kernel(plan, w, inward_turned, outward_turned, gain, scales, *rest):
     pieces = rest[: 4 if w == 0 else 2]
     saved = rest[len(pieces) : len(pieces) + SAVED]
     rest = rest[len(pieces) + SAVED :]
-    masks, scale_lanes, mean_matrix = fine_setup(scales, outward.shape[0])
+    masks, scale_lanes, mean_matrix = fine_setup(scales, outward_turned.shape[1])
     query_unit, query_factor, key_unit, key_factor, values, query_stack, probs, unit, factor = (
         x[...] for x in saved
     )
     grad = plan.window_rows(w, *pieces)
     projected_grad = norm_back(unit, factor, grad * gain[...]).astype(BF16)
-    mixture_grad = mm_t(projected_grad, outward[...])
+    mixture_grad = mm(projected_grad, outward_turned[...])
     query_grad, key_grad, value_grad = attend_back(
         probs, query_stack, key_unit.astype(BF16), values, mixture_grad, masks
     )
@@ -317,18 +326,40 @@
     packed_grad = jnp.concatenate(
         [query_grad.astype(BF16), key_grad.astype(BF16), value_grad.astype(BF16)], axis=1
     )
-    finish(plan, w, grad + mm_t(packed_grad, inward[...]), rest)
-
-
-def merge_kernel(plan, a, b, c, d, group, gain, weight, coarse, grouped_out):
+    finish(plan, w, grad + mm(packed_grad, inward_turned[...]), rest)
+
+
+def merge_kernel(plan, a, b, c, d, group, gain, weight, after, coarse, unit_out, factor_out):
     pieces = jnp.concatenate([x[...].astype(F32) for x in (a, b, c, d)], axis=0).astype(BF16)
     rows = mm(group[...], pieces)
     n = plan.merged
     grouped = jnp.concatenate([rows[g * n : (g + 1) * n] for g in range(4)], axis=1)
-    unit, _ = norm_parts(grouped)
+    unit, factor = norm_parts(grouped)
     normed = (unit * gain[...]).astype(BF16)
     coarse[...] = mm(normed, weight[...]).astype(BF16)
-    grouped_out[...] = grouped.astype(BF16)
+    unit_out[...] = unit
+    factor_out[...] = factor
+
+
+def cotangent_kernel(plan, own_cot, partner_cot, gain, rows_out, scaled_out, mean_out):
+    n = plan.merged
+    half_b = plan.breadth // 2
+    lines = [(l, r) for l in range(plan.levels) for r in range(plan.height // 2)]
+    for k, (l, r) in enumerate(lines):
+        for start, cot in ((0, own_cot), (n, partner_cot)):
+            low = start + k * half_b
+            rows_out[low : low + half_b, :] = cot[l, r].astype(F32)
+    scaled = rows_out[...] * gain[...]
+    scaled_out[...] = scaled
+    mean_out[...] = jnp.mean(scaled, axis=-1, keepdims=True)
+
+
+def output_kernel(plan, rows, coarse_out, scratch):
+    half_b = plan.breadth // 2
+    scratch[...] = rows[...].astype(F32)
+    lines = [(l, r) for l in range(plan.levels) for r in range(plan.height // 2)]
+    for k, (l, r) in enumerate(lines):
+        coarse_out[l, r] = scratch[k * half_b : (k + 1) * half_b, :].astype(BF16)
 
 
 def coarse_kernel(
@@ -336,31 +367,28 @@
     scales,
     own,
     partner,
-    own_cot,
-    partner_cot,
-    grouped,
+    cot,
+    scaled_cot,
+    cot_mean,
+    merge_unit,
+    merge_factor,
     inward,
     outward,
+    inward_turned,
+    outward_turned,
     gain,
     merge_gain,
-    merge_weight,
+    merge_turned,
     ungroup,
     coarse_out,
     ga,
     gb,
     gc,
     gd,
-    cot_rows,
-    out_rows,
 ):
     inner = outward.shape[0]
     head_size = inner // HEADS2
     n = plan.merged
-    half_b = plan.breadth // 2
-    lines = [(l, r) for l in range(plan.levels) for r in range(plan.height // 2)]
-    for k, (l, r) in enumerate(lines):
-        cot_rows[k * half_b : (k + 1) * half_b, :] = own_cot[l, r].astype(F32)
-        cot_rows[n + k * half_b : n + (k + 1) * half_b, :] = partner_cot[l, r].astype(F32)
     rows = jnp.concatenate([own[...].astype(F32), partner[...].astype(F32)], axis=0)
     packed = mm(rows.astype(BF16), inward[...]).astype(BF16).astype(F32)
     part = 256 if inner % 256 == 0 else inner
@@ -370,42 +398,40 @@
     saved, mixtures = [], []
     for g in range(inner // part):
         low = g * part
-        scale_lanes = scale_lanes_of([scales[g * per + h] for h in range(per)], masks, head_size)
+        scale_lanes = scale_lanes_of(scales[:, g * per : (g + 1) * per], masks, head_size)
         query_unit, query_factor = unit_rows(packed[:, low : low + part], mean_matrix)
         key_unit, key_factor = unit_rows(packed[:, inner + low : inner + low + part], mean_matrix)
         values = packed[:, 2 * inner + low : 2 * inner + low + part].astype(BF16)
-        query_stack = spread_heads(query_unit * scale_lanes, masks)
+        query_stack = spread_heads(query_unit * scale_lanes, masks, 2)
         key_low = key_unit.astype(BF16)
         probs = attend(query_stack, key_low, values, masks, None)
-        mixtures.append(join_heads(mm(probs.astype(BF16), values), masks).astype(BF16))
+        mixtures.append(join_heads(mm(probs.astype(BF16), values), masks, 2).astype(BF16))
         saved.append(
             (query_unit, query_factor, key_unit, key_factor, values, query_stack, key_low, probs, scale_lanes)
         )
     unit, factor = norm_parts(mm(jnp.concatenate(mixtures, axis=1), outward[...]))
-    out_rows[...] = rows[:n] + unit[:n] * gain[...]
-    for k, (l, r) in enumerate(lines):
-        coarse_out[l, r] = out_rows[k * half_b : (k + 1) * half_b, :].astype(BF16)
-
-    cot = cot_rows[...]
-    projected_grad = norm_back(unit, factor, cot * gain[...]).astype(BF16)
-    mixture_grad = mm_t(projected_grad, outward[...])
+    coarse_out[...] = (rows[:n] + unit[:n] * gain[...]).astype(BF16)
+
+    grad = scaled_cot[...]
+    second = jnp.mean(grad * unit, axis=-1, keepdims=True)
+    projected_grad = (factor * (grad - cot_mean[...] - unit * second)).astype(BF16)
+    mixture_grad = mm(projected_grad, outward_turned[...])
     query_grads, key_grads, value_grads = [], [], []
     for g, (query_unit, query_factor, key_unit, key_factor, values, query_stack, key_low, probs, scale_lanes) in enumerate(saved):
         low = g * part
         query_grad, key_grad, value_grad = attend_back(
-            probs, query_stack, key_low, values, mixture_grad[:, low : low + part], masks
+            probs, query_stack, key_low, values, mixture_grad[:, low : low + part], masks, 2
         )
         query_grads.append(
-            unit_back(query_unit[:n], query_factor[:n], query_grad[:n] * scale_lanes, mean_matrix).astype(BF16)
+            unit_back(query_unit[:n], query_factor[:n], query_grad * scale_lanes, mean_matrix).astype(BF16)
         )
-        key_grads.append(unit_back(key_unit[:n], key_factor[:n], key_grad[:n], mean_matrix).astype(BF16))
-        value_grads.append(value_grad[:n].astype(BF16))
+        key_grads.append(unit_back(key_unit[:n], key_factor[:n], key_grad, mean_matrix).astype(BF16))
+        value_grads.append(value_grad.astype(BF16))
     packed_grad = jnp.concatenate(query_grads + key_grads + value_grads, axis=1)
-    coarse_grad = (cot[:n] + mm_t(packed_grad, inward[...])).astype(BF16)
-
-    normed_grad = mm_t(coarse_grad, merge_weight[...])
-    merge_unit, merge_factor = norm_parts(grouped[...].astype(F32))
-    grouped_grad = norm_back(merge_unit, merge_factor, normed_grad * merge_gain[...])
+    coarse_grad = (cot[:n] + mm(packed_grad, inward_turned[...])).astype(BF16)
+
+    normed_grad = mm(coarse_grad, merge_turned[...])
+    grouped_grad = norm_back(merge_unit[...], merge_factor[...], normed_grad * merge_gain[...])
     width = grouped_grad.shape[1] // 4
     stacked = jnp.concatenate(
         [grouped_grad[:, g * width : (g + 1) * width] for g in range(4)], axis=0
@@ -431,47 +457,56 @@
 VMEM = functools.partial(pl.BlockSpec, memory_space=pltpu.VMEM)
 
 
-def call(kernel, name, outs, args, smem=0, scratch=(), keep_in=True, keep_out=True, cost=None):
-    specs = [SMEM()] * smem + [VMEM()] * (len(args) - smem)
+def call(kernel, name, outs, args, smem=0, scratch=(), keep_in=True, keep_out=True, cost=None, loads=()):
+    n_in, n_out, n_loads = len(args), len(outs), len(loads)
     space = pltpu.VMEM if keep_in else pltpu.HBM
     near = tuple(pltpu.with_memory_space_constraint(x, space) for x in args[smem:])
-    args = tuple(args[:smem]) + near
+    far = tuple(pltpu.with_memory_space_constraint(x, pltpu.HBM) for x in loads)
     if keep_out:
         outs = [pltpu.VMEM(o.shape, o.dtype) for o in outs]
+
+    def body(*refs):
+        ins, refs = refs[:n_in], refs[n_in:]
+        sources, refs = refs[:n_loads], refs[n_loads:]
+        results, refs = refs[:n_out], refs[n_out:]
+        targets, rest = refs[:n_loads], refs[n_loads:]
+        copies = []
+        if n_loads:
+            *rest, sems = rest
+            copies = [
+                pltpu.make_async_copy(x, y, sems.at[k]) for k, (x, y) in enumerate(zip(sources, targets))
+            ]
+        for copy in copies:
+            copy.start()
+        kernel(*ins, *results, *rest)
+        for copy in copies:
+            copy.wait()
+
+    anywhere = pl.BlockSpec(memory_space=pl.ANY)
     return pl.pallas_call(
-        kernel,
+        body,
         name=name,
-        out_shape=outs,
-        in_specs=specs,
-        out_specs=[VMEM() for _ in outs],
-        scratch_shapes=scratch,
+        out_shape=outs + [pltpu.VMEM(x.shape, x.dtype) for x in loads],
+        in_specs=[SMEM()] * smem + [VMEM()] * (n_in - smem) + [anywhere] * n_loads,
+        out_specs=[VMEM()] * (n_out + n_loads),
+        scratch_shapes=list(scratch) + ([pltpu.SemaphoreType.DMA((n_loads,))] if n_loads else []),
         cost_estimate=cost,
-        compiler_params=pltpu.CompilerParams(vmem_limit_bytes=24 * 1024 * 1024),
-    )(*args)
-
-
-def load_kernel(after, *refs):
-    n = (len(refs) - 1) // 2
-    sems = refs[-1]
-    copies = [pltpu.make_async_copy(refs[k], refs[n + k], sems.at[k]) for k in range(n)]
-    for copy in copies:
-        copy.start()
-    for copy in copies:
-        copy.wait()
-
-
-def load(after, args):
-    anywhere = pl.BlockSpec(memory_space=pl.ANY)
-    args = tuple(pltpu.with_memory_space_constraint(x, pltpu.HBM) for x in args)
-    return pl.pallas_call(
-        load_kernel,
-        name="load",
-        out_shape=[pltpu.VMEM(x.shape, x.dtype) for x in args],
-        in_specs=[anywhere] * (len(args) + 1),
-        out_specs=[VMEM() for _ in args],
-        scratch_shapes=[pltpu.SemaphoreType.DMA((len(args),))],
-        compiler_params=pltpu.CompilerParams(vmem_limit_bytes=24 * 1024 * 1024),
-    )(after, *args)
+        compiler_params=pltpu.CompilerParams(vmem_limit_bytes=20 * 1024 * 1024),
+    )(*args[:smem], *near, *far)
+
+
+def turn(source, target):
+    step = 256 if source.shape[0] % 256 == 0 else source.shape[0]
+    for k in range(0, source.shape[0], step):
+        target[:, k : k + step] = source[k : k + step, :].T
+
+
+def turn_kernel(*refs):
+    half = len(refs) // 2
+    for source, target in zip(refs[:half], refs[half:]):
+        turn(source, target)
+    if len(refs) % 2:
+        refs[-1][...] = jnp.zeros(refs[-1].shape, refs[-1].dtype)
 
 
 def local(
@@ -497,7 +532,7 @@
     constant = lambda x: jnp.asarray(x, BF16)
     row = lambda x: x.reshape(1, -1)
     band = lax.axis_index("lat").astype(jnp.int32).reshape(1)
-    masks = [jnp.asarray(m, F32) for m in plan.masks]
+    masks = [constant(m) for m in plan.masks]
 
     def gather(a, b, c, d):
         return a, shifted_to(b, 1, 0), shifted_to(c, 0, 1), shifted_to(d, 1, 1)
@@ -513,11 +548,31 @@
         keep_in=False,
     )
     region = gather(*biased)
-    fine_inward, fine_outward, fine_gain, group, merge_gain, *masks = load(
-        biased[0],
-        (fine_inward, fine_outward, row(fine_gain), constant(plan.group), row(merge_gain), *masks),
-    )
-    fine_weights = (fine_inward, fine_outward, fine_gain)
+    (
+        fine_inward,
+        fine_outward,
+        fine_gain,
+        fine_scale,
+        coarse_scale,
+        merge_gain,
+        coarse_gain,
+        *masks,
+    ) = call(
+        lambda after: None,
+        "load",
+        [],
+        (biased[0],),
+        loads=(
+            fine_inward,
+            fine_outward,
+            row(fine_gain),
+            row(fine_scale),
+            row(coarse_scale),
+            row(merge_gain),
+            row(coarse_gain),
+            *masks,
+        ),
+    )
     cost = pl.CostEstimate(flops=2 * 10**8, transcendentals=0, bytes_accessed=10**6)
     windows = len(plan.masks)
     inner = fine_outward.shape[0]
@@ -526,82 +581,111 @@
         + saved_shapes(plan.length(w), inner, width)
         for w in range(windows)
     ]
+    fine_weights = (fine_inward, fine_outward, fine_gain, fine_scale)
     others, saved = [], [None] * windows
     for w in range(1, windows):
+        first = w == 1
         result, *saved[w] = call(
             functools.partial(fine_kernel, plan, w),
             "fine_inside",
             shapes[w],
-            (band, fine_scale, *fine_weights, masks[w], region[0], region[1]),
-            smem=2,
+            (band, *fine_weights, masks[w], region[0], region[1]),
+            smem=1,
             cost=cost,
+            loads=(coarse_inward,) if first else (),
         )
+        if first:
+            (coarse_inward,) = saved[w][SAVED:]
+            del saved[w][SAVED:]
         others.append(result)
     outs = call(
         functools.partial(fine_kernel, plan, 0),
         "fine_edge",
         pieces + shapes[0][1:],
-        (band, fine_scale, *fine_weights, masks[0], *region, *others),
-        smem=2,
+        (band, *fine_weights, masks[0], *region, *others),
+        smem=1,
         cost=cost,
     )
     saved[0] = outs[4:]
-    merge_weight, coarse_inward, coarse_outward, coarse_gain, ungroup, unpack = load(
-        outs[0],
-        (
-            merge_weight,
-            coarse_inward,
-            coarse_outward,
-            row(coarse_gain),
-            constant(plan.group.T),
-            constant(plan.pack.T),
-        ),
-    )
     fine_result = give_back(*outs[:4])
+    large = (coarse_inward, merge_weight)
+    coarse_inward_turned, merge_turned, done = call(
+        turn_kernel,
+        "turn_large",
+        [jax.ShapeDtypeStruct(x.shape[::-1], x.dtype) for x in large]
+        + [jax.ShapeDtypeStruct((8, 128), F32)],
+        large,
+        cost=cost,
+    )
     partner_cot = swapped(coarse_cotangent)
-    own, grouped = call(
+    cot, scaled_cot, cot_mean = call(
+        functools.partial(cotangent_kernel, plan),
+        "cotangent",
+        [
+            jax.ShapeDtypeStruct((2 * plan.merged, width2), F32),
+            jax.ShapeDtypeStruct((2 * plan.merged, width2), F32),
+            jax.ShapeDtypeStruct((2 * plan.merged, 1), F32),
+        ],
+        (coarse_cotangent, partner_cot, coarse_gain),
+    )
+    own, merge_unit, merge_factor = call(
         functools.partial(merge_kernel, plan),
         "merge",
         [
             jax.ShapeDtypeStruct((plan.merged, width2), BF16),
-            jax.ShapeDtypeStruct((plan.merged, 4 * width), BF16),
+            jax.ShapeDtypeStruct((plan.merged, 4 * width), F32),
+            jax.ShapeDtypeStruct((plan.merged, 1), F32),
         ],
-        (*fine_result, group, merge_gain, merge_weight),
+        (*fine_result, constant(plan.group), merge_gain, merge_weight, done),
+    )
+    turned = (fine_inward, fine_outward, coarse_outward)
+    fine_inward_turned, fine_outward_turned, coarse_outward_turned = call(
+        turn_kernel,
+        "turn_small",
+        [jax.ShapeDtypeStruct(x.shape[::-1], x.dtype) for x in turned],
+        turned,
+        cost=cost,
     )
     partner = swapped(own)
-    coarse_output, *grads = call(
+    output_rows, *grads = call(
         functools.partial(coarse_kernel, plan),
         "coarse",
-        [jax.ShapeDtypeStruct(coarse_cotangent.shape, BF16)] + pieces,
+        [jax.ShapeDtypeStruct((plan.merged, width2), BF16)] + pieces,
         (
             coarse_scale,
             own,
             partner,
-            coarse_cotangent,
-            partner_cot,
-            grouped,
+            cot,
+            scaled_cot,
+            cot_mean,
+            merge_unit,
+            merge_factor,
             coarse_inward,
             coarse_outward,
+            coarse_inward_turned,
+            coarse_outward_turned,
             coarse_gain,
             merge_gain,
-            merge_weight,
-            ungroup,
+            merge_turned,
+            constant(plan.group.T),
         ),
-        smem=1,
-        scratch=[
-            pltpu.VMEM((2 * plan.merged, width2), F32),
-            pltpu.VMEM((plan.merged, width2), F32),
-        ],
+    )
+    (coarse_output,) = call(
+        functools.partial(output_kernel, plan),
+        "output",
+        [jax.ShapeDtypeStruct(coarse_cotangent.shape, BF16)],
+        (output_rows,),
+        scratch=[pltpu.VMEM(output_rows.shape, F32)],
     )
     grads = gather(*grads)
+    back_weights = (fine_inward_turned, fine_outward_turned, fine_gain, fine_scale)
     others = []
     for w in range(1, windows):
         (result,) = call(
             functools.partial(fine_back_kernel, plan, w),
             "fine_back_inside",
             shapes[w][:1],
-            (fine_scale, *fine_weights, grads[0], grads[1], *saved[w]),
-            smem=1,
+            (*back_weights, grads[0], grads[1], *saved[w]),
             cost=cost,
         )
         others.append(result)
@@ -610,8 +694,7 @@
             functools.partial(fine_back_kernel, plan, 0),
             "fine_back_edge",
             pieces,
-            (fine_scale, *fine_weights, *grads, *saved[0], *others),
-            smem=1,
+            (*back_weights, *grads, *saved[0], *others),
             cost=cost,
         )
     )
@@ -619,7 +702,7 @@
         functools.partial(unpack_kernel, plan),
         "unpack",
         [jax.ShapeDtypeStruct(tokens.shape, BF16)],
-        (*token_pieces, unpack),
+        (*token_pieces, constant(plan.pack.T)),
         keep_out=False,
     )
     return (coarse_output, token_grad)

time: 49.1 us -> 45.2 us (0.921)
  Pallas kernels: 23.7 us -> 20.2 us
  starting transfers between devices: 15 us -> 16 us
  local copies, waits for them, and re-layouts: 1.51 us -> 0.87 us
  waiting for transfers between devices: 7.72 us -> 7.21 us
    pallas_call x10 -> x13, Pallas kernels: 23.7 us -> 20.2 us  [call(): pl.pallas_call(body, name=name, out_shape=outs + [pltpu.VMEM(x.shape, x.d...]
    ppermute x12, starting transfers between devices: 14.1 us -> 15 us  [shifted_to(): return lax.ppermute(x, ('lat', 'lon'), pairs)]
    ppermute x2, waiting for transfers between devices: 1.34 us -> 0.54 us  [swapped(): lax.ppermute(x, 'lat', [(i, i ^ 1) for i in range(lax.axis_size('lat'))])]
    unnamed x10 -> x14, local copies, waits for them, and re-layouts: 1.51 us -> 0.87 us
  transfers between devices with their start and end apart: 14 -> 14, of which waited for: 7 -> 8; matrix products, arithmetic and copies ran while one was open for 2% -> 2% of each run, Pallas kernels for 21% -> 21%
where the time goes in v4:
time: 45.2 us; the launch traced here: 45.1 us
  Pallas kernels  20.2 us (45%)
  starting transfers between devices  16 us (35%)
  waiting for transfers between devices  7.21 us (16%)
  local copies, waits for them, and re-layouts  0.87 us (2%)
  between operations  0.79 us (2%)
    pallas_call x13, Pallas kernels, call(): pl.pallas_call(body, name=name, out_shape=outs + [pltpu.VMEM(x.shape, x.d...  20.2 us
    ppermute x12, starting transfers between devices, shifted_to(): return lax.ppermute(x, ('lat', 'lon'), pairs)  15 us
    ppermute x12, waiting for transfers between devices, shifted_to(): return lax.ppermute(x, ('lat', 'lon'), pairs)  6.67 us
    ppermute x2, starting transfers between devices, swapped(): lax.ppermute(x, 'lat', [(i, i ^ 1) for i in range(lax.axis_size('lat'))])  0.98 us
  transfers between devices with their start and end apart: 14, of which 8 were waited for; matrix products, arithmetic and copies ran while one was open for 2% of the time, Pallas kernels for 21%

profile of v4, /device:TPU:1, one launch (start us, length us, event | category | flops | bytes accessed | tf_op | source)
XLA Modules:
  0.0 45.1 jit_solution(11633682270836152103)
XLA Ops:
  0.6 1.5 %bias.1 = (bf16[112,512]{1,0:T(8,128)(2,1)S(1)}, bf16[112,512]{1,0:T(8,128)(2,1)S(1)}, bf16[40,512]{1,0:T(8,128)(2,1)S(1)}, bf16[40,512]{1,0:T(8,128)(2,1)S(1)}) custom-call(bf16[2,6,24,512]{3,2,1,0:T(8,128)(2,1)} %refs_0_.2, s32[6,24]{1,0:T(8,128)} %refs_1_.3, f32[1,512]{1,0:T(1,128)} %bitcast.9, bf16[304,288]{1,0:T(8,128)(2,1)} %constant.20.clone.refs_3_), custom_call_target="tpu_custom_call" | custom-call | tf_op jit(solution)/shard_map/bias/pallas_call | solution.py:486
  2.1 2.6 %collective-permute-start = (bf16[112,512]{1,0:T(8,128)(2,1)S(1)}, bf16[112,512]{1,0:T(8,128)(2,1)S(1)}, u32[]{:S(2)}, u32[]{:S(2)}) collective-permute-start(bf16[112,512]{1,0:T(8,128)(2,1)S(1)} %get-tuple-element.67), channel_id=1, source_target_pairs={{0,4},{1,5},{2,6},{3,7},{4,8},{5,9},{6,10},{7,11},{8,12},{9,13},{1... | collective-permute-start | bytes 344072 | tf_op jit(solution)/shard_map/ppermute | solution.py:30
  4.8 1.3 %collective-permute-start.1 = (bf16[40,512]{1,0:T(8,128)(2,1)S(1)}, bf16[40,512]{1,0:T(8,128)(2,1)S(1)}, u32[]{:S(2)}, u32[]{:S(2)}) collective-permute-start(bf16[40,512]{1,0:T(8,128)(2,1)S(1)} %get-tuple-element.68), channel_id=1, source_target_pairs={{0,1},{1,2},{2,3},{3,0},{4,5},{5,6},{6,7},{7,4},{8,9},{9,10},{10,1... | collective-permute-start | bytes 122888 | tf_op jit(solution)/shard_map/ppermute | solution.py:30
  6.1 1.4 %collective-permute-start.2 = (bf16[40,512]{1,0:T(8,128)(2,1)S(1)}, bf16[40,512]{1,0:T(8,128)(2,1)S(1)}, u32[]{:S(2)}, u32[]{:S(2)}) collective-permute-start(bf16[40,512]{1,0:T(8,128)(2,1)S(1)} %get-tuple-element.69), channel_id=1, source_target_pairs={{0,5},{1,6},{2,7},{3,4},{4,9},{5,10},{6,11},{7,8},{8,13},{9,14},{1... | collective-permute-start | bytes 122888 | tf_op jit(solution)/shard_map/ppermute | solution.py:30
  7.4 1.4 %load.1 = (bf16[512,768]{1,0:T(8,128)(2,1)S(1)}, bf16[256,512]{1,0:T(8,128)(2,1)S(1)}, f32[1,512]{1,0:T(1,128)S(1)}, f32[1,4]{1,0:T(1,128)S(1)}, f32[1,8]{1,0:T(...) custom-call(bf16[112,512]{1,0:T(8,128)(2,1)S(1)} %get-tuple-element., ...), custom_call_target="tpu_custom_call" | custom-call | tf_op jit(solution)/shard_map/load/pallas_call | solution.py:486
  8.9 2.6 %fine_inside.1 = (bf16[144,512]{1,0:T(8,128)(2,1)S(1)}, f32[144,256]{1,0:T(8,128)S(1)}, f32[144,256]{1,0:T(8,128)S(1)}, f32[144,256]{1,0:T(8,128)S(1)}, f32[144,...) custom-call(s32[1]{0:T(128)} %bitcast.6.refs_0_, ...), custom_call_target="tpu_custom_call" | custom-call | flops 200000000 | bytes 1000000 | tf_op jit(solution)/shard_map/fine_inside/pallas_call | solution.py:486
  11.6 1.3 %fine_edge.1 = (bf16[112,512]{1,0:T(8,128)(2,1)S(1)}, bf16[112,512]{1,0:T(8,128)(2,1)S(1)}, bf16[40,512]{1,0:T(8,128)(2,1)S(1)}, bf16[40,512]{1,0:T(8,128)(2,1)S...) custom-call(s32[1]{0:T(128)} %bitcast.6.refs_0_, ...), custom_call_target="tpu_custom_call" | custom-call | flops 200000000 | bytes 1000000 | tf_op jit(solution)/shard_map/fine_edge/pallas_call | solution.py:486
  12.9 0.8 %collective-permute-start.3 = (bf16[112,512]{1,0:T(8,128)(2,1)S(1)}, bf16[112,512]{1,0:T(8,128)(2,1)S(1)}, u32[]{:S(2)}, u32[]{:S(2)}) collective-permute-start(bf16[112,512]{1,0:T(8,128)(2,1)S(1)} %get-tuple-element.73), channel_id=1, source_target_pairs={{0,28},{1,29},{2,30},{3,31},{4,0},{5,1},{6,2},{7,3},{8,4},{9,5},{1... | collective-permute-start | bytes 344072 | tf_op jit(solution)/shard_map/ppermute | solution.py:30
  13.7 2.3 %collective-permute-start.4 = (bf16[40,512]{1,0:T(8,128)(2,1)S(1)}, bf16[40,512]{1,0:T(8,128)(2,1)S(1)}, u32[]{:S(2)}, u32[]{:S(2)}) collective-permute-start(bf16[40,512]{1,0:T(8,128)(2,1)S(1)} %get-tuple-element.74), channel_id=1, source_target_pairs={{0,3},{1,0},{2,1},{3,2},{4,7},{5,4},{6,5},{7,6},{8,11},{9,8},{10,9... | collective-permute-start | bytes 122888 | tf_op jit(solution)/shard_map/ppermute | solution.py:30
  16.0 0.7 %collective-permute-start.5 = (bf16[40,512]{1,0:T(8,128)(2,1)S(1)}, bf16[40,512]{1,0:T(8,128)(2,1)S(1)}, u32[]{:S(2)}, u32[]{:S(2)}) collective-permute-start(bf16[40,512]{1,0:T(8,128)(2,1)S(1)} %get-tuple-element.75), channel_id=1, source_target_pairs={{0,31},{1,28},{2,29},{3,30},{4,3},{5,0},{6,1},{7,2},{8,7},{9,4},{1... | collective-permute-start | bytes 122888 | tf_op jit(solution)/shard_map/ppermute | solution.py:30
  16.8 0.9 %collective-permute-start.7 = (bf16[2,3,12,1024]{3,2,1,0:T(8,128)(2,1)S(1)}, bf16[2,3,12,1024]{3,2,1,0:T(8,128)(2,1)S(1)}, u32[]{:S(2)}, u32[]{:S(2)}) collective-permute-start(bf16[2,3,12,1024]{3,2,1,0:T(8,128)(2,1)S(1)} %copy.23.refs_0_), channel_id=1, source_target_pairs={{0,4},{4,0},{8,12},{12,8},{16,20},{20,16},{24,28},{28,24},{1,5},{5... | collective-permute-start | bytes 442376 | tf_op jit(solution)/shard_map/ppermute | solution.py:34
  17.7 2.1 %turn_large.1 = (bf16[1536,1024]{1,0:T(8,128)(2,1)S(1)}, bf16[1024,2048]{1,0:T(8,128)(2,1)S(1)}, f32[8,128]{1,0:T(8,128)S(1)}) custom-call(bf16[1024,1536]{1,0:T(8,128)(2,1)S(1)} %get-tuple-element.77.refs_0_.refs_8_, bf16[2048,1024]{1,0:T(8,128)(2,1)S(1)} %copy-done), custom_call_target="tpu_custom_call" | custom-call | flops 200000000 | bytes 1000000 | tf_op jit(solution)/shard_map/turn_large/pallas_call | solution.py:486
  19.8 0.5 %collective-permute-done.5.refs_3_ = bf16[40,512]{1,0:T(8,128)(2,1)S(1)} collective-permute-done((bf16[40,512]{1,0:T(8,128)(2,1)S(1)}, bf16[40,512]{1,0:T(8,128)(2,1)S(1)}, u32[]{:S(2)}, u32[]{:S(2)}) %collective-permute-start.5) | collective-permute-done | bytes 40992 | tf_op jit(solution)/shard_map/ppermute | solution.py:30
  20.3 1.3 %merge.1 = (bf16[72,1024]{1,0:T(8,128)(2,1)S(1)}, f32[72,2048]{1,0:T(8,128)S(1)}, f32[72,1]{1,0:T(8,128)S(1)}) custom-call(bf16[112,512]{1,0:T(8,128)(2,1)S(1)} %get-tuple-element.72.refs_0_, bf16[112,512]{1,0:T(8,128)(2,1)S(1)} %collective-permute-done.3.refs_1_, bf16[40,512]{1,0:T(8,128)(2,1)S(1)} %collective-permute-done.4.refs_2_, ...), custom_call_target="tpu_custom_call" | custom-call | tf_op jit(solution)/shard_map/merge/pallas_call | solution.py:486
  21.8 0.6 %turn_small.1 = (bf16[768,512]{1,0:T(8,128)(2,1)S(1)}, bf16[512,256]{1,0:T(8,128)(2,1)S(1)}, bf16[1024,512]{1,0:T(8,128)(2,1)S(1)}) custom-call(bf16[512,768]{1,0:T(8,128)(2,1)S(1)} %get-tuple-element.62.refs_1_.refs_0_, bf16[256,512]{1,0:T(8,128)(2,1)S(1)} %get-tuple-element.63.refs_2_.refs_1_, bf16[512,1024]{1,0:T(8,128)(2,1)S(1)} %copy-done.1), custom_call_target="tpu_custom_call" | custom-call | flops 200000000 | bytes 1000000 | tf_op jit(solution)/shard_map/turn_small/pallas_call | solution.py:486
  22.4 0.2 cotangent.1
  22.6 0.5 %collective-permute-done.6.refs_2_ = bf16[72,1024]{1,0:T(8,128)(2,1)S(1)} collective-permute-done((bf16[72,1024]{1,0:T(8,128)(2,1)S(1)}, bf16[72,1024]{1,0:T(8,128)(2,1)S(1)}, u32[]{:S(2)}, u32[]{:S(2)}) %collective-permute-start.6) | collective-permute-done | bytes 147488 | tf_op jit(solution)/shard_map/ppermute | solution.py:34
  23.1 5.5 %coarse.1 = (bf16[72,1024]{1,0:T(8,128)(2,1)S(1)}, bf16[112,512]{1,0:T(8,128)(2,1)S(1)}, bf16[112,512]{1,0:T(8,128)(2,1)S(1)}, bf16[40,512]{1,0:T(8,128)(2,1)S(1)}, bf16[40,512]{1,0:T(8,128)(2,1)S(1)}) custom-call(f32[1,8]{1,0:T(1,128)S(1)} %get-tuple-element.61.refs_0_, bf16[72,1024]{1,0:T(8,128)(2,1)S(1)} %get-tuple-element.79.refs_1_, ...), custom_call_target="tpu_custom_call" | custom-call | tf_op jit(solution)/shard_map/coarse/pallas_call | solution.py:486
  28.6 1.7 %collective-permute-start.8 = (bf16[112,512]{1,0:T(8,128)(2,1)S(1)}, bf16[112,512]{1,0:T(8,128)(2,1)S(1)}, u32[]{:S(2)}, u32[]{:S(2)}) collective-permute-start(bf16[112,512]{1,0:T(8,128)(2,1)S(1)} %get-tuple-element.93), channel_id=1, source_target_pairs={{0,4},{1,5},{2,6},{3,7},{4,8},{5,9},{6,10},{7,11},{8,12},{9,13},{1... | collective-permute-start | bytes 344072 | tf_op jit(solution)/shard_map/ppermute | solution.py:30
  30.4 1.1 %collective-permute-start.10 = (bf16[40,512]{1,0:T(8,128)(2,1)S(1)}, bf16[40,512]{1,0:T(8,128)(2,1)S(1)}, u32[]{:S(2)}, u32[]{:S(2)}) collective-permute-start(bf16[40,512]{1,0:T(8,128)(2,1)S(1)} %get-tuple-element.95), channel_id=1, source_target_pairs={{0,5},{1,6},{2,7},{3,4},{4,9},{5,10},{6,11},{7,8},{8,13},{9,14},{1... | collective-permute-start | bytes 122888 | tf_op jit(solution)/shard_map/ppermute | solution.py:30
  31.5 0.6 %collective-permute-done.8.refs_5_ = bf16[112,512]{1,0:T(8,128)(2,1)S(1)} collective-permute-done((bf16[112,512]{1,0:T(8,128)(2,1)S(1)}, bf16[112,512]{1,0:T(8,128)(2,1)S(1)}, u32[]{:S(2)}, u32[]{:S(2)}) %collective-permute-start.8) | collective-permute-done | bytes 114720 | tf_op jit(solution)/shard_map/ppermute | solution.py:30
  32.2 1.3 %fine_back_inside.1.refs_17_ = bf16[144,512]{1,0:T(8,128)(2,1)S(1)} custom-call(bf16[768,512]{1,0:T(8,128)(2,1)S(1)} %get-tuple-element.90.refs_0_, bf16[512,256]{1,0:T(8,128)(2,1)S(1)} %get-tuple-element.91.refs_1_, f32[1,512]{1,0:T(1,128)S(1)} %get-tuple-element.64.refs_3_.refs_2_, f32[1,4]{1,0:T(1,128)S(1)} %get-tuple-element.65.refs_4_.refs_3_, ...), custom_call_target="tpu_custom_call" | custom-call | flops 200000000 | bytes 1000000 | tf_op jit(solution)/shard_map/fine_back_inside/pallas_call | solution.py:486
  33.5 1.6 %collective-permute-done.9.refs_6_ = bf16[40,512]{1,0:T(8,128)(2,1)S(1)} collective-permute-done((bf16[40,512]{1,0:T(8,128)(2,1)S(1)}, bf16[40,512]{1,0:T(8,128)(2,1)S(1)}, u32[]{:S(2)}, u32[]{:S(2)}) %collective-permute-start.9) | collective-permute-done | bytes 40992 | tf_op jit(solution)/shard_map/ppermute | solution.py:30
  35.0 0.9 %collective-permute-done.10.refs_7_ = bf16[40,512]{1,0:T(8,128)(2,1)S(1)} collective-permute-done((bf16[40,512]{1,0:T(8,128)(2,1)S(1)}, bf16[40,512]{1,0:T(8,128)(2,1)S(1)}, u32[]{:S(2)}, u32[]{:S(2)}) %collective-permute-start.10) | collective-permute-done | bytes 40992 | tf_op jit(solution)/shard_map/ppermute | solution.py:30
  35.9 1.3 %fine_back_edge.1 = (bf16[112,512]{1,0:T(8,128)(2,1)S(1)}, bf16[112,512]{1,0:T(8,128)(2,1)S(1)}, bf16[40,512]{1,0:T(8,128)(2,1)S(1)}, bf16[40,512]{1,0:T(8,128)(2,1)S(1)}) custom-call(bf16[768,512]{1,0:T(8,128)(2,1)S(1)} %get-tuple-element.90.refs_0_, bf16[512,256]{1,0:T(8,128)(2,1)S(1)} %get-tuple-element.91.refs_1_, ...), custom_call_target="tpu_custom_call" | custom-call | flops 200000000 | bytes 1000000 | tf_op jit(solution)/shard_map/fine_back_edge/pallas_call | solution.py:486
  37.3 1.7 %collective-permute-start.11 = (bf16[112,512]{1,0:T(8,128)(2,1)S(1)}, bf16[112,512]{1,0:T(8,128)(2,1)S(1)}, u32[]{:S(2)}, u32[]{:S(2)}) collective-permute-start(bf16[112,512]{1,0:T(8,128)(2,1)S(1)} %get-tuple-element.115), channel_id=1, source_target_pairs={{0,28},{1,29},{2,30},{3,31},{4,0},{5,1},{6,2},{7,3},{8,4},{9,5},{1... | collective-permute-start | bytes 344072 | tf_op jit(solution)/shard_map/ppermute | solution.py:30
  39.0 0.6 %collective-permute-start.12 = (bf16[40,512]{1,0:T(8,128)(2,1)S(1)}, bf16[40,512]{1,0:T(8,128)(2,1)S(1)}, u32[]{:S(2)}, u32[]{:S(2)}) collective-permute-start(bf16[40,512]{1,0:T(8,128)(2,1)S(1)} %get-tuple-element.116), channel_id=1, source_target_pairs={{0,3},{1,0},{2,1},{3,2},{4,7},{5,4},{6,5},{7,6},{8,11},{9,8},{10,9... | collective-permute-start | bytes 122888 | tf_op jit(solution)/shard_map/ppermute | solution.py:30
  39.6 0.6 %collective-permute-start.13 = (bf16[40,512]{1,0:T(8,128)(2,1)S(1)}, bf16[40,512]{1,0:T(8,128)(2,1)S(1)}, u32[]{:S(2)}, u32[]{:S(2)}) collective-permute-start(bf16[40,512]{1,0:T(8,128)(2,1)S(1)} %get-tuple-element.117), channel_id=1, source_target_pairs={{0,31},{1,28},{2,29},{3,30},{4,3},{5,0},{6,1},{7,2},{8,7},{9,4},{1... | collective-permute-start | bytes 122888 | tf_op jit(solution)/shard_map/ppermute | solution.py:30
  40.2 0.8 %copy.24 = bf16[2,3,12,1024]{3,0,2,1:T(2,128)(2,1)} copy(bf16[2,3,12,1024]{3,2,1,0:T(8,128)(2,1)S(1)} %output.1) | data formatting | bytes 294912
  41.0 0.8 %collective-permute-done.12.refs_2_ = bf16[40,512]{1,0:T(8,128)(2,1)S(1)} collective-permute-done((bf16[40,512]{1,0:T(8,128)(2,1)S(1)}, bf16[40,512]{1,0:T(8,128)(2,1)S(1)}, u32[]{:S(2)}, u32[]{:S(2)}) %collective-permute-start.12) | collective-permute-done | bytes 40992 | tf_op jit(solution)/shard_map/ppermute | solution.py:30
  41.8 2.2 %collective-permute-done.13.refs_3_ = bf16[40,512]{1,0:T(8,128)(2,1)S(1)} collective-permute-done((bf16[40,512]{1,0:T(8,128)(2,1)S(1)}, bf16[40,512]{1,0:T(8,128)(2,1)S(1)}, u32[]{:S(2)}, u32[]{:S(2)}) %collective-permute-start.13) | collective-permute-done | bytes 40992 | tf_op jit(solution)/shard_map/ppermute | solution.py:30
  44.0 1.0 %unpack.1 = bf16[2,6,24,512]{3,2,1,0:T(8,128)(2,1)} custom-call(bf16[112,512]{1,0:T(8,128)(2,1)S(1)} %get-tuple-element.114.refs_0_, bf16[112,512]{1,0:T(8,128)(2,1)S(1)} %collective-permute-done.11.refs_1_, bf16[40,512]{1,0:T(8,128)(2,1)S(1)} %collective-permute-done.12.refs_2_, bf16[40,512]{1,0:T(8,128)(2,1)S(1)} %collective-permute-done.13.refs_3_, ...), custom_call_target="tpu_custom_call" | custom-call | tf_op jit(solution)/shard_map/unpack/pallas_call | solution.py:486
  (23 shorter events, 0.3 us)
Async XLA Ops:
  2.1 6.8 %collective-permute-start = (bf16[112,512]{1,0:T(8,128)(2,1)S(1)}, bf16[112,512]{1,0:T(8,128)(2,1)S(1)}, u32[]{:S(2)}, u32[]{:S(2)}) collective-permute-start(bf16[112,512]{1,0:T(8,128)(2,1)S(1)} %get-tuple-element.67), channel_id=1, source_target_pairs={{0,4},{1,5},{2,6},{3,7},{4,8},{5,9},{6,10},{7,11},{8,12},{9,13},{1... | collective-permute-start | bytes 344072 | tf_op jit(solution)/shard_map/ppermute | solution.py:30
  4.8 6.7 %collective-permute-start.1 = (bf16[40,512]{1,0:T(8,128)(2,1)S(1)}, bf16[40,512]{1,0:T(8,128)(2,1)S(1)}, u32[]{:S(2)}, u32[]{:S(2)}) collective-permute-start(bf16[40,512]{1,0:T(8,128)(2,1)S(1)} %get-tuple-element.68), channel_id=1, source_target_pairs={{0,1},{1,2},{2,3},{3,0},{4,5},{5,6},{6,7},{7,4},{8,9},{9,10},{10,1... | collective-permute-start | bytes 122888 | tf_op jit(solution)/shard_map/ppermute | solution.py:30
  6.1 5.5 %collective-permute-start.2 = (bf16[40,512]{1,0:T(8,128)(2,1)S(1)}, bf16[40,512]{1,0:T(8,128)(2,1)S(1)}, u32[]{:S(2)}, u32[]{:S(2)}) collective-permute-start(bf16[40,512]{1,0:T(8,128)(2,1)S(1)} %get-tuple-element.69), channel_id=1, source_target_pairs={{0,5},{1,6},{2,7},{3,4},{4,9},{5,10},{6,11},{7,8},{8,13},{9,14},{1... | collective-permute-start | bytes 122888 | tf_op jit(solution)/shard_map/ppermute | solution.py:30
  8.9 7.9 %copy-start.5 = (bf16[2,3,12,1024]{3,0,2,1:T(2,128)(2,1)S(1)}, bf16[2,3,12,1024]{3,0,2,1:T(2,128)(2,1)}, u32[]{:S(2)}) copy-start(bf16[2,3,12,1024]{3,0,2,1:T(2,128)(2,1)} %param.33) | copy-start | bytes 442372
  8.9 8.8 %copy-start = (bf16[2048,1024]{1,0:T(8,128)(2,1)S(1)}, bf16[2048,1024]{1,0:T(8,128)(2,1)}, u32[]{:S(2)}) copy-start(bf16[2048,1024]{1,0:T(8,128)(2,1)} %refs_6_.1) | copy-start | bytes 12582916
  12.9 7.5 %collective-permute-start.3 = (bf16[112,512]{1,0:T(8,128)(2,1)S(1)}, bf16[112,512]{1,0:T(8,128)(2,1)S(1)}, u32[]{:S(2)}, u32[]{:S(2)}) collective-permute-start(bf16[112,512]{1,0:T(8,128)(2,1)S(1)} %get-tuple-element.73), channel_id=1, source_target_pairs={{0,28},{1,29},{2,30},{3,31},{4,0},{5,1},{6,2},{7,3},{8,4},{9,5},{1... | collective-permute-start | bytes 344072 | tf_op jit(solution)/shard_map/ppermute | solution.py:30
  13.7 6.2 %collective-permute-start.4 = (bf16[40,512]{1,0:T(8,128)(2,1)S(1)}, bf16[40,512]{1,0:T(8,128)(2,1)S(1)}, u32[]{:S(2)}, u32[]{:S(2)}) collective-permute-start(bf16[40,512]{1,0:T(8,128)(2,1)S(1)} %get-tuple-element.74), channel_id=1, source_target_pairs={{0,3},{1,0},{2,1},{3,2},{4,7},{5,4},{6,5},{7,6},{8,11},{9,8},{10,9... | collective-permute-start | bytes 122888 | tf_op jit(solution)/shard_map/ppermute | solution.py:30
  16.0 4.3 %collective-permute-start.5 = (bf16[40,512]{1,0:T(8,128)(2,1)S(1)}, bf16[40,512]{1,0:T(8,128)(2,1)S(1)}, u32[]{:S(2)}, u32[]{:S(2)}) collective-permute-start(bf16[40,512]{1,0:T(8,128)(2,1)S(1)} %get-tuple-element.75), channel_id=1, source_target_pairs={{0,31},{1,28},{2,29},{3,30},{4,3},{5,0},{6,1},{7,2},{8,7},{9,4},{1... | collective-permute-start | bytes 122888 | tf_op jit(solution)/shard_map/ppermute | solution.py:30
  16.8 5.6 %collective-permute-start.7 = (bf16[2,3,12,1024]{3,2,1,0:T(8,128)(2,1)S(1)}, bf16[2,3,12,1024]{3,2,1,0:T(8,128)(2,1)S(1)}, u32[]{:S(2)}, u32[]{:S(2)}) collective-permute-start(bf16[2,3,12,1024]{3,2,1,0:T(8,128)(2,1)S(1)} %copy.23.refs_0_), channel_id=1, source_target_pairs={{0,4},{4,0},{8,12},{12,8},{16,20},{20,16},{24,28},{28,24},{1,5},{5... | collective-permute-start | bytes 442376 | tf_op jit(solution)/shard_map/ppermute | solution.py:34
  17.7 2.7 %copy-start.4 = (bf16[288,304]{1,0:T(8,128)(2,1)S(1)}, bf16[288,304]{1,0:T(8,128)(2,1)}, u32[]{:S(2)}) copy-start(bf16[288,304]{1,0:T(8,128)(2,1)} %constant.21.clone.refs_4_) | copy-start | bytes 525316
  19.8 1.9 %copy-start.1 = (bf16[512,1024]{1,0:T(8,128)(2,1)S(1)}, bf16[512,1024]{1,0:T(8,128)(2,1)}, u32[]{:S(2)}) copy-start(bf16[512,1024]{1,0:T(8,128)(2,1)} %refs_9_.2) | copy-start | bytes 3145732
  20.3 2.8 %copy-start.2 = (bf16[304,288]{1,0:T(8,128)(2,1)S(1)}, bf16[304,288]{1,0:T(8,128)(2,1)}, u32[]{:S(2)}) copy-start(bf16[304,288]{1,0:T(8,128)(2,1)} %constant.22.clone.refs_15_) | copy-start | bytes 525316
  21.7 1.4 %collective-permute-start.6 = (bf16[72,1024]{1,0:T(8,128)(2,1)S(1)}, bf16[72,1024]{1,0:T(8,128)(2,1)S(1)}, u32[]{:S(2)}, u32[]{:S(2)}) collective-permute-start(bf16[72,1024]{1,0:T(8,128)(2,1)S(1)} %get-tuple-element.79.refs_1_), channel_id=1, source_target_pairs={{0,4},{4,0},{8,12},{12,8},{16,20},{20,16},{24,28},{28,24},{1,5},{5... | collective-permute-start | bytes 442376 | tf_op jit(solution)/shard_map/ppermute | solution.py:34
  28.6 3.5 %collective-permute-start.8 = (bf16[112,512]{1,0:T(8,128)(2,1)S(1)}, bf16[112,512]{1,0:T(8,128)(2,1)S(1)}, u32[]{:S(2)}, u32[]{:S(2)}) collective-permute-start(bf16[112,512]{1,0:T(8,128)(2,1)S(1)} %get-tuple-element.93), channel_id=1, source_target_pairs={{0,4},{1,5},{2,6},{3,7},{4,8},{5,9},{6,10},{7,11},{8,12},{9,13},{1... | collective-permute-start | bytes 344072 | tf_op jit(solution)/shard_map/ppermute | solution.py:30
  30.4 4.7 %collective-permute-start.9 = (bf16[40,512]{1,0:T(8,128)(2,1)S(1)}, bf16[40,512]{1,0:T(8,128)(2,1)S(1)}, u32[]{:S(2)}, u32[]{:S(2)}) collective-permute-start(bf16[40,512]{1,0:T(8,128)(2,1)S(1)} %get-tuple-element.94), channel_id=1, source_target_pairs={{0,1},{1,2},{2,3},{3,0},{4,5},{5,6},{6,7},{7,4},{8,9},{9,10},{10,1... | collective-permute-start | bytes 122888 | tf_op jit(solution)/shard_map/ppermute | solution.py:30
  30.4 5.5 %collective-permute-start.10 = (bf16[40,512]{1,0:T(8,128)(2,1)S(1)}, bf16[40,512]{1,0:T(8,128)(2,1)S(1)}, u32[]{:S(2)}, u32[]{:S(2)}) collective-permute-start(bf16[40,512]{1,0:T(8,128)(2,1)S(1)} %get-tuple-element.95), channel_id=1, source_target_pairs={{0,5},{1,6},{2,7},{3,4},{4,9},{5,10},{6,11},{7,8},{8,13},{9,14},{1... | collective-permute-start | bytes 122888 | tf_op jit(solution)/shard_map/ppermute | solution.py:30
  32.2 11.9 %copy-start.3 = (bf16[288,304]{1,0:T(8,128)(2,1)S(1)}, bf16[288,304]{1,0:T(8,128)(2,1)}, u32[]{:S(2)}) copy-start(bf16[288,304]{1,0:T(8,128)(2,1)} %constant.23.clone.refs_4_) | copy-start | bytes 525316
  37.3 6.8 %collective-permute-start.11 = (bf16[112,512]{1,0:T(8,128)(2,1)S(1)}, bf16[112,512]{1,0:T(8,128)(2,1)S(1)}, u32[]{:S(2)}, u32[]{:S(2)}) collective-permute-start(bf16[112,512]{1,0:T(8,128)(2,1)S(1)} %get-tuple-element.115), channel_id=1, source_target_pairs={{0,28},{1,29},{2,30},{3,31},{4,0},{5,1},{6,2},{7,3},{8,4},{9,5},{1... | collective-permute-start | bytes 344072 | tf_op jit(solution)/shard_map/ppermute | solution.py:30
  39.0 2.9 %collective-permute-start.12 = (bf16[40,512]{1,0:T(8,128)(2,1)S(1)}, bf16[40,512]{1,0:T(8,128)(2,1)S(1)}, u32[]{:S(2)}, u32[]{:S(2)}) collective-permute-start(bf16[40,512]{1,0:T(8,128)(2,1)S(1)} %get-tuple-element.116), channel_id=1, source_target_pairs={{0,3},{1,0},{2,1},{3,2},{4,7},{5,4},{6,5},{7,6},{8,11},{9,8},{10,9... | collective-permute-start | bytes 122888 | tf_op jit(solution)/shard_map/ppermute | solution.py:30
  39.6 4.4 %collective-permute-start.13 = (bf16[40,512]{1,0:T(8,128)(2,1)S(1)}, bf16[40,512]{1,0:T(8,128)(2,1)S(1)}, u32[]{:S(2)}, u32[]{:S(2)}) collective-permute-start(bf16[40,512]{1,0:T(8,128)(2,1)S(1)} %get-tuple-element.117), channel_id=1, source_target_pairs={{0,31},{1,28},{2,29},{3,30},{4,3},{5,0},{6,1},{7,2},{8,7},{9,4},{1... | collective-permute-start | bytes 122888 | tf_op jit(solution)/shard_map/ppermute | solution.py:30
